TPU v7x, 128 devices: a whole 4x4x4 slice. The times are simulated.
128 devices in a mesh: var: 16 (over x, y), samp: 8 (over z, core).
Axes of the slice: x: 4, y: 4, z: 4, core: 2. Of those that a mesh axis runs over, the one named last changes fastest.
Arguments:
- dosage: int32 [24576, 8192], P('samp', 'var'), may hold values from 0 to 2, as said below
- phenotype: float32 [24576], P('samp'), may hold values from -6 to 6
- perm_index: int32 [1024, 24576], P('var', 'samp'), may hold values from 0 to 24575, each once within a row
- seg_lengths: int32 [128], replicated, may hold values from 1 to 128, 8192 in all
Outputs:
- zscore: float32 [1024, 8192], P('samp', 'var')
- thresholds: float32 [1024, 128], P('samp')
Inputs may be any that keep to these rules, and one draw needn't show every extreme that they name: `dosage`: each entry is an allele count. `perm_index`: each row is a permutation of the 24576 sample numbers. `seg_lengths`: the lengths sum to 8192, one of them equals 128.
All inputs are finite; a program needn't handle non-finite values.
Results may differ from a plain program's by a relative error of at most 0.0039.
Values may be sent and summed in bfloat16 or wider, within the bound.
No kernel may reach another device: no remote copies, remote signals or barrier semaphores. Data moves between devices by JAX's collectives and lax.ppermute only.
A program may use at most 64 MiB of HBM per device.

v0:
```python
import jax
import jax.numpy as jnp
from jax import lax
from jax.experimental import pallas as pl
from jax.experimental.pallas import tpu as pltpu
from jax.sharding import Mesh, PartitionSpec as P


EPSILON = 1e-05
RING = 4
AXES = ("x", "y", "z", "c")
CHUNKS = 2
LOW = 128
AT_ONCE = 24
PLACES = [
    (x, y, z, c) for x in range(RING) for y in range(RING) for z in range(RING) for c in range(2)
]
VMEM = pl.BlockSpec(memory_space=pltpu.VMEM)
SMEM = pl.BlockSpec(memory_space=pltpu.SMEM)


def at(x, y, z, c):
    return (((x % RING) * RING + y % RING) * RING + z % RING) * 2 + c


def shift(value, target):
    return lax.ppermute(value, AXES, [(at(*d), at(*target(*d))) for d in PLACES])


def along(value, axis, step):
    return lax.ppermute(value, axis, [(i, (i + step) % RING) for i in range(RING)])


def other_core(value):
    return lax.ppermute(value, "c", [(0, 1), (1, 0)])


def out_of(shape, dtype):
    return jax.ShapeDtypeStruct(shape, dtype)


def room(mib):
    return pltpu.CompilerParams(vmem_limit_bytes=mib << 20)


def dosage_kernel(dosage_ref, out_ref, totals_ref, acc_ref):
    @pl.when(pl.program_id(0) == 0)
    def _():
        acc_ref[...] = jnp.zeros_like(acc_ref)

    d = dosage_ref[...]
    out_ref[...] = d.astype(jnp.bfloat16)
    groups = d.reshape(d.shape[0] // 8, 8, d.shape[1])
    acc_ref[0:8] += jnp.sum(groups, axis=0)
    acc_ref[8:16] += jnp.sum(groups * groups, axis=0)

    @pl.when(pl.program_id(0) == pl.num_programs(0) - 1)
    def _():
        totals_ref[...] = acc_ref[...].astype(jnp.float32)


def convert_dosage(dosage):
    samples, width = dosage.shape
    block = 512
    return pl.pallas_call(
        dosage_kernel,
        grid=(samples // block,),
        out_shape=(out_of(dosage.shape, jnp.bfloat16), out_of((16, width), jnp.float32)),
        in_specs=[pl.BlockSpec((block, width), lambda i: (i, 0))],
        out_specs=(
            pl.BlockSpec((block, width), lambda i: (i, 0)),
            pl.BlockSpec((16, width), lambda i: (0, 0)),
        ),
        scratch_shapes=[pltpu.VMEM((16, width), jnp.int32)],
        compiler_params=room(8),
    )(dosage)


def table_kernel(*refs):
    blocks, (table_ref, scale_ref, var_ref, code_ref) = refs[:8], refs[8:]
    z, c = lax.axis_index("z"), lax.axis_index("c")
    depth = blocks[0].shape[0]
    count = len(blocks) * blocks[0].size
    values = [r[...] for r in blocks]
    mean = jnp.sum(sum(values)) / count
    values = [v - mean for v in values]
    var_ref[0, 0] = jnp.sum(sum(v * v for v in values)) / count
    rounded = [v.astype(jnp.bfloat16).astype(jnp.float32) for v in values]
    most = jnp.abs(rounded[0])
    for r in rounded[1:]:
        most = jnp.maximum(most, jnp.abs(r))
    most = jnp.full((1, LOW), jnp.maximum(jnp.max(most), 1e-30), jnp.float32)
    for k, r in enumerate(rounded):
        code = jnp.round(jnp.sqrt(jnp.sqrt(jnp.abs(r) / most)) * 32767.0).astype(jnp.int32)
        code = jnp.where(r < 0, -code, code)
        core = c if k < RING else 1 - c
        start = (((z + RING - k % RING) % RING) * 2 + core) * depth
        code_ref[pl.ds(pl.multiple_of(start, 8), depth), :] = code
    half = table_ref.shape[0]
    table_ref[...] = lax.shift_left(code_ref[half:, :], 16) + (code_ref[:half, :] & 0xFFFF)
    scale_ref[...] = jnp.sqrt(jnp.sqrt(most)) / 32767.0


def make_table(blocks):
    rows = len(blocks) * blocks[0].shape[0]
    return pl.pallas_call(
        table_kernel,
        out_shape=(
            out_of((rows // 2, LOW), jnp.int32),
            out_of((1, LOW), jnp.float32),
            out_of((1, 1), jnp.float32),
        ),
        in_specs=[VMEM] * 8,
        out_specs=(VMEM, VMEM, SMEM),
        scratch_shapes=[pltpu.VMEM((rows, LOW), jnp.int32)],
        compiler_params=room(2),
    )(*blocks)


def lookup_kernel(index_ref, table_ref, scale_ref, *rest):
    out_ref = rest[-1]
    rows, width = index_ref.shape
    first = out_ref.shape[0] - rows
    if first:
        out_ref[:first, :] = rest[0][...]
    half = table_ref.shape[0]
    parts = AT_ONCE // (rows // 8)
    span = parts * LOW
    scale = jnp.broadcast_to(scale_ref[...], (8, LOW))

    def step(j, _):
        for part in range(parts):
            base = pl.multiple_of(j * span + part * LOW, LOW)
            found = []
            for i in range(0, rows, 8):
                index = index_ref[pl.ds(i, 8), pl.ds(base, LOW)]
                lane = index & (LOW - 1)
                row = lax.shift_right_logical(index, 7)
                upper = row >= half
                row = jnp.where(upper, row - half, row)
                word = jnp.zeros((8, LOW), jnp.int32)
                for r in range(half):
                    source = jnp.broadcast_to(table_ref[r : r + 1, :], (8, LOW))
                    taken = jnp.take_along_axis(source, lane, axis=1, mode="promise_in_bounds")
                    word = jnp.where(row == r, taken, word)
                code = lax.shift_right_arithmetic(
                    jnp.where(upper, word, lax.shift_left(word, 16)), 16
                )
                root = code.astype(jnp.float32) * scale
                root = root * root
                root = root * root
                found.append(jnp.where(code < 0, -root, root))
            out_ref[first:, pl.ds(base, LOW)] = jnp.concatenate(found, axis=0).astype(jnp.bfloat16)
        return 0

    lax.fori_loop(0, width // span, step, 0)


def lookup(index, k, rows, table, scale, before=()):
    width = index.shape[1]
    shape = (rows + sum(b.shape[0] for b in before), width)
    whole = lambda i: (0, 0)
    return pl.pallas_call(
        lookup_kernel,
        grid=(1,),
        out_shape=out_of(shape, jnp.bfloat16),
        in_specs=[
            pl.BlockSpec((rows, width), lambda i: (k, 0)),
            pl.BlockSpec(table.shape, whole),
            pl.BlockSpec(scale.shape, whole),
        ]
        + [pl.BlockSpec(b.shape, whole) for b in before],
        out_specs=pl.BlockSpec(shape, whole),
        compiler_params=room(3),
    )(index, table, scale, *before)


def ring_gather(value, first, turn):
    def line(sign):
        def target(x, y, z, c):
            step = sign if c == turn else -sign
            if (c == 0) == first:
                return (x + step, y, z, c)
            return (x, y + step, z, c)

        return target

    behind = shift(value, line(1))
    ahead = shift(value, line(-1))
    onward = shift(behind, line(1))
    return [value, behind, ahead, onward]


def offset(k, turn, c):
    step = jnp.where(c == turn, 1, -1)
    return (0, -step, step, 2)[k]


def stack_kernel(a0, a1, a2, a3, out_ref):
    for k, a in enumerate((a0, a1, a2, a3)):
        out_ref[k] = a[...]


def stacked(pieces):
    return pl.pallas_call(
        stack_kernel,
        out_shape=out_of((len(pieces), *pieces[0].shape), pieces[0].dtype),
        in_specs=[VMEM] * 4,
        out_specs=VMEM,
        compiler_params=room(3),
    )(*pieces)


def product_kernel(
    a0, a1, a2, a3, dosage_ref, totals_ref, keep_ref, send_ref, lhs_ref, *, turn_near, turn_far
):
    rows = a0.shape[1]
    extra = keep_ref.shape[1] - 2 * rows
    dest = destinations(turn_near, turn_far)
    for u, a in enumerate((a0, a1, a2, a3)):
        for t in range(RING):
            start = pl.multiple_of(dest(u, t) * rows, rows)
            lhs_ref[pl.ds(start, rows), :] = a[t]
    part = jnp.dot(lhs_ref[...], dosage_ref[...], preferred_element_type=jnp.float32)
    for h, ref in enumerate((keep_ref, send_ref)):
        for k in range(RING):
            start = (h * RING + k) * 2 * rows
            ref[k, : 2 * rows, :] = part[start : start + 2 * rows]
            if extra:
                ref[k, 2 * rows :, :] = totals_ref[...]


def product(pieces, dosage, totals, with_totals, turn_near, turn_far):
    rows = pieces[0].shape[1]
    shape = (RING, 2 * rows + (totals.shape[0] if with_totals else 0), dosage.shape[1])
    return pl.pallas_call(
        lambda *refs: product_kernel(*refs, turn_near=turn_near, turn_far=turn_far),
        out_shape=(out_of(shape, jnp.float32), out_of(shape, jnp.float32)),
        in_specs=[VMEM] * 6,
        out_specs=(VMEM, VMEM),
        scratch_shapes=[pltpu.VMEM((rows * RING * RING, dosage.shape[0]), jnp.bfloat16)],
        compiler_params=room(20),
    )(*pieces, dosage, totals)


def add_kernel(a_ref, b_ref, o0, o1, o2, o3):
    for k, o in enumerate((o0, o1, o2, o3)):
        o[...] = a_ref[k] + b_ref[k]


def core_sum(keep, got):
    one = out_of(keep.shape[1:], jnp.float32)
    return pl.pallas_call(
        add_kernel,
        out_shape=(one,) * 4,
        in_specs=[VMEM] * 2,
        out_specs=(VMEM,) * 4,
        compiler_params=room(4),
    )(keep, got)


def destinations(turn_near, turn_far):
    x, y, z, c = (lax.axis_index(a) for a in AXES)
    step = 1 - 2 * c

    def of(u, t):
        far, near = offset(u, turn_far, c), offset(t, turn_near, c)
        px = (x + RING + jnp.where(c == 0, near, far)) % RING
        py = (y + RING + jnp.where(c == 0, far, near)) % RING
        away = jnp.where(py // 2 == c, 0, 1)
        owner = ((1 - 2 * away) * step * (px - z) + 2 * RING) % RING
        return away * 8 + owner * 2 + py % 2

    return of


def z_line(sign):
    def target(x, y, z, c):
        return (x, y, z + (sign if c == 0 else -sign), c)

    return target


def reduced(keep, send):
    got = other_core(send)
    own, ahead, opposite, behind = core_sum(keep, got)
    passing = shift(opposite, z_line(1))
    from_ahead = shift(behind, z_line(-1))
    from_behind = shift(ahead + passing, z_line(1))
    return own, from_behind, from_ahead


def final_kernel(*refs, extra, count):
    if extra:
        var_ref, end_ref, p, q, r, z_ref, most_ref, inverse_ref = refs
        rows = (p.shape[0] - extra) // 2
        totals = p[2 * rows :, :] + q[2 * rows :, :] + r[2 * rows :, :]
        allele_sum = jnp.sum(totals[0:8], axis=0, keepdims=True)
        allele_sq = jnp.sum(totals[8:16], axis=0, keepdims=True)
        allele_var = allele_sq / count - (allele_sum / count) ** 2
        inverse = 1.0 / jnp.sqrt(count * (var_ref[0, 0] + EPSILON) * (allele_var + EPSILON))
        inverse_ref[...] = inverse
        places = [0, rows]
    else:
        end_ref, inverse_ref, z0, most0, p, q, r, z_ref, most_ref = refs
        rows = p.shape[0] // 2
        inverse = inverse_ref[...]
        for h in range(2):
            z_ref[2 * h * rows : (2 * h + 1) * rows, :] = z0[h * rows : (h + 1) * rows, :]
            most_ref[2 * h * rows : (2 * h + 1) * rows, :] = most0[h * rows : (h + 1) * rows, :]
        places = [rows, 3 * rows]
    width = z_ref.shape[1]
    ends = end_ref[...]
    clipped = jnp.clip(ends, 0, width - 1)
    both = 2 * rows
    z = (p[:both, :] + q[:both, :] + r[:both, :]) * inverse
    lanes = lax.broadcasted_iota(jnp.int32, (both, LOW), 1)
    lane = jnp.broadcast_to(clipped % LOW, (both, LOW))
    group = jnp.broadcast_to(clipped // LOW, (both, LOW))
    parts = [jnp.abs(z[:, g * LOW : (g + 1) * LOW]) for g in range(width // LOW)]
    wholes = [jnp.max(v, axis=1, keepdims=True) for v in parts]
    step = 1
    while step < LOW:
        parts = [
            jnp.maximum(v, jnp.where(lanes >= step, pltpu.roll(v, step, 1), 0.0)) for v in parts
        ]
        step *= 2
    chosen = jnp.zeros((both, LOW), jnp.float32)
    before = jnp.zeros((both, 1), jnp.float32)
    for g, v in enumerate(parts):
        taken = jnp.take_along_axis(v, lane, axis=1, mode="promise_in_bounds")
        chosen = jnp.where(group == g, jnp.maximum(taken, before), chosen)
        before = jnp.maximum(before, wholes[g])
    chosen = jnp.where(jnp.broadcast_to(ends >= 0, (both, LOW)), chosen, 0.0)
    for h, place in enumerate(places):
        z_ref[place : place + rows, :] = z[h * rows : (h + 1) * rows]
        most_ref[place : place + rows, :] = chosen[h * rows : (h + 1) * rows]


def final_first(pheno_var, ends, parts, extra, count):
    rows, width = parts[0].shape[0] - extra, parts[0].shape[1]
    return pl.pallas_call(
        lambda *refs: final_kernel(*refs, extra=extra, count=count),
        out_shape=(
            out_of((rows, width), jnp.float32),
            out_of((rows, ends.shape[1]), jnp.float32),
            out_of((1, width), jnp.float32),
        ),
        in_specs=[SMEM] + [VMEM] * 4,
        out_specs=(VMEM,) * 3,
        compiler_params=room(4),
    )(pheno_var, ends, *parts)


def final_second(ends, inverse, z0, most0, parts, count):
    rows, width = parts[0].shape
    return pl.pallas_call(
        lambda *refs: final_kernel(*refs, extra=0, count=count),
        out_shape=(
            out_of((CHUNKS * rows, width), jnp.float32),
            out_of((CHUNKS * rows, ends.shape[1]), jnp.float32),
        ),
        in_specs=[VMEM] * 7,
        out_specs=(VMEM,) * 2,
        compiler_params=room(4),
    )(ends, inverse, z0, most0, *parts)


def largest(value, first):
    def line(step):
        def target(x, y, z, c):
            return (x + step, y, z, c) if (c == 0) == first else (x, y + step, z, c)

        return target

    got = [shift(value, line(k)) for k in (2, 1, 3)]
    return jnp.maximum(jnp.maximum(value, got[0]), jnp.maximum(got[1], got[2]))


def per_device(dosage, phenotype, perm_index, seg_lengths):
    samples, width = dosage.shape
    x, y = lax.axis_index("x"), lax.axis_index("y")
    own = phenotype.reshape(-1, LOW)
    mine = [own] + [along(own, "z", k) for k in (1, 2, 3)]
    dosage_bf, totals = convert_dosage(dosage)
    table, scale, pheno_var = make_table(mine + [other_core(m) for m in mine])
    ends = (jnp.cumsum(seg_lengths) - 1 - (x * RING + y) * width)[None, :].astype(jnp.int32)
    count = float(samples * lax.axis_size("z") * lax.axis_size("c"))

    rows = perm_index.shape[0] // CHUNKS
    part = rows // 2
    traits = lookup(perm_index, 0, rows, table, scale)
    near = ring_gather(traits, True, 0)
    traits = lookup(perm_index, 2, part, table, scale)
    traits = lookup(perm_index, 3, part, table, scale, (traits,))
    far = ring_gather(stacked(near), False, 1)
    near = ring_gather(traits, True, 1)
    keep, send = product(far, dosage_bf, totals, True, 0, 1)
    parts = reduced(keep, send)
    z0, most0, inverse = final_first(pheno_var, ends, parts, totals.shape[0], count)

    far = ring_gather(stacked(near), False, 0)
    keep, send = product(far, dosage_bf, totals, False, 1, 0)
    parts = reduced(keep, send)
    zscore, most = final_second(ends, inverse, z0, most0, parts, count)
    return (zscore, largest(largest(most, True), False))


def solution(mesh):
    fine = Mesh(mesh.devices.reshape(RING, RING, RING, 2), AXES)
    var, samp = ("x", "y"), ("z", "c")
    return jax.shard_map(
        per_device,
        mesh=fine,
        in_specs=(P(samp, var), P(samp), P(var, samp), P()),
        out_specs=(P(samp, var), P(samp, None)),
        check_vma=False,
    )
```

profile of v0, /device:TPU:0, one launch (start us, length us, event | category | flops | bytes accessed | tf_op | source)
XLA Modules:
  0.0 121.2 jit_solution(2563823836138669696)
XLA Ops:
  0.6 2.1 %collective-permute-start = (f32[24,128]{1,0:T(8,128)}, f32[24,128]{1,0:T(8,128)S(1)}, u32[]{:S(2)}, u32[]{:S(2)}) collective-permute-start(f32[24,128]{1,0:T(8,128)} %bitcast.2), channel_id=1, source_target_pairs={{0,2},{2,4},{4,6},{6,0},{1,3},{3,5},{5,7},{7,1},{8,10},{10,12},{12... | collective-permute-start | bytes 36872 | tf_op jit(solution)/shard_map/ppermute | solution.py:31
  2.7 3.6 %collective-permute-start.1 = (f32[24,128]{1,0:T(8,128)}, f32[24,128]{1,0:T(8,128)S(1)}, u32[]{:S(2)}, u32[]{:S(2)}) collective-permute-start(f32[24,128]{1,0:T(8,128)} %bitcast.3), channel_id=1, source_target_pairs={{0,4},{2,6},{4,0},{6,2},{1,5},{3,7},{5,1},{7,3},{8,12},{10,14},{12... | collective-permute-start | bytes 36872 | tf_op jit(solution)/shard_map/ppermute | solution.py:31
  8.3 1.9 %collective-permute-done.2.refs_3_ = f32[24,128]{1,0:T(8,128)S(1)} collective-permute-done((f32[24,128]{1,0:T(8,128)}, f32[24,128]{1,0:T(8,128)S(1)}, u32[]{:S(2)}, u32[]{:S(2)}) %collective-permute-start.2) | collective-permute-done | bytes 12320 | tf_op jit(solution)/shard_map/ppermute | solution.py:31
  14.0 10.3 %shard_map.60.a0 = bf16[32,3072]{1,0:T(8,128)(2,1)S(1)} custom-call(s32[64,3072]{1,0:T(8,128)S(1)} %copy-done, s32[96,128]{1,0:T(8,128)S(1)} %get-tuple-element.25.table_ref, f32[1,128]{1,0:T(1,128)S(1)} %get-tuple-element.26.scale_ref), custom_call_target="tpu_custom_call" | custom-call | tf_op jit(solution)/shard_map/pallas_call | solution.py:163
  24.3 1.6 %collective-permute-start.7 = (bf16[32,3072]{1,0:T(8,128)(2,1)S(1)}, bf16[32,3072]{1,0:T(8,128)(2,1)S(1)}, u32[]{:S(2)}, u32[]{:S(2)}) collective-permute-start(bf16[32,3072]{1,0:T(8,128)(2,1)S(1)} %shard_map.60.a0), channel_id=1, source_target_pairs={{0,32},{1,25},{2,34},{3,27},{4,36},{5,29},{6,38},{7,31},{8,40},{9,... | collective-permute-start | bytes 589832 | tf_op jit(solution)/shard_map/ppermute | solution.py:27
  25.9 5.2 %shard_map.66.rest_0_ = bf16[16,3072]{1,0:T(8,128)(2,1)S(1)} custom-call(s32[64,3072]{1,0:T(8,128)S(1)} %copy-done, s32[96,128]{1,0:T(8,128)S(1)} %get-tuple-element.25.table_ref, f32[1,128]{1,0:T(1,128)S(1)} %get-tuple-element.26.scale_ref), custom_call_target="tpu_custom_call" | custom-call | tf_op jit(solution)/shard_map/pallas_call | solution.py:163
  31.1 5.2 %shard_map.67.a0 = bf16[32,3072]{1,0:T(8,128)(2,1)S(1)} custom-call(s32[64,3072]{1,0:T(8,128)S(1)} %copy-done, s32[96,128]{1,0:T(8,128)S(1)} %get-tuple-element.25.table_ref, f32[1,128]{1,0:T(1,128)S(1)} %get-tuple-element.26.scale_ref, bf16[16,3072]{1,0:T(8,128)(2,1)S(1)} %shard_map.66.rest_0_), custom_call_target="tpu_custom_call" | custom-call | tf_op jit(solution)/shard_map/pallas_call | solution.py:163
  36.3 1.8 %collective-permute-start.17 = (bf16[32,3072]{1,0:T(8,128)(2,1)S(1)}, bf16[32,3072]{1,0:T(8,128)(2,1)S(1)}, u32[]{:S(2)}, u32[]{:S(2)}) collective-permute-start(bf16[32,3072]{1,0:T(8,128)(2,1)S(1)} %shard_map.67.a0), channel_id=1, source_target_pairs={{0,96},{1,9},{2,98},{3,11},{4,100},{5,13},{6,102},{7,15},{8,104},{... | collective-permute-start | bytes 589832 | tf_op jit(solution)/shard_map/ppermute | solution.py:27
  38.1 1.5 %collective-permute-start.8 = (bf16[32,3072]{1,0:T(8,128)(2,1)S(1)}, bf16[32,3072]{1,0:T(8,128)(2,1)S(1)}, u32[]{:S(2)}, u32[]{:S(2)}) collective-permute-start(bf16[32,3072]{1,0:T(8,128)(2,1)S(1)} %shard_map.60.a0), channel_id=1, source_target_pairs={{0,96},{1,9},{2,98},{3,11},{4,100},{5,13},{6,102},{7,15},{8,104},{... | collective-permute-start | bytes 589832 | tf_op jit(solution)/shard_map/ppermute | solution.py:27
  40.4 1.6 %collective-permute-done.17.a1 = bf16[32,3072]{1,0:T(8,128)(2,1)S(1)} collective-permute-done((bf16[32,3072]{1,0:T(8,128)(2,1)S(1)}, bf16[32,3072]{1,0:T(8,128)(2,1)S(1)}, u32[]{:S(2)}, u32[]{:S(2)}) %collective-permute-start.17) | collective-permute-done | bytes 196640 | tf_op jit(solution)/shard_map/ppermute | solution.py:27
  42.0 3.0 %collective-permute-start.19 = (bf16[32,3072]{1,0:T(8,128)(2,1)S(1)}, bf16[32,3072]{1,0:T(8,128)(2,1)S(1)}, u32[]{:S(2)}, u32[]{:S(2)}) collective-permute-start(bf16[32,3072]{1,0:T(8,128)(2,1)S(1)} %collective-permute-done.17.a1), channel_id=1, source_target_pairs={{0,96},{1,9},{2,98},{3,11},{4,100},{5,13},{6,102},{7,15},{8,104},{... | collective-permute-start | bytes 589832 | tf_op jit(solution)/shard_map/ppermute | solution.py:27
  45.0 1.5 %collective-permute-done.9.a3 = bf16[32,3072]{1,0:T(8,128)(2,1)S(1)} collective-permute-done((bf16[32,3072]{1,0:T(8,128)(2,1)S(1)}, bf16[32,3072]{1,0:T(8,128)(2,1)S(1)}, u32[]{:S(2)}, u32[]{:S(2)}) %collective-permute-start.9) | collective-permute-done | bytes 196640 | tf_op jit(solution)/shard_map/ppermute | solution.py:27
  46.6 3.1 %collective-permute-start.10 = (bf16[4,32,3072]{2,1,0:T(8,128)(2,1)S(1)}, bf16[4,32,3072]{2,1,0:T(8,128)(2,1)S(1)}, u32[]{:S(2)}, u32[]{:S(2)}) collective-permute-start(bf16[4,32,3072]{2,1,0:T(8,128)(2,1)S(1)} %shard_map.61.refs_0_), channel_id=1, source_target_pairs={{0,24},{1,33},{2,26},{3,35},{4,28},{5,37},{6,30},{7,39},{8,0},{9,4... | collective-permute-start | bytes 2359304 | tf_op jit(solution)/shard_map/ppermute | solution.py:27
  49.7 1.9 %collective-permute-start.20 = (bf16[4,32,3072]{2,1,0:T(8,128)(2,1)S(1)}, bf16[4,32,3072]{2,1,0:T(8,128)(2,1)S(1)}, u32[]{:S(2)}, u32[]{:S(2)}) collective-permute-start(bf16[4,32,3072]{2,1,0:T(8,128)(2,1)S(1)} %shard_map.68.refs_0_), channel_id=1, source_target_pairs={{0,8},{1,97},{2,10},{3,99},{4,12},{5,101},{6,14},{7,103},{8,16},{9... | collective-permute-start | bytes 2359304 | tf_op jit(solution)/shard_map/ppermute | solution.py:27
  53.1 6.1 %collective-permute-done.10.refs_1_ = bf16[4,32,3072]{2,1,0:T(8,128)(2,1)S(1)} collective-permute-done((bf16[4,32,3072]{2,1,0:T(8,128)(2,1)S(1)}, bf16[4,32,3072]{2,1,0:T(8,128)(2,1)S(1)}, u32[]{:S(2)}, u32[]{:S(2)}) %collective-permute-start.10) | collective-permute-done | bytes 786464 | tf_op jit(solution)/shard_map/ppermute | solution.py:27
  59.2 3.7 %collective-permute-start.12 = (bf16[4,32,3072]{2,1,0:T(8,128)(2,1)S(1)}, bf16[4,32,3072]{2,1,0:T(8,128)(2,1)S(1)}, u32[]{:S(2)}, u32[]{:S(2)}) collective-permute-start(bf16[4,32,3072]{2,1,0:T(8,128)(2,1)S(1)} %collective-permute-done.10.refs_1_), channel_id=1, source_target_pairs={{0,24},{1,33},{2,26},{3,35},{4,28},{5,37},{6,30},{7,39},{8,0},{9,4... | collective-permute-start | bytes 2359304 | tf_op jit(solution)/shard_map/ppermute | solution.py:27
  63.0 1.9 %collective-permute-start.22 = (bf16[4,32,3072]{2,1,0:T(8,128)(2,1)S(1)}, bf16[4,32,3072]{2,1,0:T(8,128)(2,1)S(1)}, u32[]{:S(2)}, u32[]{:S(2)}) collective-permute-start(bf16[4,32,3072]{2,1,0:T(8,128)(2,1)S(1)} %collective-permute-done.20.refs_1_), channel_id=1, source_target_pairs={{0,8},{1,97},{2,10},{3,99},{4,12},{5,101},{6,14},{7,103},{8,16},{9... | collective-permute-start | bytes 2359304 | tf_op jit(solution)/shard_map/ppermute | solution.py:27
  64.9 2.8 %copy-done.1 = s32[3072,512]{1,0:T(8,128)S(1)} copy-done((s32[3072,512]{1,0:T(8,128)S(1)}, s32[3072,512]{1,0:T(8,128)}, u32[]{:S(2)}) %copy-start.1) | copy-done | bytes 6291480
  68.7 2.7 %collective-permute-done.11.refs_2_ = bf16[4,32,3072]{2,1,0:T(8,128)(2,1)S(1)} collective-permute-done((bf16[4,32,3072]{2,1,0:T(8,128)(2,1)S(1)}, bf16[4,32,3072]{2,1,0:T(8,128)(2,1)S(1)}, u32[]{:S(2)}, u32[]{:S(2)}) %collective-permute-start.11) | collective-permute-done | bytes 786464 | tf_op jit(solution)/shard_map/ppermute | solution.py:27
  72.4 2.1 %shard_map.63 = (f32[4,80,512]{2,1,0:T(8,128)S(1)}, f32[4,80,512]{2,1,0:T(8,128)S(1)}) custom-call(bf16[4,32,3072]{2,1,0:T(8,128)(2,1)S(1)} %shard_map.61.refs_0_, bf16[4,32,3072]{2,1,0:T(8,128)(2,1)S(1)} %collective-permute-done.10.refs_1_, bf16[4,32,3072]{2,1,0:T(8,128)(2,1)S(1)} %collective-permute-done.11.refs_2_, ...), custom_call_target="tpu_custom_call" | custom-call | tf_op jit(solution)/shard_map/pallas_call | solution.py:236
  74.5 6.2 %collective-permute-done.21.refs_2_ = bf16[4,32,3072]{2,1,0:T(8,128)(2,1)S(1)} collective-permute-done((bf16[4,32,3072]{2,1,0:T(8,128)(2,1)S(1)}, bf16[4,32,3072]{2,1,0:T(8,128)(2,1)S(1)}, u32[]{:S(2)}, u32[]{:S(2)}) %collective-permute-start.21) | collective-permute-done | bytes 786464 | tf_op jit(solution)/shard_map/ppermute | solution.py:27
  80.8 2.1 %shard_map.69 = (f32[4,64,512]{2,1,0:T(8,128)S(1)}, f32[4,64,512]{2,1,0:T(8,128)S(1)}) custom-call(bf16[4,32,3072]{2,1,0:T(8,128)(2,1)S(1)} %shard_map.68.refs_0_, bf16[4,32,3072]{2,1,0:T(8,128)(2,1)S(1)} %collective-permute-done.20.refs_1_, bf16[4,32,3072]{2,1,0:T(8,128)(2,1)S(1)} %collective-permute-done.21.refs_2_, ...), custom_call_target="tpu_custom_call" | custom-call | tf_op jit(solution)/shard_map/pallas_call | solution.py:236
  83.1 1.7 %collective-permute-done.23.b_ref = f32[4,64,512]{2,1,0:T(8,128)S(1)} collective-permute-done((f32[4,64,512]{2,1,0:T(8,128)S(1)}, f32[4,64,512]{2,1,0:T(8,128)S(1)}, u32[]{:S(2)}, u32[]{:S(2)}) %collective-permute-start.23) | collective-permute-done | bytes 524320 | tf_op jit(solution)/shard_map/ppermute | solution.py:35
  85.3 3.2 %collective-permute-start.26 = (f32[64,512]{1,0:T(8,128)S(1)}, f32[64,512]{1,0:T(8,128)S(1)}, u32[]{:S(2)}, u32[]{:S(2)}) collective-permute-start(f32[64,512]{1,0:T(8,128)S(1)} %get-tuple-element.43), channel_id=1, source_target_pairs={{0,6},{1,3},{2,0},{3,5},{4,2},{5,7},{6,4},{7,1},{8,14},{9,11},{10,... | collective-permute-start | bytes 393224 | tf_op jit(solution)/shard_map/ppermute | solution.py:27
  89.6 1.6 %collective-permute-done.24 = f32[64,512]{1,0:T(8,128)S(1)} collective-permute-done((f32[64,512]{1,0:T(8,128)S(1)}, f32[64,512]{1,0:T(8,128)S(1)}, u32[]{:S(2)}, u32[]{:S(2)}) %collective-permute-start.24) | collective-permute-done | bytes 131104 | tf_op jit(solution)/shard_map/ppermute | solution.py:27
  91.3 2.0 %collective-permute-start.15 = (f32[80,512]{1,0:T(8,128)S(1)}, f32[80,512]{1,0:T(8,128)S(1)}, u32[]{:S(2)}, u32[]{:S(2)}) collective-permute-start(f32[80,512]{1,0:T(8,128)S(1)} %add.18), channel_id=1, source_target_pairs={{0,2},{1,7},{2,4},{3,1},{4,6},{5,3},{6,0},{7,5},{8,10},{9,15},{10,... | collective-permute-start | bytes 491528 | tf_op jit(solution)/shard_map/ppermute | solution.py:27
  94.5 4.7 %collective-permute-done.15.refs_3_ = f32[80,512]{1,0:T(8,128)S(1)} collective-permute-done((f32[80,512]{1,0:T(8,128)S(1)}, f32[80,512]{1,0:T(8,128)S(1)}, u32[]{:S(2)}, u32[]{:S(2)}) %collective-permute-start.15) | collective-permute-done | bytes 163872 | tf_op jit(solution)/shard_map/ppermute | solution.py:27
  101.8 3.2 %collective-permute-start.29 = (f32[128,128]{1,0:T(8,128)S(1)}, f32[128,128]{1,0:T(8,128)S(1)}, u32[]{:S(2)}, u32[]{:S(2)}) collective-permute-start(f32[128,128]{1,0:T(8,128)S(1)} %get-tuple-element.45), channel_id=1, source_target_pairs={{0,96},{1,25},{2,98},{3,27},{4,100},{5,29},{6,102},{7,31},{8,104},... | collective-permute-start | bytes 196616 | tf_op jit(solution)/shard_map/ppermute | solution.py:27
  105.0 2.2 %collective-permute-done.28 = f32[128,128]{1,0:T(8,128)S(1)} collective-permute-done((f32[128,128]{1,0:T(8,128)S(1)}, f32[128,128]{1,0:T(8,128)S(1)}, u32[]{:S(2)}, u32[]{:S(2)}) %collective-permute-start.28) | collective-permute-done | bytes 65568 | tf_op jit(solution)/shard_map/ppermute | solution.py:27
  107.5 3.6 %collective-permute-done.27 = f32[128,128]{1,0:T(8,128)S(1)} collective-permute-done((f32[128,128]{1,0:T(8,128)S(1)}, f32[128,128]{1,0:T(8,128)S(1)}, u32[]{:S(2)}, u32[]{:S(2)}) %collective-permute-start.27) | collective-permute-done | bytes 65568 | tf_op jit(solution)/shard_map/ppermute | solution.py:27
  111.2 3.5 %collective-permute-start.32 = (f32[128,128]{1,0:T(8,128)S(1)}, f32[128,128]{1,0:T(8,128)S(1)}, u32[]{:S(2)}, u32[]{:S(2)}) collective-permute-start(f32[128,128]{1,0:T(8,128)S(1)} %maximum_maximum_fusion.1), channel_id=1, source_target_pairs={{0,24},{1,97},{2,26},{3,99},{4,28},{5,101},{6,30},{7,103},{8,0},{9... | collective-permute-start | bytes 196616 | tf_op jit(solution)/shard_map/ppermute | solution.py:27
  116.9 3.6 %collective-permute-done.30 = f32[128,128]{1,0:T(8,128)S(1)} collective-permute-done((f32[128,128]{1,0:T(8,128)S(1)}, f32[128,128]{1,0:T(8,128)S(1)}, u32[]{:S(2)}, u32[]{:S(2)}) %collective-permute-start.30) | collective-permute-done | bytes 65568 | tf_op jit(solution)/shard_map/ppermute | solution.py:27
  (61 shorter events, 19.1 us)
Async XLA Ops:
  0.6 6.7 %collective-permute-start = (f32[24,128]{1,0:T(8,128)}, f32[24,128]{1,0:T(8,128)S(1)}, u32[]{:S(2)}, u32[]{:S(2)}) collective-permute-start(f32[24,128]{1,0:T(8,128)} %bitcast.2), channel_id=1, source_target_pairs={{0,2},{2,4},{4,6},{6,0},{1,3},{3,5},{5,7},{7,1},{8,10},{10,12},{12... | collective-permute-start | bytes 36872 | tf_op jit(solution)/shard_map/ppermute | solution.py:31
  2.7 5.6 %collective-permute-start.1 = (f32[24,128]{1,0:T(8,128)}, f32[24,128]{1,0:T(8,128)S(1)}, u32[]{:S(2)}, u32[]{:S(2)}) collective-permute-start(f32[24,128]{1,0:T(8,128)} %bitcast.3), channel_id=1, source_target_pairs={{0,4},{2,6},{4,0},{6,2},{1,5},{3,7},{5,1},{7,3},{8,12},{10,14},{12... | collective-permute-start | bytes 36872 | tf_op jit(solution)/shard_map/ppermute | solution.py:31
  6.3 3.9 %collective-permute-start.2 = (f32[24,128]{1,0:T(8,128)}, f32[24,128]{1,0:T(8,128)S(1)}, u32[]{:S(2)}, u32[]{:S(2)}) collective-permute-start(f32[24,128]{1,0:T(8,128)} %bitcast.4), channel_id=1, source_target_pairs={{0,6},{2,0},{4,2},{6,4},{1,7},{3,1},{5,3},{7,5},{8,14},{10,8},{12,... | collective-permute-start | bytes 36872 | tf_op jit(solution)/shard_map/ppermute | solution.py:31
  7.3 2.9 %collective-permute-start.3 = (f32[24,128]{1,0:T(8,128)}, f32[24,128]{1,0:T(8,128)S(1)}, u32[]{:S(2)}, u32[]{:S(2)}) collective-permute-start(f32[24,128]{1,0:T(8,128)} %bitcast.5), channel_id=1, source_target_pairs={{0,1},{1,0},{2,3},{3,2},{4,5},{5,4},{6,7},{7,6},{8,9},{9,8},{10,11... | collective-permute-start | bytes 36872 | tf_op jit(solution)/shard_map/ppermute | solution.py:35
  7.3 2.9 %collective-permute-start.4 = (f32[24,128]{1,0:T(8,128)S(1)}, f32[24,128]{1,0:T(8,128)S(1)}, u32[]{:S(2)}, u32[]{:S(2)}) collective-permute-start(f32[24,128]{1,0:T(8,128)S(1)} %collective-permute-done.refs_1_), channel_id=1, source_target_pairs={{0,1},{1,0},{2,3},{3,2},{4,5},{5,4},{6,7},{7,6},{8,9},{9,8},{10,11... | collective-permute-start | bytes 36872 | tf_op jit(solution)/shard_map/ppermute | solution.py:35
  8.3 1.9 %collective-permute-start.5 = (f32[24,128]{1,0:T(8,128)S(1)}, f32[24,128]{1,0:T(8,128)S(1)}, u32[]{:S(2)}, u32[]{:S(2)}) collective-permute-start(f32[24,128]{1,0:T(8,128)S(1)} %collective-permute-done.1.refs_2_), channel_id=1, source_target_pairs={{0,1},{1,0},{2,3},{3,2},{4,5},{5,4},{6,7},{7,6},{8,9},{9,8},{10,11... | collective-permute-start | bytes 36872 | tf_op jit(solution)/shard_map/ppermute | solution.py:35
  24.3 15.3 %collective-permute-start.7 = (bf16[32,3072]{1,0:T(8,128)(2,1)S(1)}, bf16[32,3072]{1,0:T(8,128)(2,1)S(1)}, u32[]{:S(2)}, u32[]{:S(2)}) collective-permute-start(bf16[32,3072]{1,0:T(8,128)(2,1)S(1)} %shard_map.60.a0), channel_id=1, source_target_pairs={{0,32},{1,25},{2,34},{3,27},{4,36},{5,29},{6,38},{7,31},{8,40},{9,... | collective-permute-start | bytes 589832 | tf_op jit(solution)/shard_map/ppermute | solution.py:27
  36.3 5.7 %collective-permute-start.17 = (bf16[32,3072]{1,0:T(8,128)(2,1)S(1)}, bf16[32,3072]{1,0:T(8,128)(2,1)S(1)}, u32[]{:S(2)}, u32[]{:S(2)}) collective-permute-start(bf16[32,3072]{1,0:T(8,128)(2,1)S(1)} %shard_map.67.a0), channel_id=1, source_target_pairs={{0,96},{1,9},{2,98},{3,11},{4,100},{5,13},{6,102},{7,15},{8,104},{... | collective-permute-start | bytes 589832 | tf_op jit(solution)/shard_map/ppermute | solution.py:27
  38.1 6.9 %collective-permute-start.8 = (bf16[32,3072]{1,0:T(8,128)(2,1)S(1)}, bf16[32,3072]{1,0:T(8,128)(2,1)S(1)}, u32[]{:S(2)}, u32[]{:S(2)}) collective-permute-start(bf16[32,3072]{1,0:T(8,128)(2,1)S(1)} %shard_map.60.a0), channel_id=1, source_target_pairs={{0,96},{1,9},{2,98},{3,11},{4,100},{5,13},{6,102},{7,15},{8,104},{... | collective-permute-start | bytes 589832 | tf_op jit(solution)/shard_map/ppermute | solution.py:27
  39.6 6.9 %collective-permute-start.9 = (bf16[32,3072]{1,0:T(8,128)(2,1)S(1)}, bf16[32,3072]{1,0:T(8,128)(2,1)S(1)}, u32[]{:S(2)}, u32[]{:S(2)}) collective-permute-start(bf16[32,3072]{1,0:T(8,128)(2,1)S(1)} %collective-permute-done.7.a1), channel_id=1, source_target_pairs={{0,32},{1,25},{2,34},{3,27},{4,36},{5,29},{6,38},{7,31},{8,40},{9,... | collective-permute-start | bytes 589832 | tf_op jit(solution)/shard_map/ppermute | solution.py:27
  40.1 9.5 %collective-permute-start.18 = (bf16[32,3072]{1,0:T(8,128)(2,1)S(1)}, bf16[32,3072]{1,0:T(8,128)(2,1)S(1)}, u32[]{:S(2)}, u32[]{:S(2)}) collective-permute-start(bf16[32,3072]{1,0:T(8,128)(2,1)S(1)} %shard_map.67.a0), channel_id=1, source_target_pairs={{0,32},{1,25},{2,34},{3,27},{4,36},{5,29},{6,38},{7,31},{8,40},{9,... | collective-permute-start | bytes 589832 | tf_op jit(solution)/shard_map/ppermute | solution.py:27
  42.0 7.7 %collective-permute-start.19 = (bf16[32,3072]{1,0:T(8,128)(2,1)S(1)}, bf16[32,3072]{1,0:T(8,128)(2,1)S(1)}, u32[]{:S(2)}, u32[]{:S(2)}) collective-permute-start(bf16[32,3072]{1,0:T(8,128)(2,1)S(1)} %collective-permute-done.17.a1), channel_id=1, source_target_pairs={{0,96},{1,9},{2,98},{3,11},{4,100},{5,13},{6,102},{7,15},{8,104},{... | collective-permute-start | bytes 589832 | tf_op jit(solution)/shard_map/ppermute | solution.py:27
  46.6 12.6 %collective-permute-start.10 = (bf16[4,32,3072]{2,1,0:T(8,128)(2,1)S(1)}, bf16[4,32,3072]{2,1,0:T(8,128)(2,1)S(1)}, u32[]{:S(2)}, u32[]{:S(2)}) collective-permute-start(bf16[4,32,3072]{2,1,0:T(8,128)(2,1)S(1)} %shard_map.61.refs_0_), channel_id=1, source_target_pairs={{0,24},{1,33},{2,26},{3,35},{4,28},{5,37},{6,30},{7,39},{8,0},{9,4... | collective-permute-start | bytes 2359304 | tf_op jit(solution)/shard_map/ppermute | solution.py:27
  49.7 13.3 %collective-permute-start.20 = (bf16[4,32,3072]{2,1,0:T(8,128)(2,1)S(1)}, bf16[4,32,3072]{2,1,0:T(8,128)(2,1)S(1)}, u32[]{:S(2)}, u32[]{:S(2)}) collective-permute-start(bf16[4,32,3072]{2,1,0:T(8,128)(2,1)S(1)} %shard_map.68.refs_0_), channel_id=1, source_target_pairs={{0,8},{1,97},{2,10},{3,99},{4,12},{5,101},{6,14},{7,103},{8,16},{9... | collective-permute-start | bytes 2359304 | tf_op jit(solution)/shard_map/ppermute | solution.py:27
  51.6 19.8 %collective-permute-start.11 = (bf16[4,32,3072]{2,1,0:T(8,128)(2,1)S(1)}, bf16[4,32,3072]{2,1,0:T(8,128)(2,1)S(1)}, u32[]{:S(2)}, u32[]{:S(2)}) collective-permute-start(bf16[4,32,3072]{2,1,0:T(8,128)(2,1)S(1)} %shard_map.61.refs_0_), channel_id=1, source_target_pairs={{0,8},{1,97},{2,10},{3,99},{4,12},{5,101},{6,14},{7,103},{8,16},{9... | collective-permute-start | bytes 2359304 | tf_op jit(solution)/shard_map/ppermute | solution.py:27
  59.2 13.2 %collective-permute-start.12 = (bf16[4,32,3072]{2,1,0:T(8,128)(2,1)S(1)}, bf16[4,32,3072]{2,1,0:T(8,128)(2,1)S(1)}, u32[]{:S(2)}, u32[]{:S(2)}) collective-permute-start(bf16[4,32,3072]{2,1,0:T(8,128)(2,1)S(1)} %collective-permute-done.10.refs_1_), channel_id=1, source_target_pairs={{0,24},{1,33},{2,26},{3,35},{4,28},{5,37},{6,30},{7,39},{8,0},{9,4... | collective-permute-start | bytes 2359304 | tf_op jit(solution)/shard_map/ppermute | solution.py:27
  62.8 17.9 %collective-permute-start.21 = (bf16[4,32,3072]{2,1,0:T(8,128)(2,1)S(1)}, bf16[4,32,3072]{2,1,0:T(8,128)(2,1)S(1)}, u32[]{:S(2)}, u32[]{:S(2)}) collective-permute-start(bf16[4,32,3072]{2,1,0:T(8,128)(2,1)S(1)} %shard_map.68.refs_0_), channel_id=1, source_target_pairs={{0,24},{1,33},{2,26},{3,35},{4,28},{5,37},{6,30},{7,39},{8,0},{9,4... | collective-permute-start | bytes 2359304 | tf_op jit(solution)/shard_map/ppermute | solution.py:27
  63.0 17.8 %collective-permute-start.22 = (bf16[4,32,3072]{2,1,0:T(8,128)(2,1)S(1)}, bf16[4,32,3072]{2,1,0:T(8,128)(2,1)S(1)}, u32[]{:S(2)}, u32[]{:S(2)}) collective-permute-start(bf16[4,32,3072]{2,1,0:T(8,128)(2,1)S(1)} %collective-permute-done.20.refs_1_), channel_id=1, source_target_pairs={{0,8},{1,97},{2,10},{3,99},{4,12},{5,101},{6,14},{7,103},{8,16},{9... | collective-permute-start | bytes 2359304 | tf_op jit(solution)/shard_map/ppermute | solution.py:27
  74.4 8.5 %collective-permute-start.13 = (f32[4,80,512]{2,1,0:T(8,128)S(1)}, f32[4,80,512]{2,1,0:T(8,128)S(1)}, u32[]{:S(2)}, u32[]{:S(2)}) collective-permute-start(f32[4,80,512]{2,1,0:T(8,128)S(1)} %get-tuple-element.30), channel_id=1, source_target_pairs={{0,1},{1,0},{2,3},{3,2},{4,5},{5,4},{6,7},{7,6},{8,9},{9,8},{10,11... | collective-permute-start | bytes 1966088 | tf_op jit(solution)/shard_map/ppermute | solution.py:35
  82.9 2.0 %collective-permute-start.23 = (f32[4,64,512]{2,1,0:T(8,128)S(1)}, f32[4,64,512]{2,1,0:T(8,128)S(1)}, u32[]{:S(2)}, u32[]{:S(2)}) collective-permute-start(f32[4,64,512]{2,1,0:T(8,128)S(1)} %get-tuple-element.39), channel_id=1, source_target_pairs={{0,1},{1,0},{2,3},{3,2},{4,5},{5,4},{6,7},{7,6},{8,9},{9,8},{10,11... | collective-permute-start | bytes 1572872 | tf_op jit(solution)/shard_map/ppermute | solution.py:35
  83.0 8.2 %collective-permute-start.14 = (f32[80,512]{1,0:T(8,128)S(1)}, f32[80,512]{1,0:T(8,128)S(1)}, u32[]{:S(2)}, u32[]{:S(2)}) collective-permute-start(f32[80,512]{1,0:T(8,128)S(1)} %get-tuple-element.33), channel_id=1, source_target_pairs={{0,2},{1,7},{2,4},{3,1},{4,6},{5,3},{6,0},{7,5},{8,10},{9,15},{10,... | collective-permute-start | bytes 491528 | tf_op jit(solution)/shard_map/ppermute | solution.py:27
  84.9 6.2 %collective-permute-start.24 = (f32[64,512]{1,0:T(8,128)S(1)}, f32[64,512]{1,0:T(8,128)S(1)}, u32[]{:S(2)}, u32[]{:S(2)}) collective-permute-start(f32[64,512]{1,0:T(8,128)S(1)} %get-tuple-element.42), channel_id=1, source_target_pairs={{0,2},{1,7},{2,4},{3,1},{4,6},{5,3},{6,0},{7,5},{8,10},{9,15},{10,... | collective-permute-start | bytes 393224 | tf_op jit(solution)/shard_map/ppermute | solution.py:27
  85.3 15.2 %collective-permute-start.26 = (f32[64,512]{1,0:T(8,128)S(1)}, f32[64,512]{1,0:T(8,128)S(1)}, u32[]{:S(2)}, u32[]{:S(2)}) collective-permute-start(f32[64,512]{1,0:T(8,128)S(1)} %get-tuple-element.43), channel_id=1, source_target_pairs={{0,6},{1,3},{2,0},{3,5},{4,2},{5,7},{6,4},{7,1},{8,14},{9,11},{10,... | collective-permute-start | bytes 393224 | tf_op jit(solution)/shard_map/ppermute | solution.py:27
  88.6 6.0 %collective-permute-start.16 = (f32[80,512]{1,0:T(8,128)S(1)}, f32[80,512]{1,0:T(8,128)S(1)}, u32[]{:S(2)}, u32[]{:S(2)}) collective-permute-start(f32[80,512]{1,0:T(8,128)S(1)} %get-tuple-element.34), channel_id=1, source_target_pairs={{0,6},{1,3},{2,0},{3,5},{4,2},{5,7},{6,4},{7,1},{8,14},{9,11},{10,... | collective-permute-start | bytes 491528 | tf_op jit(solution)/shard_map/ppermute | solution.py:27
  91.2 9.3 %collective-permute-start.25 = (f32[64,512]{1,0:T(8,128)S(1)}, f32[64,512]{1,0:T(8,128)S(1)}, u32[]{:S(2)}, u32[]{:S(2)}) collective-permute-start(f32[64,512]{1,0:T(8,128)S(1)} %add.19), channel_id=1, source_target_pairs={{0,2},{1,7},{2,4},{3,1},{4,6},{5,3},{6,0},{7,5},{8,10},{9,15},{10,... | collective-permute-start | bytes 393224 | tf_op jit(solution)/shard_map/ppermute | solution.py:27
  91.3 7.9 %collective-permute-start.15 = (f32[80,512]{1,0:T(8,128)S(1)}, f32[80,512]{1,0:T(8,128)S(1)}, u32[]{:S(2)}, u32[]{:S(2)}) collective-permute-start(f32[80,512]{1,0:T(8,128)S(1)} %add.18), channel_id=1, source_target_pairs={{0,2},{1,7},{2,4},{3,1},{4,6},{5,3},{6,0},{7,5},{8,10},{9,15},{10,... | collective-permute-start | bytes 491528 | tf_op jit(solution)/shard_map/ppermute | solution.py:27
  101.8 5.5 %collective-permute-start.28 = (f32[128,128]{1,0:T(8,128)S(1)}, f32[128,128]{1,0:T(8,128)S(1)}, u32[]{:S(2)}, u32[]{:S(2)}) collective-permute-start(f32[128,128]{1,0:T(8,128)S(1)} %get-tuple-element.45), channel_id=1, source_target_pairs={{0,32},{1,9},{2,34},{3,11},{4,36},{5,13},{6,38},{7,15},{8,40},{9,1... | collective-permute-start | bytes 196616 | tf_op jit(solution)/shard_map/ppermute | solution.py:27
  101.8 5.8 %collective-permute-start.29 = (f32[128,128]{1,0:T(8,128)S(1)}, f32[128,128]{1,0:T(8,128)S(1)}, u32[]{:S(2)}, u32[]{:S(2)}) collective-permute-start(f32[128,128]{1,0:T(8,128)S(1)} %get-tuple-element.45), channel_id=1, source_target_pairs={{0,96},{1,25},{2,98},{3,27},{4,100},{5,29},{6,102},{7,31},{8,104},... | collective-permute-start | bytes 196616 | tf_op jit(solution)/shard_map/ppermute | solution.py:27
  105.0 6.1 %collective-permute-start.27 = (f32[128,128]{1,0:T(8,128)S(1)}, f32[128,128]{1,0:T(8,128)S(1)}, u32[]{:S(2)}, u32[]{:S(2)}) collective-permute-start(f32[128,128]{1,0:T(8,128)S(1)} %get-tuple-element.45), channel_id=1, source_target_pairs={{0,64},{1,17},{2,66},{3,19},{4,68},{5,21},{6,70},{7,23},{8,72},{9,... | collective-permute-start | bytes 196616 | tf_op jit(solution)/shard_map/ppermute | solution.py:27
  111.1 5.8 %collective-permute-start.31 = (f32[128,128]{1,0:T(8,128)S(1)}, f32[128,128]{1,0:T(8,128)S(1)}, u32[]{:S(2)}, u32[]{:S(2)}) collective-permute-start(f32[128,128]{1,0:T(8,128)S(1)} %maximum_maximum_fusion.1), channel_id=1, source_target_pairs={{0,8},{1,33},{2,10},{3,35},{4,12},{5,37},{6,14},{7,39},{8,16},{9,4... | collective-permute-start | bytes 196616 | tf_op jit(solution)/shard_map/ppermute | solution.py:27
  111.2 5.7 %collective-permute-start.32 = (f32[128,128]{1,0:T(8,128)S(1)}, f32[128,128]{1,0:T(8,128)S(1)}, u32[]{:S(2)}, u32[]{:S(2)}) collective-permute-start(f32[128,128]{1,0:T(8,128)S(1)} %maximum_maximum_fusion.1), channel_id=1, source_target_pairs={{0,24},{1,97},{2,26},{3,99},{4,28},{5,101},{6,30},{7,103},{8,0},{9... | collective-permute-start | bytes 196616 | tf_op jit(solution)/shard_map/ppermute | solution.py:27
  114.8 5.8 %collective-permute-start.30 = (f32[128,128]{1,0:T(8,128)S(1)}, f32[128,128]{1,0:T(8,128)S(1)}, u32[]{:S(2)}, u32[]{:S(2)}) collective-permute-start(f32[128,128]{1,0:T(8,128)S(1)} %maximum_maximum_fusion.1), channel_id=1, source_target_pairs={{0,16},{1,65},{2,18},{3,67},{4,20},{5,69},{6,22},{7,71},{8,24},{9,... | collective-permute-start | bytes 196616 | tf_op jit(solution)/shard_map/ppermute | solution.py:27
  (5 other events, 18.5 us)
where the time goes:
time: 121 us
  starting transfers between devices  42.7 us (35%)
  waiting for transfers between devices  42.6 us (35%)
  Pallas kernels  29.4 us (24%)
  local copies, waits for them, and re-layouts  4.62 us (4%)
    ppermute x24, waiting for transfers between devices, shift(): lax.ppermute(value, AXES, [(at(*d), at(*target(*d))) for d in PLACES])  37.3 us
    ppermute x24, starting transfers between devices, shift(): lax.ppermute(value, AXES, [(at(*d), at(*target(*d))) for d in PLACES])  35.4 us
    pallas_call x3, Pallas kernels, lookup(): pl.pallas_call(lookup_kernel, grid=(1,), out_shape=out_of(shape, jnp.bflo...  20.7 us
    ppermute x3, starting transfers between devices, along(): lax.ppermute(value, axis, [(i, (i + step) % RING) for i in range(RING)])  6.69 us
    unnamed x8, local copies, waits for them, and re-layouts  4.62 us
    pallas_call x2, Pallas kernels, product(): pl.pallas_call(lambda *refs: product_kernel(*refs, turn_near=turn_near, t...  4.16 us
    ppermute x6, waiting for transfers between devices, other_core(): return lax.ppermute(value, 'c', [(0, 1), (1, 0)])  2.89 us
  transfers between devices with their start and end apart: 33, of which 19 were waited for; matrix products, arithmetic and copies ran while one was open for 0% of the time, Pallas kernels for 14%

commit v1 on v0

--- a/solution.py
+++ b/solution.py
@@ -76,12 +76,23 @@
     )(dosage)
 
 
-def table_kernel(*refs):
-    blocks, (table_ref, scale_ref, var_ref, code_ref) = refs[:8], refs[8:]
+def table_kernel(pair_ref, mine_ref, theirs_ref, far_ref, other_ref, *rest):
+    table_ref, scale_ref, var_ref, code_ref = rest
     z, c = lax.axis_index("z"), lax.axis_index("c")
-    depth = blocks[0].shape[0]
-    count = len(blocks) * blocks[0].size
-    values = [r[...] for r in blocks]
+    step = 1 - 2 * c
+    depth = far_ref.shape[0]
+    blocks = (
+        (pair_ref[:depth], z, c),
+        (pair_ref[depth:], z, 1 - c),
+        (mine_ref[:depth], z - step, c),
+        (mine_ref[depth:], z - step, 1 - c),
+        (theirs_ref[:depth], z + step, 1 - c),
+        (theirs_ref[depth:], z + step, c),
+        (far_ref[...], z + 2, c),
+        (other_ref[...], z + 2, 1 - c),
+    )
+    values = [b[0] for b in blocks]
+    count = len(values) * values[0].size
     mean = jnp.sum(sum(values)) / count
     values = [v - mean for v in values]
     var_ref[0, 0] = jnp.sum(sum(v * v for v in values)) / count
@@ -90,19 +101,27 @@
     for r in rounded[1:]:
         most = jnp.maximum(most, jnp.abs(r))
     most = jnp.full((1, LOW), jnp.maximum(jnp.max(most), 1e-30), jnp.float32)
-    for k, r in enumerate(rounded):
+    for r, (_, at_z, core) in zip(rounded, blocks):
         code = jnp.round(jnp.sqrt(jnp.sqrt(jnp.abs(r) / most)) * 32767.0).astype(jnp.int32)
         code = jnp.where(r < 0, -code, code)
-        core = c if k < RING else 1 - c
-        start = (((z + RING - k % RING) % RING) * 2 + core) * depth
+        start = (((at_z + RING) % RING) * 2 + core) * depth
         code_ref[pl.ds(pl.multiple_of(start, 8), depth), :] = code
     half = table_ref.shape[0]
     table_ref[...] = lax.shift_left(code_ref[half:, :], 16) + (code_ref[:half, :] & 0xFFFF)
     scale_ref[...] = jnp.sqrt(jnp.sqrt(most)) / 32767.0
 
 
-def make_table(blocks):
-    rows = len(blocks) * blocks[0].shape[0]
+def make_table(own):
+    def line(x, y, z, c):
+        return (x, y, z + 1 - 2 * c, c)
+
+    other = other_core(own)
+    far = along(own, "z", 2)
+    pair = join(own, other)
+    mine = shift(pair, line)
+    far_other = other_core(far)
+    theirs = other_core(mine)
+    rows = 2 * RING * own.shape[0]
     return pl.pallas_call(
         table_kernel,
         out_shape=(
@@ -110,11 +129,40 @@
             out_of((1, LOW), jnp.float32),
             out_of((1, 1), jnp.float32),
         ),
-        in_specs=[VMEM] * 8,
+        in_specs=[VMEM] * 5,
         out_specs=(VMEM, VMEM, SMEM),
         scratch_shapes=[pltpu.VMEM((rows, LOW), jnp.int32)],
         compiler_params=room(2),
-    )(*blocks)
+    )(pair, mine, theirs, far, far_other)
+
+
+def join_kernel(a_ref, b_ref, out_ref):
+    out_ref[: a_ref.shape[0]] = a_ref[...]
+    out_ref[a_ref.shape[0] :] = b_ref[...]
+
+
+def join(a, b):
+    return pl.pallas_call(
+        join_kernel,
+        out_shape=out_of((a.shape[0] + b.shape[0], a.shape[1]), a.dtype),
+        in_specs=[VMEM] * 2,
+        out_specs=VMEM,
+        compiler_params=room(2),
+    )(a, b)
+
+
+def copy_kernel(a_ref, out_ref):
+    out_ref[...] = a_ref[...]
+
+
+def fetched(a):
+    return pl.pallas_call(
+        copy_kernel,
+        out_shape=out_of(a.shape, a.dtype),
+        in_specs=[VMEM],
+        out_specs=VMEM,
+        compiler_params=room(4),
+    )(a)
 
 
 def lookup_kernel(index_ref, table_ref, scale_ref, *rest):
@@ -175,7 +223,7 @@
     )(index, table, scale, *before)
 
 
-def ring_gather(value, first, turn):
+def ring_gather(value, first, turn, dim):
     def line(sign):
         def target(x, y, z, c):
             step = sign if c == turn else -sign
@@ -187,8 +235,26 @@
 
     behind = shift(value, line(1))
     ahead = shift(value, line(-1))
-    onward = shift(behind, line(1))
-    return [value, behind, ahead, onward]
+    low = shift(half_of(behind, 0, dim), line(1))
+    high = shift(half_of(ahead, 1, dim), line(-1))
+    return [value, behind, ahead, low, high]
+
+
+def half_kernel(a_ref, out_ref, *, which, dim):
+    size = out_ref.shape[dim]
+    part = pl.ds(which * size, size)
+    out_ref[...] = a_ref[part] if dim == 0 else a_ref[:, part]
+
+
+def half_of(a, which, dim):
+    shape = tuple(n // 2 if d == dim else n for d, n in enumerate(a.shape))
+    return pl.pallas_call(
+        lambda *refs: half_kernel(*refs, which=which, dim=dim),
+        out_shape=out_of(shape, a.dtype),
+        in_specs=[VMEM],
+        out_specs=VMEM,
+        compiler_params=room(3),
+    )(a)
 
 
 def offset(k, turn, c):
@@ -196,51 +262,89 @@
     return (0, -step, step, 2)[k]
 
 
-def stack_kernel(a0, a1, a2, a3, out_ref):
-    for k, a in enumerate((a0, a1, a2, a3)):
-        out_ref[k] = a[...]
-
-
-def stacked(pieces):
-    return pl.pallas_call(
-        stack_kernel,
-        out_shape=out_of((len(pieces), *pieces[0].shape), pieces[0].dtype),
+def stack_kernel(own, behind, ahead, opposite, out_ref, *, which):
+    rows = out_ref.shape[1]
+    part = slice(which * rows, (which + 1) * rows)
+    for k, a in enumerate((own, behind, ahead)):
+        out_ref[k] = a[part, :]
+    out_ref[3] = opposite[...]
+
+
+def stacked(near, which):
+    own, behind, ahead = near[:3]
+    opposite = near[3 + which]
+    return pl.pallas_call(
+        lambda *refs: stack_kernel(*refs, which=which),
+        out_shape=out_of((RING, *opposite.shape), own.dtype),
         in_specs=[VMEM] * 4,
         out_specs=VMEM,
-        compiler_params=room(3),
-    )(*pieces)
-
-
-def product_kernel(
-    a0, a1, a2, a3, dosage_ref, totals_ref, keep_ref, send_ref, lhs_ref, *, turn_near, turn_far
+        compiler_params=room(4),
+    )(own, behind, ahead, opposite)
+
+
+def early_kernel(a0, a1, a2, dosage_ref, out_ref, lhs_ref):
+    rows = a0.shape[0] * a0.shape[1]
+    for u, a in enumerate((a0, a1, a2)):
+        lhs_ref[u * rows : (u + 1) * rows, :] = a[...].reshape(rows, a.shape[2])
+    out_ref[...] = jnp.dot(lhs_ref[...], dosage_ref[...], preferred_element_type=jnp.float32)
+
+
+def early_product(pieces, dosage):
+    rows = sum(p.shape[0] * p.shape[1] for p in pieces)
+    return pl.pallas_call(
+        early_kernel,
+        out_shape=out_of((rows, dosage.shape[1]), jnp.float32),
+        in_specs=[VMEM] * 4,
+        out_specs=VMEM,
+        scratch_shapes=[pltpu.VMEM((rows, dosage.shape[0]), jnp.bfloat16)],
+        compiler_params=room(16),
+    )(*pieces, dosage)
+
+
+def late_kernel(
+    early_ref, low_ref, high_ref, dosage_ref, totals_ref, keep_ref, send_ref, lhs_ref, all_ref,
+    *, turn_near, turn_far,
 ):
-    rows = a0.shape[1]
+    rows = low_ref.shape[1]
+    half = low_ref.shape[0] * rows
     extra = keep_ref.shape[1] - 2 * rows
     dest = destinations(turn_near, turn_far)
-    for u, a in enumerate((a0, a1, a2, a3)):
+
+    def place(u, t, value):
+        start = pl.multiple_of(dest(u, t) * rows, rows)
+        all_ref[pl.ds(start, rows), :] = value
+
+    lhs_ref[:half, :] = low_ref[...].reshape(half, lhs_ref.shape[1])
+    lhs_ref[half:, :] = high_ref[...].reshape(half, lhs_ref.shape[1])
+    part = jnp.dot(lhs_ref[...], dosage_ref[...], preferred_element_type=jnp.float32)
+    for u in range(RING - 1):
         for t in range(RING):
-            start = pl.multiple_of(dest(u, t) * rows, rows)
-            lhs_ref[pl.ds(start, rows), :] = a[t]
-    part = jnp.dot(lhs_ref[...], dosage_ref[...], preferred_element_type=jnp.float32)
+            start = (u * RING + t) * rows
+            place(u, t, early_ref[start : start + rows, :])
+    for t in range(RING):
+        place(RING - 1, t, part[t * rows : (t + 1) * rows])
     for h, ref in enumerate((keep_ref, send_ref)):
         for k in range(RING):
             start = (h * RING + k) * 2 * rows
-            ref[k, : 2 * rows, :] = part[start : start + 2 * rows]
+            ref[k, : 2 * rows, :] = all_ref[start : start + 2 * rows, :]
             if extra:
                 ref[k, 2 * rows :, :] = totals_ref[...]
 
 
-def product(pieces, dosage, totals, with_totals, turn_near, turn_far):
-    rows = pieces[0].shape[1]
+def late_product(early, low, high, dosage, totals, with_totals, turn_near, turn_far):
+    rows = low.shape[1]
     shape = (RING, 2 * rows + (totals.shape[0] if with_totals else 0), dosage.shape[1])
     return pl.pallas_call(
-        lambda *refs: product_kernel(*refs, turn_near=turn_near, turn_far=turn_far),
+        lambda *refs: late_kernel(*refs, turn_near=turn_near, turn_far=turn_far),
         out_shape=(out_of(shape, jnp.float32), out_of(shape, jnp.float32)),
-        in_specs=[VMEM] * 6,
+        in_specs=[VMEM] * 5,
         out_specs=(VMEM, VMEM),
-        scratch_shapes=[pltpu.VMEM((rows * RING * RING, dosage.shape[0]), jnp.bfloat16)],
-        compiler_params=room(20),
-    )(*pieces, dosage, totals)
+        scratch_shapes=[
+            pltpu.VMEM((RING * rows, dosage.shape[0]), jnp.bfloat16),
+            pltpu.VMEM((RING * RING * rows, dosage.shape[1]), jnp.float32),
+        ],
+        compiler_params=room(16),
+    )(early, low, high, dosage, totals)
 
 
 def add_kernel(a_ref, b_ref, o0, o1, o2, o3):
@@ -281,7 +385,10 @@
     return target
 
 
-def reduced(keep, send):
+def reduced(far, dosage, totals, with_totals):
+    early = early_product(far[:3], dosage)
+    low, high = far[3:]
+    keep, send = late_product(early, low, high, dosage, totals, with_totals, 0, 1)
     got = other_core(send)
     own, ahead, opposite, behind = core_sum(keep, got)
     passing = shift(opposite, z_line(1))
@@ -334,7 +441,7 @@
     chosen = jnp.where(jnp.broadcast_to(ends >= 0, (both, LOW)), chosen, 0.0)
     for h, place in enumerate(places):
         z_ref[place : place + rows, :] = z[h * rows : (h + 1) * rows]
-        most_ref[place : place + rows, :] = chosen[h * rows : (h + 1) * rows]
+        most_ref[place : place + rows, :] = chosen[h * rows : (h + 1) * rows].astype(most_ref.dtype)
 
 
 def final_first(pheno_var, ends, parts, extra, count):
@@ -343,7 +450,7 @@
         lambda *refs: final_kernel(*refs, extra=extra, count=count),
         out_shape=(
             out_of((rows, width), jnp.float32),
-            out_of((rows, ends.shape[1]), jnp.float32),
+            out_of((rows, ends.shape[1]), jnp.bfloat16),
             out_of((1, width), jnp.float32),
         ),
         in_specs=[SMEM] + [VMEM] * 4,
@@ -358,7 +465,7 @@
         lambda *refs: final_kernel(*refs, extra=0, count=count),
         out_shape=(
             out_of((CHUNKS * rows, width), jnp.float32),
-            out_of((CHUNKS * rows, ends.shape[1]), jnp.float32),
+            out_of((CHUNKS * rows, ends.shape[1]), jnp.bfloat16),
         ),
         in_specs=[VMEM] * 7,
         out_specs=(VMEM,) * 2,
@@ -380,30 +487,20 @@
 def per_device(dosage, phenotype, perm_index, seg_lengths):
     samples, width = dosage.shape
     x, y = lax.axis_index("x"), lax.axis_index("y")
-    own = phenotype.reshape(-1, LOW)
-    mine = [own] + [along(own, "z", k) for k in (1, 2, 3)]
+    perm_index = fetched(perm_index)
     dosage_bf, totals = convert_dosage(dosage)
-    table, scale, pheno_var = make_table(mine + [other_core(m) for m in mine])
+    table, scale, pheno_var = make_table(phenotype.reshape(-1, LOW))
     ends = (jnp.cumsum(seg_lengths) - 1 - (x * RING + y) * width)[None, :].astype(jnp.int32)
     count = float(samples * lax.axis_size("z") * lax.axis_size("c"))
 
-    rows = perm_index.shape[0] // CHUNKS
-    part = rows // 2
-    traits = lookup(perm_index, 0, rows, table, scale)
-    near = ring_gather(traits, True, 0)
-    traits = lookup(perm_index, 2, part, table, scale)
-    traits = lookup(perm_index, 3, part, table, scale, (traits,))
-    far = ring_gather(stacked(near), False, 1)
-    near = ring_gather(traits, True, 1)
-    keep, send = product(far, dosage_bf, totals, True, 0, 1)
-    parts = reduced(keep, send)
+    traits = lookup(perm_index, 0, perm_index.shape[0], table, scale)
+    near = ring_gather(traits, True, 0, 0)
+    far = [ring_gather(stacked(near, k), False, 1, 0) for k in range(CHUNKS)]
+    parts = reduced(far[0], dosage_bf, totals, True)
     z0, most0, inverse = final_first(pheno_var, ends, parts, totals.shape[0], count)
-
-    far = ring_gather(stacked(near), False, 0)
-    keep, send = product(far, dosage_bf, totals, False, 1, 0)
-    parts = reduced(keep, send)
+    parts = reduced(far[1], dosage_bf, totals, False)
     zscore, most = final_second(ends, inverse, z0, most0, parts, count)
-    return (zscore, largest(largest(most, True), False))
+    return (zscore, largest(largest(most, True), False).astype(jnp.float32))
 
 
 def solution(mesh):

time: 121 us -> 119 us (0.983)
  local copies, waits for them, and re-layouts: 4.62 us -> 1.85 us
    ppermute x3 -> x1, starting transfers between devices: 6.69 us -> 3.58 us  [along(): lax.ppermute(value, axis, [(i, (i + step) % RING) for i in range(RING)])]
    unnamed x8, local copies, waits for them, and re-layouts: 4.62 us -> 1.85 us
    ppermute x24 -> x25, starting transfers between devices: 35.4 us -> 37.8 us  [shift(): lax.ppermute(value, AXES, [(at(*d), at(*target(*d))) for d in PLACES])]
    ppermute x24 -> x25, waiting for transfers between devices: 37.3 us -> 38.6 us  [shift(): lax.ppermute(value, AXES, [(at(*d), at(*target(*d))) for d in PLACES])]
    ppermute x6 -> x5, waiting for transfers between devices: 2.89 us -> 2.06 us  [other_core(): return lax.ppermute(value, 'c', [(0, 1), (1, 0)])]
    pallas_call x4 -> x14, Pallas kernels: 4.26 us -> 4.6 us  [the longest x2 2.74 us: early_product(): pl.pallas_call(early_kernel, out_shape=out_of((rows, dosage.shape[1]), jn...]
    pallas_call x3 -> x1, Pallas kernels: 20.7 us -> 20.7 us  [lookup(): pl.pallas_call(lookup_kernel, grid=(1,), out_shape=out_of(shape, jnp.bflo...]
  transfers between devices with their start and end apart: 33 -> 31, of which waited for: 19 -> 16; matrix products, arithmetic and copies ran while one was open for 0% -> 0% of each run, Pallas kernels for 14% -> 6%
where the time goes in v1:
time: 119 us; the launch traced here: 118 us
  starting transfers between devices  42.4 us (36%)
  waiting for transfers between devices  42.2 us (35%)
  Pallas kernels  29.8 us (25%)
  local copies, waits for them, and re-layouts  1.85 us (2%)
    ppermute x25, waiting for transfers between devices, shift(): lax.ppermute(value, AXES, [(at(*d), at(*target(*d))) for d in PLACES])  38.6 us
    ppermute x25, starting transfers between devices, shift(): lax.ppermute(value, AXES, [(at(*d), at(*target(*d))) for d in PLACES])  37.8 us
    pallas_call x1, Pallas kernels, lookup(): pl.pallas_call(lookup_kernel, grid=(1,), out_shape=out_of(shape, jnp.bflo...  20.7 us
    ppermute x1, starting transfers between devices, along(): lax.ppermute(value, axis, [(i, (i + step) % RING) for i in range(RING)])  3.58 us
    pallas_call x2, Pallas kernels, early_product(): pl.pallas_call(early_kernel, out_shape=out_of((rows, dosage.shape[1]), jn...  2.74 us
  transfers between devices with their start and end apart: 31, of which 16 were waited for; matrix products, arithmetic and copies ran while one was open for 0% of the time, Pallas kernels for 6%

profile of v1, /device:TPU:0, one launch (start us, length us, event | category | flops | bytes accessed | tf_op | source)
XLA Modules:
  0.0 118.2 jit_solution(6432397749580292647)
XLA Ops:
  0.7 1.4 %collective-permute-done.b_ref = f32[24,128]{1,0:T(8,128)S(1)} collective-permute-done((f32[24,128]{1,0:T(8,128)}, f32[24,128]{1,0:T(8,128)S(1)}, u32[]{:S(2)}, u32[]{:S(2)}) %collective-permute-start) | collective-permute-done | bytes 12320 | tf_op jit(solution)/shard_map/ppermute | solution.py:35
  2.8 2.0 %collective-permute-start.1 = (f32[48,128]{1,0:T(8,128)S(1)}, f32[48,128]{1,0:T(8,128)S(1)}, u32[]{:S(2)}, u32[]{:S(2)}) collective-permute-start(f32[48,128]{1,0:T(8,128)S(1)} %shard_map.59.pair_ref), channel_id=1, source_target_pairs={{0,2},{1,7},{2,4},{3,1},{4,6},{5,3},{6,0},{7,5},{8,10},{9,15},{10,... | collective-permute-start | bytes 73736 | tf_op jit(solution)/shard_map/ppermute | solution.py:27
  4.8 3.6 %collective-permute-start.3 = (f32[24,128]{1,0:T(8,128)S(1)}, f32[24,128]{1,0:T(8,128)S(1)}, u32[]{:S(2)}, u32[]{:S(2)}) collective-permute-start(f32[24,128]{1,0:T(8,128)S(1)} %bitcast.4), channel_id=1, source_target_pairs={{0,4},{2,6},{4,0},{6,2},{1,5},{3,7},{5,1},{7,3},{8,12},{10,14},{12... | collective-permute-start | bytes 36872 | tf_op jit(solution)/shard_map/ppermute | solution.py:31
  8.8 1.6 %collective-permute-done.3.far_ref = f32[24,128]{1,0:T(8,128)S(1)} collective-permute-done((f32[24,128]{1,0:T(8,128)S(1)}, f32[24,128]{1,0:T(8,128)S(1)}, u32[]{:S(2)}, u32[]{:S(2)}) %collective-permute-start.3) | collective-permute-done | bytes 12320 | tf_op jit(solution)/shard_map/ppermute | solution.py:31
  12.9 20.7 %shard_map.62.refs_0_ = bf16[64,3072]{1,0:T(8,128)(2,1)S(1)} custom-call(s32[64,3072]{1,0:T(8,128)S(1)} %shard_map.61.index_ref, s32[96,128]{1,0:T(8,128)S(1)} %get-tuple-element.25.table_ref, f32[1,128]{1,0:T(1,128)S(1)} %get-tuple-element.26.scale_ref), custom_call_target="tpu_custom_call" | custom-call | tf_op jit(solution)/shard_map/pallas_call | solution.py:211
  33.6 1.6 %collective-permute-start.5 = (bf16[64,3072]{1,0:T(8,128)(2,1)S(1)}, bf16[64,3072]{1,0:T(8,128)(2,1)S(1)}, u32[]{:S(2)}, u32[]{:S(2)}) collective-permute-start(bf16[64,3072]{1,0:T(8,128)(2,1)S(1)} %shard_map.62.refs_0_), channel_id=1, source_target_pairs={{0,32},{1,25},{2,34},{3,27},{4,36},{5,29},{6,38},{7,31},{8,40},{9,... | collective-permute-start | bytes 1179656 | tf_op jit(solution)/shard_map/ppermute | solution.py:27
  35.1 1.7 %collective-permute-start.6 = (bf16[64,3072]{1,0:T(8,128)(2,1)S(1)}, bf16[64,3072]{1,0:T(8,128)(2,1)S(1)}, u32[]{:S(2)}, u32[]{:S(2)}) collective-permute-start(bf16[64,3072]{1,0:T(8,128)(2,1)S(1)} %shard_map.62.refs_0_), channel_id=1, source_target_pairs={{0,96},{1,9},{2,98},{3,11},{4,100},{5,13},{6,102},{7,15},{8,104},{... | collective-permute-start | bytes 1179656 | tf_op jit(solution)/shard_map/ppermute | solution.py:27
  36.9 5.8 %collective-permute-done.5.refs_0_.refs_1_ = bf16[64,3072]{1,0:T(8,128)(2,1)S(1)} collective-permute-done((bf16[64,3072]{1,0:T(8,128)(2,1)S(1)}, bf16[64,3072]{1,0:T(8,128)(2,1)S(1)}, u32[]{:S(2)}, u32[]{:S(2)}) %collective-permute-start.5) | collective-permute-done | bytes 393248 | tf_op jit(solution)/shard_map/ppermute | solution.py:27
  43.0 3.0 %collective-permute-start.16 = (bf16[32,3072]{1,0:T(8,128)(2,1)S(1)}, bf16[32,3072]{1,0:T(8,128)(2,1)S(1)}, u32[]{:S(2)}, u32[]{:S(2)}) collective-permute-start(bf16[32,3072]{1,0:T(8,128)(2,1)S(1)} %shard_map.72), channel_id=1, source_target_pairs={{0,96},{1,9},{2,98},{3,11},{4,100},{5,13},{6,102},{7,15},{8,104},{... | collective-permute-start | bytes 589832 | tf_op jit(solution)/shard_map/ppermute | solution.py:27
  46.0 3.6 %collective-permute-done.7.refs_3_ = bf16[32,3072]{1,0:T(8,128)(2,1)S(1)} collective-permute-done((bf16[32,3072]{1,0:T(8,128)(2,1)S(1)}, bf16[32,3072]{1,0:T(8,128)(2,1)S(1)}, u32[]{:S(2)}, u32[]{:S(2)}) %collective-permute-start.7) | collective-permute-done | bytes 196640 | tf_op jit(solution)/shard_map/ppermute | solution.py:27
  49.7 3.1 %collective-permute-start.8 = (bf16[4,32,3072]{2,1,0:T(8,128)(2,1)S(1)}, bf16[4,32,3072]{2,1,0:T(8,128)(2,1)S(1)}, u32[]{:S(2)}, u32[]{:S(2)}) collective-permute-start(bf16[4,32,3072]{2,1,0:T(8,128)(2,1)S(1)} %shard_map.64.a0), channel_id=1, source_target_pairs={{0,24},{1,33},{2,26},{3,35},{4,28},{5,37},{6,30},{7,39},{8,0},{9,4... | collective-permute-start | bytes 2359304 | tf_op jit(solution)/shard_map/ppermute | solution.py:27
  52.8 3.3 %collective-permute-start.17 = (bf16[4,32,3072]{2,1,0:T(8,128)(2,1)S(1)}, bf16[4,32,3072]{2,1,0:T(8,128)(2,1)S(1)}, u32[]{:S(2)}, u32[]{:S(2)}) collective-permute-start(bf16[4,32,3072]{2,1,0:T(8,128)(2,1)S(1)} %shard_map.73.a0), channel_id=1, source_target_pairs={{0,24},{1,33},{2,26},{3,35},{4,28},{5,37},{6,30},{7,39},{8,0},{9,4... | collective-permute-start | bytes 2359304 | tf_op jit(solution)/shard_map/ppermute | solution.py:27
  56.1 6.1 %collective-permute-done.8.a1.refs_0_ = bf16[4,32,3072]{2,1,0:T(8,128)(2,1)S(1)} collective-permute-done((bf16[4,32,3072]{2,1,0:T(8,128)(2,1)S(1)}, bf16[4,32,3072]{2,1,0:T(8,128)(2,1)S(1)}, u32[]{:S(2)}, u32[]{:S(2)}) %collective-permute-start.8) | collective-permute-done | bytes 786464 | tf_op jit(solution)/shard_map/ppermute | solution.py:27
  62.3 3.8 %collective-permute-start.10 = (bf16[2,32,3072]{2,1,0:T(8,128)(2,1)S(1)}, bf16[2,32,3072]{2,1,0:T(8,128)(2,1)S(1)}, u32[]{:S(2)}, u32[]{:S(2)}) collective-permute-start(bf16[2,32,3072]{2,1,0:T(8,128)(2,1)S(1)} %shard_map.67), channel_id=1, source_target_pairs={{0,24},{1,33},{2,26},{3,35},{4,28},{5,37},{6,30},{7,39},{8,0},{9,4... | collective-permute-start | bytes 1179656 | tf_op jit(solution)/shard_map/ppermute | solution.py:27
  66.2 4.5 %collective-permute-done.17.a1.refs_0_ = bf16[4,32,3072]{2,1,0:T(8,128)(2,1)S(1)} collective-permute-done((bf16[4,32,3072]{2,1,0:T(8,128)(2,1)S(1)}, bf16[4,32,3072]{2,1,0:T(8,128)(2,1)S(1)}, u32[]{:S(2)}, u32[]{:S(2)}) %collective-permute-start.17) | collective-permute-done | bytes 786464 | tf_op jit(solution)/shard_map/ppermute | solution.py:27
  70.7 3.8 %collective-permute-start.19 = (bf16[2,32,3072]{2,1,0:T(8,128)(2,1)S(1)}, bf16[2,32,3072]{2,1,0:T(8,128)(2,1)S(1)}, u32[]{:S(2)}, u32[]{:S(2)}) collective-permute-start(bf16[2,32,3072]{2,1,0:T(8,128)(2,1)S(1)} %shard_map.75), channel_id=1, source_target_pairs={{0,24},{1,33},{2,26},{3,35},{4,28},{5,37},{6,30},{7,39},{8,0},{9,4... | collective-permute-start | bytes 1179656 | tf_op jit(solution)/shard_map/ppermute | solution.py:27
  75.6 1.4 %shard_map.66.refs_0_ = f32[384,512]{1,0:T(8,128)S(1)} custom-call(bf16[4,32,3072]{2,1,0:T(8,128)(2,1)S(1)} %shard_map.64.a0, bf16[4,32,3072]{2,1,0:T(8,128)(2,1)S(1)} %collective-permute-done.8.a1.refs_0_, bf16[4,32,3072]{2,1,0:T(8,128)(2,1)S(1)} %collective-permute-done.9.a2.refs_0_, bf16[3072,512]{1,0:T(8,128)(2,1)S(1)} %get-tuple-element.27.dosage_ref.refs_3_), custom_call_target="tpu_custom_call" | custom-call | tf_op jit(solution)/shard_map/pallas_call | solution.py:294
  77.0 1.6 %collective-permute-done.11.refs_2_ = bf16[2,32,3072]{2,1,0:T(8,128)(2,1)S(1)} collective-permute-done((bf16[2,32,3072]{2,1,0:T(8,128)(2,1)S(1)}, bf16[2,32,3072]{2,1,0:T(8,128)(2,1)S(1)}, u32[]{:S(2)}, u32[]{:S(2)}) %collective-permute-start.11) | collective-permute-done | bytes 393248 | tf_op jit(solution)/shard_map/ppermute | solution.py:27
  79.7 1.4 %shard_map.74.refs_0_ = f32[384,512]{1,0:T(8,128)S(1)} custom-call(bf16[4,32,3072]{2,1,0:T(8,128)(2,1)S(1)} %shard_map.73.a0, bf16[4,32,3072]{2,1,0:T(8,128)(2,1)S(1)} %collective-permute-done.17.a1.refs_0_, bf16[4,32,3072]{2,1,0:T(8,128)(2,1)S(1)} %collective-permute-done.18.a2.refs_0_, bf16[3072,512]{1,0:T(8,128)(2,1)S(1)} %get-tuple-element.27.dosage_ref.refs_3_), custom_call_target="tpu_custom_call" | custom-call | tf_op jit(solution)/shard_map/pallas_call | solution.py:294
  81.0 2.5 %collective-permute-done.20.refs_2_ = bf16[2,32,3072]{2,1,0:T(8,128)(2,1)S(1)} collective-permute-done((bf16[2,32,3072]{2,1,0:T(8,128)(2,1)S(1)}, bf16[2,32,3072]{2,1,0:T(8,128)(2,1)S(1)}, u32[]{:S(2)}, u32[]{:S(2)}) %collective-permute-start.20) | collective-permute-done | bytes 393248 | tf_op jit(solution)/shard_map/ppermute | solution.py:27
  84.5 1.1 collective-permute-start.13
  87.8 2.2 %collective-permute-start.24 = (f32[64,512]{1,0:T(8,128)S(1)}, f32[64,512]{1,0:T(8,128)S(1)}, u32[]{:S(2)}, u32[]{:S(2)}) collective-permute-start(f32[64,512]{1,0:T(8,128)S(1)} %get-tuple-element.43), channel_id=1, source_target_pairs={{0,6},{1,3},{2,0},{3,5},{4,2},{5,7},{6,4},{7,1},{8,14},{9,11},{10,... | collective-permute-start | bytes 393224 | tf_op jit(solution)/shard_map/ppermute | solution.py:27
  90.0 3.2 %collective-permute-done.22 = f32[64,512]{1,0:T(8,128)S(1)} collective-permute-done((f32[64,512]{1,0:T(8,128)S(1)}, f32[64,512]{1,0:T(8,128)S(1)}, u32[]{:S(2)}, u32[]{:S(2)}) %collective-permute-start.22) | collective-permute-done | bytes 131104 | tf_op jit(solution)/shard_map/ppermute | solution.py:27
  93.8 2.7 %collective-permute-start.15 = (f32[80,512]{1,0:T(8,128)S(1)}, f32[80,512]{1,0:T(8,128)S(1)}, u32[]{:S(2)}, u32[]{:S(2)}) collective-permute-start(f32[80,512]{1,0:T(8,128)S(1)} %get-tuple-element.34), channel_id=1, source_target_pairs={{0,6},{1,3},{2,0},{3,5},{4,2},{5,7},{6,4},{7,1},{8,14},{9,11},{10,... | collective-permute-start | bytes 491528 | tf_op jit(solution)/shard_map/ppermute | solution.py:27
  96.6 3.1 %collective-permute-done.15.refs_4_ = f32[80,512]{1,0:T(8,128)S(1)} collective-permute-done((f32[80,512]{1,0:T(8,128)S(1)}, f32[80,512]{1,0:T(8,128)S(1)}, u32[]{:S(2)}, u32[]{:S(2)}) %collective-permute-start.15) | collective-permute-done | bytes 163872 | tf_op jit(solution)/shard_map/ppermute | solution.py:27
  99.7 3.4 %collective-permute-done.14.refs_3_ = f32[80,512]{1,0:T(8,128)S(1)} collective-permute-done((f32[80,512]{1,0:T(8,128)S(1)}, f32[80,512]{1,0:T(8,128)S(1)}, u32[]{:S(2)}, u32[]{:S(2)}) %collective-permute-start.14) | collective-permute-done | bytes 163872 | tf_op jit(solution)/shard_map/ppermute | solution.py:27
  103.1 1.3 %shard_map.71 = (f32[64,512]{1,0:T(8,128)S(1)}, bf16[64,128]{1,0:T(8,128)(2,1)S(1)}, f32[1,512]{1,0:T(1,128)S(1)}) custom-call(f32[1,1]{1,0:T(1,128)} %get-tuple-element.24.refs_0_, s32[1,128]{1,0:T(1,128)S(1)} %add_subtract_fusion.refs_1_.refs_0_, f32[80,512]{1,0:T(8,128)S(1)} %get-tuple-element.31.refs_2_, f32[80,512]{1,0:T(8,128)S(1)} %collective-permute-done.14.refs_3_, ...), custom_call_target="tpu_custom_call" | custom-call | tf_op jit(solution)/shard_map/pallas_call | solution.py:449
  104.5 1.3 %shard_map.79 = (f32[128,512]{1,0:T(8,128)}, bf16[128,128]{1,0:T(8,128)(2,1)S(1)}) custom-call(s32[1,128]{1,0:T(1,128)S(1)} %add_subtract_fusion.refs_1_.refs_0_, f32[1,512]{1,0:T(1,128)S(1)} %get-tuple-element.35.refs_1_, f32[64,512]{1,0:T(8,128)S(1)} %get-tuple-element.36.refs_2_, bf16[64,128]{1,0:T(8,128)(2,1)S(1)} %get-tuple-element.37.refs_3_, ...), custom_call_target="tpu_custom_call" | custom-call | tf_op jit(solution)/shard_map/pallas_call | solution.py:464
  107.0 2.6 %collective-permute-start.27 = (bf16[128,128]{1,0:T(8,128)(2,1)S(1)}, bf16[128,128]{1,0:T(8,128)(2,1)S(1)}, u32[]{:S(2)}, u32[]{:S(2)}) collective-permute-start(bf16[128,128]{1,0:T(8,128)(2,1)S(1)} %get-tuple-element.45), channel_id=1, source_target_pairs={{0,96},{1,25},{2,98},{3,27},{4,100},{5,29},{6,102},{7,31},{8,104},... | collective-permute-start | bytes 98312 | tf_op jit(solution)/shard_map/ppermute | solution.py:27
  109.6 1.9 %collective-permute-done.25 = bf16[128,128]{1,0:T(8,128)(2,1)S(1)} collective-permute-done((bf16[128,128]{1,0:T(8,128)(2,1)S(1)}, bf16[128,128]{1,0:T(8,128)(2,1)S(1)}, u32[]{:S(2)}, u32[]{:S(2)}) %collective-permute-start.25) | collective-permute-done | bytes 32800 | tf_op jit(solution)/shard_map/ppermute | solution.py:27
  112.4 2.9 %collective-permute-start.30 = (bf16[128,128]{1,0:T(8,128)(2,1)S(1)}, bf16[128,128]{1,0:T(8,128)(2,1)S(1)}, u32[]{:S(2)}, u32[]{:S(2)}) collective-permute-start(bf16[128,128]{1,0:T(8,128)(2,1)S(1)} %maximum_maximum_fusion), channel_id=1, source_target_pairs={{0,24},{1,97},{2,26},{3,99},{4,28},{5,101},{6,30},{7,103},{8,0},{9... | collective-permute-start | bytes 98312 | tf_op jit(solution)/shard_map/ppermute | solution.py:27
  115.3 2.2 %collective-permute-done.28 = bf16[128,128]{1,0:T(8,128)(2,1)S(1)} collective-permute-done((bf16[128,128]{1,0:T(8,128)(2,1)S(1)}, bf16[128,128]{1,0:T(8,128)(2,1)S(1)}, u32[]{:S(2)}, u32[]{:S(2)}) %collective-permute-start.28) | collective-permute-done | bytes 32800 | tf_op jit(solution)/shard_map/ppermute | solution.py:27
  (65 shorter events, 13.1 us)
Async XLA Ops:
  0.6 1.5 %collective-permute-start = (f32[24,128]{1,0:T(8,128)}, f32[24,128]{1,0:T(8,128)S(1)}, u32[]{:S(2)}, u32[]{:S(2)}) collective-permute-start(f32[24,128]{1,0:T(8,128)} %bitcast.2), channel_id=1, source_target_pairs={{0,1},{1,0},{2,3},{3,2},{4,5},{5,4},{6,7},{7,6},{8,9},{9,8},{10,11... | collective-permute-start | bytes 36872 | tf_op jit(solution)/shard_map/ppermute | solution.py:35
  2.8 71.8 %copy-start = (s32[3072,512]{1,0:T(8,128)S(1)}, s32[3072,512]{1,0:T(8,128)}, u32[]{:S(2)}) copy-start(s32[3072,512]{1,0:T(8,128)} %dosage_ref.1) | copy-start | bytes 18874372
  2.8 6.0 %collective-permute-start.1 = (f32[48,128]{1,0:T(8,128)S(1)}, f32[48,128]{1,0:T(8,128)S(1)}, u32[]{:S(2)}, u32[]{:S(2)}) collective-permute-start(f32[48,128]{1,0:T(8,128)S(1)} %shard_map.59.pair_ref), channel_id=1, source_target_pairs={{0,2},{1,7},{2,4},{3,1},{4,6},{5,3},{6,0},{7,5},{8,10},{9,15},{10,... | collective-permute-start | bytes 73736 | tf_op jit(solution)/shard_map/ppermute | solution.py:27
  4.8 5.5 %collective-permute-start.3 = (f32[24,128]{1,0:T(8,128)S(1)}, f32[24,128]{1,0:T(8,128)S(1)}, u32[]{:S(2)}, u32[]{:S(2)}) collective-permute-start(f32[24,128]{1,0:T(8,128)S(1)} %bitcast.4), channel_id=1, source_target_pairs={{0,4},{2,6},{4,0},{6,2},{1,5},{3,7},{5,1},{7,3},{8,12},{10,14},{12... | collective-permute-start | bytes 36872 | tf_op jit(solution)/shard_map/ppermute | solution.py:31
  8.8 3.3 %collective-permute-start.2 = (f32[48,128]{1,0:T(8,128)S(1)}, f32[48,128]{1,0:T(8,128)S(1)}, u32[]{:S(2)}, u32[]{:S(2)}) collective-permute-start(f32[48,128]{1,0:T(8,128)S(1)} %collective-permute-done.1.mine_ref), channel_id=1, source_target_pairs={{0,1},{1,0},{2,3},{3,2},{4,5},{5,4},{6,7},{7,6},{8,9},{9,8},{10,11... | collective-permute-start | bytes 73736 | tf_op jit(solution)/shard_map/ppermute | solution.py:35
  10.4 1.7 %collective-permute-start.4 = (f32[24,128]{1,0:T(8,128)S(1)}, f32[24,128]{1,0:T(8,128)S(1)}, u32[]{:S(2)}, u32[]{:S(2)}) collective-permute-start(f32[24,128]{1,0:T(8,128)S(1)} %collective-permute-done.3.far_ref), channel_id=1, source_target_pairs={{0,1},{1,0},{2,3},{3,2},{4,5},{5,4},{6,7},{7,6},{8,9},{9,8},{10,11... | collective-permute-start | bytes 36872 | tf_op jit(solution)/shard_map/ppermute | solution.py:35
  33.6 9.1 %collective-permute-start.5 = (bf16[64,3072]{1,0:T(8,128)(2,1)S(1)}, bf16[64,3072]{1,0:T(8,128)(2,1)S(1)}, u32[]{:S(2)}, u32[]{:S(2)}) collective-permute-start(bf16[64,3072]{1,0:T(8,128)(2,1)S(1)} %shard_map.62.refs_0_), channel_id=1, source_target_pairs={{0,32},{1,25},{2,34},{3,27},{4,36},{5,29},{6,38},{7,31},{8,40},{9,... | collective-permute-start | bytes 1179656 | tf_op jit(solution)/shard_map/ppermute | solution.py:27
  35.1 7.9 %collective-permute-start.6 = (bf16[64,3072]{1,0:T(8,128)(2,1)S(1)}, bf16[64,3072]{1,0:T(8,128)(2,1)S(1)}, u32[]{:S(2)}, u32[]{:S(2)}) collective-permute-start(bf16[64,3072]{1,0:T(8,128)(2,1)S(1)} %shard_map.62.refs_0_), channel_id=1, source_target_pairs={{0,96},{1,9},{2,98},{3,11},{4,100},{5,13},{6,102},{7,15},{8,104},{... | collective-permute-start | bytes 1179656 | tf_op jit(solution)/shard_map/ppermute | solution.py:27
  42.6 6.9 %collective-permute-start.7 = (bf16[32,3072]{1,0:T(8,128)(2,1)S(1)}, bf16[32,3072]{1,0:T(8,128)(2,1)S(1)}, u32[]{:S(2)}, u32[]{:S(2)}) collective-permute-start(bf16[32,3072]{1,0:T(8,128)(2,1)S(1)} %shard_map.63), channel_id=1, source_target_pairs={{0,32},{1,25},{2,34},{3,27},{4,36},{5,29},{6,38},{7,31},{8,40},{9,... | collective-permute-start | bytes 589832 | tf_op jit(solution)/shard_map/ppermute | solution.py:27
  43.0 9.7 %collective-permute-start.16 = (bf16[32,3072]{1,0:T(8,128)(2,1)S(1)}, bf16[32,3072]{1,0:T(8,128)(2,1)S(1)}, u32[]{:S(2)}, u32[]{:S(2)}) collective-permute-start(bf16[32,3072]{1,0:T(8,128)(2,1)S(1)} %shard_map.72), channel_id=1, source_target_pairs={{0,96},{1,9},{2,98},{3,11},{4,100},{5,13},{6,102},{7,15},{8,104},{... | collective-permute-start | bytes 589832 | tf_op jit(solution)/shard_map/ppermute | solution.py:27
  49.7 12.6 %collective-permute-start.8 = (bf16[4,32,3072]{2,1,0:T(8,128)(2,1)S(1)}, bf16[4,32,3072]{2,1,0:T(8,128)(2,1)S(1)}, u32[]{:S(2)}, u32[]{:S(2)}) collective-permute-start(bf16[4,32,3072]{2,1,0:T(8,128)(2,1)S(1)} %shard_map.64.a0), channel_id=1, source_target_pairs={{0,24},{1,33},{2,26},{3,35},{4,28},{5,37},{6,30},{7,39},{8,0},{9,4... | collective-permute-start | bytes 2359304 | tf_op jit(solution)/shard_map/ppermute | solution.py:27
  52.7 13.3 %collective-permute-start.9 = (bf16[4,32,3072]{2,1,0:T(8,128)(2,1)S(1)}, bf16[4,32,3072]{2,1,0:T(8,128)(2,1)S(1)}, u32[]{:S(2)}, u32[]{:S(2)}) collective-permute-start(bf16[4,32,3072]{2,1,0:T(8,128)(2,1)S(1)} %shard_map.64.a0), channel_id=1, source_target_pairs={{0,8},{1,97},{2,10},{3,99},{4,12},{5,101},{6,14},{7,103},{8,16},{9... | collective-permute-start | bytes 2359304 | tf_op jit(solution)/shard_map/ppermute | solution.py:27
  52.8 17.9 %collective-permute-start.17 = (bf16[4,32,3072]{2,1,0:T(8,128)(2,1)S(1)}, bf16[4,32,3072]{2,1,0:T(8,128)(2,1)S(1)}, u32[]{:S(2)}, u32[]{:S(2)}) collective-permute-start(bf16[4,32,3072]{2,1,0:T(8,128)(2,1)S(1)} %shard_map.73.a0), channel_id=1, source_target_pairs={{0,24},{1,33},{2,26},{3,35},{4,28},{5,37},{6,30},{7,39},{8,0},{9,4... | collective-permute-start | bytes 2359304 | tf_op jit(solution)/shard_map/ppermute | solution.py:27
  56.1 18.4 %collective-permute-start.18 = (bf16[4,32,3072]{2,1,0:T(8,128)(2,1)S(1)}, bf16[4,32,3072]{2,1,0:T(8,128)(2,1)S(1)}, u32[]{:S(2)}, u32[]{:S(2)}) collective-permute-start(bf16[4,32,3072]{2,1,0:T(8,128)(2,1)S(1)} %shard_map.73.a0), channel_id=1, source_target_pairs={{0,8},{1,97},{2,10},{3,99},{4,12},{5,101},{6,14},{7,103},{8,16},{9... | collective-permute-start | bytes 2359304 | tf_op jit(solution)/shard_map/ppermute | solution.py:27
  62.3 14.7 %collective-permute-start.10 = (bf16[2,32,3072]{2,1,0:T(8,128)(2,1)S(1)}, bf16[2,32,3072]{2,1,0:T(8,128)(2,1)S(1)}, u32[]{:S(2)}, u32[]{:S(2)}) collective-permute-start(bf16[2,32,3072]{2,1,0:T(8,128)(2,1)S(1)} %shard_map.67), channel_id=1, source_target_pairs={{0,24},{1,33},{2,26},{3,35},{4,28},{5,37},{6,30},{7,39},{8,0},{9,4... | collective-permute-start | bytes 1179656 | tf_op jit(solution)/shard_map/ppermute | solution.py:27
  66.1 12.5 %collective-permute-start.11 = (bf16[2,32,3072]{2,1,0:T(8,128)(2,1)S(1)}, bf16[2,32,3072]{2,1,0:T(8,128)(2,1)S(1)}, u32[]{:S(2)}, u32[]{:S(2)}) collective-permute-start(bf16[2,32,3072]{2,1,0:T(8,128)(2,1)S(1)} %shard_map.68), channel_id=1, source_target_pairs={{0,8},{1,97},{2,10},{3,99},{4,12},{5,101},{6,14},{7,103},{8,16},{9... | collective-permute-start | bytes 1179656 | tf_op jit(solution)/shard_map/ppermute | solution.py:27
  70.7 10.3 %collective-permute-start.19 = (bf16[2,32,3072]{2,1,0:T(8,128)(2,1)S(1)}, bf16[2,32,3072]{2,1,0:T(8,128)(2,1)S(1)}, u32[]{:S(2)}, u32[]{:S(2)}) collective-permute-start(bf16[2,32,3072]{2,1,0:T(8,128)(2,1)S(1)} %shard_map.75), channel_id=1, source_target_pairs={{0,24},{1,33},{2,26},{3,35},{4,28},{5,37},{6,30},{7,39},{8,0},{9,4... | collective-permute-start | bytes 1179656 | tf_op jit(solution)/shard_map/ppermute | solution.py:27
  74.5 9.1 %collective-permute-start.20 = (bf16[2,32,3072]{2,1,0:T(8,128)(2,1)S(1)}, bf16[2,32,3072]{2,1,0:T(8,128)(2,1)S(1)}, u32[]{:S(2)}, u32[]{:S(2)}) collective-permute-start(bf16[2,32,3072]{2,1,0:T(8,128)(2,1)S(1)} %shard_map.76), channel_id=1, source_target_pairs={{0,8},{1,97},{2,10},{3,99},{4,12},{5,101},{6,14},{7,103},{8,16},{9... | collective-permute-start | bytes 1179656 | tf_op jit(solution)/shard_map/ppermute | solution.py:27
  79.4 5.1 %collective-permute-start.12 = (f32[4,80,512]{2,1,0:T(8,128)S(1)}, f32[4,80,512]{2,1,0:T(8,128)S(1)}, u32[]{:S(2)}, u32[]{:S(2)}) collective-permute-start(f32[4,80,512]{2,1,0:T(8,128)S(1)} %get-tuple-element.30), channel_id=1, source_target_pairs={{0,1},{1,0},{2,3},{3,2},{4,5},{5,4},{6,7},{7,6},{8,9},{9,8},{10,11... | collective-permute-start | bytes 1966088 | tf_op jit(solution)/shard_map/ppermute | solution.py:35
  84.3 2.0 %collective-permute-start.21 = (f32[4,64,512]{2,1,0:T(8,128)S(1)}, f32[4,64,512]{2,1,0:T(8,128)S(1)}, u32[]{:S(2)}, u32[]{:S(2)}) collective-permute-start(f32[4,64,512]{2,1,0:T(8,128)S(1)} %get-tuple-element.39), channel_id=1, source_target_pairs={{0,1},{1,0},{2,3},{3,2},{4,5},{5,4},{6,7},{7,6},{8,9},{9,8},{10,11... | collective-permute-start | bytes 1572872 | tf_op jit(solution)/shard_map/ppermute | solution.py:35
  84.5 12.0 %collective-permute-start.13 = (f32[80,512]{1,0:T(8,128)S(1)}, f32[80,512]{1,0:T(8,128)S(1)}, u32[]{:S(2)}, u32[]{:S(2)}) collective-permute-start(f32[80,512]{1,0:T(8,128)S(1)} %get-tuple-element.33), channel_id=1, source_target_pairs={{0,2},{1,7},{2,4},{3,1},{4,6},{5,3},{6,0},{7,5},{8,10},{9,15},{10,... | collective-permute-start | bytes 491528 | tf_op jit(solution)/shard_map/ppermute | solution.py:27
  86.4 6.8 %collective-permute-start.22 = (f32[64,512]{1,0:T(8,128)S(1)}, f32[64,512]{1,0:T(8,128)S(1)}, u32[]{:S(2)}, u32[]{:S(2)}) collective-permute-start(f32[64,512]{1,0:T(8,128)S(1)} %get-tuple-element.42), channel_id=1, source_target_pairs={{0,2},{1,7},{2,4},{3,1},{4,6},{5,3},{6,0},{7,5},{8,10},{9,15},{10,... | collective-permute-start | bytes 393224 | tf_op jit(solution)/shard_map/ppermute | solution.py:27
  87.8 16.6 %collective-permute-start.24 = (f32[64,512]{1,0:T(8,128)S(1)}, f32[64,512]{1,0:T(8,128)S(1)}, u32[]{:S(2)}, u32[]{:S(2)}) collective-permute-start(f32[64,512]{1,0:T(8,128)S(1)} %get-tuple-element.43), channel_id=1, source_target_pairs={{0,6},{1,3},{2,0},{3,5},{4,2},{5,7},{6,4},{7,1},{8,14},{9,11},{10,... | collective-permute-start | bytes 393224 | tf_op jit(solution)/shard_map/ppermute | solution.py:27
  93.2 11.3 %collective-permute-start.23 = (f32[64,512]{1,0:T(8,128)S(1)}, f32[64,512]{1,0:T(8,128)S(1)}, u32[]{:S(2)}, u32[]{:S(2)}) collective-permute-start(f32[64,512]{1,0:T(8,128)S(1)} %add.19), channel_id=1, source_target_pairs={{0,2},{1,7},{2,4},{3,1},{4,6},{5,3},{6,0},{7,5},{8,10},{9,15},{10,... | collective-permute-start | bytes 393224 | tf_op jit(solution)/shard_map/ppermute | solution.py:27
  93.8 5.9 %collective-permute-start.15 = (f32[80,512]{1,0:T(8,128)S(1)}, f32[80,512]{1,0:T(8,128)S(1)}, u32[]{:S(2)}, u32[]{:S(2)}) collective-permute-start(f32[80,512]{1,0:T(8,128)S(1)} %get-tuple-element.34), channel_id=1, source_target_pairs={{0,6},{1,3},{2,0},{3,5},{4,2},{5,7},{6,4},{7,1},{8,14},{9,11},{10,... | collective-permute-start | bytes 491528 | tf_op jit(solution)/shard_map/ppermute | solution.py:27
  96.5 6.6 %collective-permute-start.14 = (f32[80,512]{1,0:T(8,128)S(1)}, f32[80,512]{1,0:T(8,128)S(1)}, u32[]{:S(2)}, u32[]{:S(2)}) collective-permute-start(f32[80,512]{1,0:T(8,128)S(1)} %add.18), channel_id=1, source_target_pairs={{0,2},{1,7},{2,4},{3,1},{4,6},{5,3},{6,0},{7,5},{8,10},{9,15},{10,... | collective-permute-start | bytes 491528 | tf_op jit(solution)/shard_map/ppermute | solution.py:27
  105.8 5.7 %collective-permute-start.25 = (bf16[128,128]{1,0:T(8,128)(2,1)S(1)}, bf16[128,128]{1,0:T(8,128)(2,1)S(1)}, u32[]{:S(2)}, u32[]{:S(2)}) collective-permute-start(bf16[128,128]{1,0:T(8,128)(2,1)S(1)} %get-tuple-element.45), channel_id=1, source_target_pairs={{0,64},{1,17},{2,66},{3,19},{4,68},{5,21},{6,70},{7,23},{8,72},{9,... | collective-permute-start | bytes 98312 | tf_op jit(solution)/shard_map/ppermute | solution.py:27
  106.4 5.5 %collective-permute-start.26 = (bf16[128,128]{1,0:T(8,128)(2,1)S(1)}, bf16[128,128]{1,0:T(8,128)(2,1)S(1)}, u32[]{:S(2)}, u32[]{:S(2)}) collective-permute-start(bf16[128,128]{1,0:T(8,128)(2,1)S(1)} %get-tuple-element.45), channel_id=1, source_target_pairs={{0,32},{1,9},{2,34},{3,11},{4,36},{5,13},{6,38},{7,15},{8,40},{9,1... | collective-permute-start | bytes 98312 | tf_op jit(solution)/shard_map/ppermute | solution.py:27
  107.0 4.9 %collective-permute-start.27 = (bf16[128,128]{1,0:T(8,128)(2,1)S(1)}, bf16[128,128]{1,0:T(8,128)(2,1)S(1)}, u32[]{:S(2)}, u32[]{:S(2)}) collective-permute-start(bf16[128,128]{1,0:T(8,128)(2,1)S(1)} %get-tuple-element.45), channel_id=1, source_target_pairs={{0,96},{1,25},{2,98},{3,27},{4,100},{5,29},{6,102},{7,31},{8,104},... | collective-permute-start | bytes 98312 | tf_op jit(solution)/shard_map/ppermute | solution.py:27
  111.9 5.6 %collective-permute-start.28 = (bf16[128,128]{1,0:T(8,128)(2,1)S(1)}, bf16[128,128]{1,0:T(8,128)(2,1)S(1)}, u32[]{:S(2)}, u32[]{:S(2)}) collective-permute-start(bf16[128,128]{1,0:T(8,128)(2,1)S(1)} %maximum_maximum_fusion), channel_id=1, source_target_pairs={{0,16},{1,65},{2,18},{3,67},{4,20},{5,69},{6,22},{7,71},{8,24},{9,... | collective-permute-start | bytes 98312 | tf_op jit(solution)/shard_map/ppermute | solution.py:27
  112.0 5.5 %collective-permute-start.29 = (bf16[128,128]{1,0:T(8,128)(2,1)S(1)}, bf16[128,128]{1,0:T(8,128)(2,1)S(1)}, u32[]{:S(2)}, u32[]{:S(2)}) collective-permute-start(bf16[128,128]{1,0:T(8,128)(2,1)S(1)} %maximum_maximum_fusion), channel_id=1, source_target_pairs={{0,8},{1,33},{2,10},{3,35},{4,12},{5,37},{6,14},{7,39},{8,16},{9,4... | collective-permute-start | bytes 98312 | tf_op jit(solution)/shard_map/ppermute | solution.py:27
  112.4 5.1 %collective-permute-start.30 = (bf16[128,128]{1,0:T(8,128)(2,1)S(1)}, bf16[128,128]{1,0:T(8,128)(2,1)S(1)}, u32[]{:S(2)}, u32[]{:S(2)}) collective-permute-start(bf16[128,128]{1,0:T(8,128)(2,1)S(1)} %maximum_maximum_fusion), channel_id=1, source_target_pairs={{0,24},{1,97},{2,26},{3,99},{4,28},{5,101},{6,30},{7,103},{8,0},{9... | collective-permute-start | bytes 98312 | tf_op jit(solution)/shard_map/ppermute | solution.py:27
  (3 other events, 10.0 us)

commit v2 on v1

--- a/solution.py
+++ b/solution.py
@@ -11,7 +11,7 @@
 AXES = ("x", "y", "z", "c")
 CHUNKS = 2
 LOW = 128
-AT_ONCE = 24
+COLUMNS = 3
 PLACES = [
     (x, y, z, c) for x in range(RING) for y in range(RING) for z in range(RING) for c in range(2)
 ]
@@ -77,7 +77,7 @@
 
 
 def table_kernel(pair_ref, mine_ref, theirs_ref, far_ref, other_ref, *rest):
-    table_ref, scale_ref, var_ref, code_ref = rest
+    table_ref, scale_ref, var_ref, plain_ref, code_ref, value_ref = rest
     z, c = lax.axis_index("z"), lax.axis_index("c")
     step = 1 - 2 * c
     depth = far_ref.shape[0]
@@ -104,9 +104,12 @@
     for r, (_, at_z, core) in zip(rounded, blocks):
         code = jnp.round(jnp.sqrt(jnp.sqrt(jnp.abs(r) / most)) * 32767.0).astype(jnp.int32)
         code = jnp.where(r < 0, -code, code)
-        start = (((at_z + RING) % RING) * 2 + core) * depth
-        code_ref[pl.ds(pl.multiple_of(start, 8), depth), :] = code
+        start = pl.multiple_of((((at_z + RING) % RING) * 2 + core) * depth, 8)
+        code_ref[pl.ds(start, depth), :] = code
+        value_ref[pl.ds(start, depth), :] = r
     half = table_ref.shape[0]
+    plain_ref[:, :LOW] = value_ref[:half, :].astype(jnp.bfloat16)
+    plain_ref[:, LOW:] = value_ref[half:, :].astype(jnp.bfloat16)
     table_ref[...] = lax.shift_left(code_ref[half:, :], 16) + (code_ref[:half, :] & 0xFFFF)
     scale_ref[...] = jnp.sqrt(jnp.sqrt(most)) / 32767.0
 
@@ -128,10 +131,11 @@
             out_of((rows // 2, LOW), jnp.int32),
             out_of((1, LOW), jnp.float32),
             out_of((1, 1), jnp.float32),
+            out_of((rows // 2, 2 * LOW), jnp.bfloat16),
         ),
         in_specs=[VMEM] * 5,
-        out_specs=(VMEM, VMEM, SMEM),
-        scratch_shapes=[pltpu.VMEM((rows, LOW), jnp.int32)],
+        out_specs=(VMEM, VMEM, SMEM, VMEM),
+        scratch_shapes=[pltpu.VMEM((rows, LOW), jnp.int32), pltpu.VMEM((rows, LOW), jnp.float32)],
         compiler_params=room(2),
     )(pair, mine, theirs, far, far_other)
 
@@ -165,62 +169,118 @@
     )(a)
 
 
-def lookup_kernel(index_ref, table_ref, scale_ref, *rest):
-    out_ref = rest[-1]
+def places_of(index, half):
+    row = lax.shift_right_logical(index, 7)
+    upper = row >= half
+    return index & (LOW - 1), jnp.where(upper, row - half, row), upper
+
+
+def by_gathers(index, table_ref, scale):
+    half = table_ref.shape[0]
+    lane, row, upper = places_of(index, half)
+    word = jnp.zeros((8, LOW), jnp.int32)
+    for r in range(half):
+        source = jnp.broadcast_to(table_ref[r : r + 1, :], (8, LOW))
+        taken = jnp.take_along_axis(source, lane, axis=1, mode="promise_in_bounds")
+        word = jnp.where(row == r, taken, word)
+        yield None
+    code = lax.shift_right_arithmetic(jnp.where(upper, word, lax.shift_left(word, 16)), 16)
+    root = code.astype(jnp.float32) * scale
+    root = root * root
+    root = root * root
+    yield jnp.where(code < 0, -root, root)
+
+
+def by_products(index, plain_ref, lane_ref, row_ref):
+    half = plain_ref.shape[0]
+    lane, row, upper = places_of(index, half)
+    lane_ref[...] = jnp.where(upper, lane + LOW, lane).astype(jnp.float32)
+    row_ref[...] = row
+    one = jnp.ones((16, LOW), jnp.bfloat16)
+    zero = jnp.zeros((16, LOW), jnp.bfloat16)
+    along_16 = lax.broadcasted_iota(jnp.int32, (16, LOW), 0).astype(jnp.float32)
+    along_16 = along_16.astype(jnp.bfloat16)
+    along_8 = lax.broadcasted_iota(jnp.int32, (8, LOW), 0)
+    found = []
+    for i in range(0, 8, 2):
+        columns = []
+        for j in (i, i + 1):
+            want = jnp.broadcast_to(lane_ref[j : j + 1, :], (16, LOW)).astype(jnp.bfloat16)
+            hot = [
+                jnp.where(want == along_16 + jnp.bfloat16(16 * k), one, zero)
+                for k in range(2 * LOW // 16)
+            ]
+            columns.append(jnp.concatenate(hot, axis=0))
+        picked = jnp.dot(
+            plain_ref[...], jnp.concatenate(columns, axis=1), preferred_element_type=jnp.float32
+        )
+        for part, j in enumerate((i, i + 1)):
+            want = jnp.broadcast_to(row_ref[j : j + 1, :], (8, LOW))
+            value = jnp.zeros((8, LOW), jnp.float32)
+            for q in range(half // 8):
+                here = picked[8 * q : 8 * q + 8, part * LOW : (part + 1) * LOW]
+                value = jnp.where(want == along_8 + 8 * q, here, value)
+            found.append(jnp.sum(value, axis=0, keepdims=True))
+        yield None
+    yield jnp.concatenate(found, axis=0)
+
+
+def lookup_kernel(index_ref, table_ref, scale_ref, plain_ref, out_ref, found_ref, lane_ref, row_ref):
     rows, width = index_ref.shape
-    first = out_ref.shape[0] - rows
-    if first:
-        out_ref[:first, :] = rest[0][...]
-    half = table_ref.shape[0]
-    parts = AT_ONCE // (rows // 8)
-    span = parts * LOW
+    groups = rows // 8
     scale = jnp.broadcast_to(scale_ref[...], (8, LOW))
-
-    def step(j, _):
-        for part in range(parts):
-            base = pl.multiple_of(j * span + part * LOW, LOW)
-            found = []
-            for i in range(0, rows, 8):
-                index = index_ref[pl.ds(i, 8), pl.ds(base, LOW)]
-                lane = index & (LOW - 1)
-                row = lax.shift_right_logical(index, 7)
-                upper = row >= half
-                row = jnp.where(upper, row - half, row)
-                word = jnp.zeros((8, LOW), jnp.int32)
-                for r in range(half):
-                    source = jnp.broadcast_to(table_ref[r : r + 1, :], (8, LOW))
-                    taken = jnp.take_along_axis(source, lane, axis=1, mode="promise_in_bounds")
-                    word = jnp.where(row == r, taken, word)
-                code = lax.shift_right_arithmetic(
-                    jnp.where(upper, word, lax.shift_left(word, 16)), 16
-                )
-                root = code.astype(jnp.float32) * scale
-                root = root * root
-                root = root * root
-                found.append(jnp.where(code < 0, -root, root))
-            out_ref[first:, pl.ds(base, LOW)] = jnp.concatenate(found, axis=0).astype(jnp.bfloat16)
+    units = COLUMNS * groups
+    dotted = units // 2
+
+    def step(t, _):
+        base = pl.multiple_of(t * COLUMNS * LOW, LOW)
+
+        def work(unit):
+            column, i = unit // groups, unit % groups * 8
+            index = index_ref[i : i + 8, pl.ds(base + column * LOW, LOW)]
+            if unit < dotted:
+                steps = by_products(index, plain_ref, lane_ref.at[unit], row_ref.at[unit])
+            else:
+                steps = by_gathers(index, table_ref, scale)
+            for value in steps:
+                if value is not None:
+                    found_ref[i : i + 8, column * LOW : (column + 1) * LOW] = value
+                yield
+
+        products = [work(u) for u in range(dotted)]
+        gathers = [work(u) for u in range(dotted, units)]
+        first = (None for g in products for _ in g)
+        second = (None for g in gathers for _ in g)
+        fine = table_ref.shape[0] + 1
+        for k in range((units - dotted) * fine):
+            next(second, None)
+            if k % (fine // 5) == 0:
+                next(first, None)
+        for _ in first:
+            pass
+        for _ in second:
+            pass
+        out_ref[:, pl.ds(base, COLUMNS * LOW)] = found_ref[...].astype(jnp.bfloat16)
         return 0
 
-    lax.fori_loop(0, width // span, step, 0)
-
-
-def lookup(index, k, rows, table, scale, before=()):
-    width = index.shape[1]
-    shape = (rows + sum(b.shape[0] for b in before), width)
-    whole = lambda i: (0, 0)
+    lax.fori_loop(0, width // (COLUMNS * LOW), step, 0)
+
+
+def lookup(index, table, scale, plain):
+    groups = index.shape[0] // 8
+    slots = (COLUMNS * groups // 2, 8, LOW)
     return pl.pallas_call(
         lookup_kernel,
-        grid=(1,),
-        out_shape=out_of(shape, jnp.bfloat16),
-        in_specs=[
-            pl.BlockSpec((rows, width), lambda i: (k, 0)),
-            pl.BlockSpec(table.shape, whole),
-            pl.BlockSpec(scale.shape, whole),
-        ]
-        + [pl.BlockSpec(b.shape, whole) for b in before],
-        out_specs=pl.BlockSpec(shape, whole),
-        compiler_params=room(3),
-    )(index, table, scale, *before)
+        out_shape=out_of(index.shape, jnp.bfloat16),
+        in_specs=[VMEM] * 4,
+        out_specs=VMEM,
+        scratch_shapes=[
+            pltpu.VMEM((index.shape[0], COLUMNS * LOW), jnp.float32),
+            pltpu.VMEM(slots, jnp.float32),
+            pltpu.VMEM(slots, jnp.int32),
+        ],
+        compiler_params=room(6),
+    )(index, table, scale, plain)
 
 
 def ring_gather(value, first, turn, dim):
@@ -489,11 +549,11 @@
     x, y = lax.axis_index("x"), lax.axis_index("y")
     perm_index = fetched(perm_index)
     dosage_bf, totals = convert_dosage(dosage)
-    table, scale, pheno_var = make_table(phenotype.reshape(-1, LOW))
+    table, scale, pheno_var, plain = make_table(phenotype.reshape(-1, LOW))
     ends = (jnp.cumsum(seg_lengths) - 1 - (x * RING + y) * width)[None, :].astype(jnp.int32)
     count = float(samples * lax.axis_size("z") * lax.axis_size("c"))
 
-    traits = lookup(perm_index, 0, perm_index.shape[0], table, scale)
+    traits = lookup(perm_index, table, scale, plain)
     near = ring_gather(traits, True, 0, 0)
     far = [ring_gather(stacked(near, k), False, 1, 0) for k in range(CHUNKS)]
     parts = reduced(far[0], dosage_bf, totals, True)

time: 119 us -> 114 us (0.958)
  Pallas kernels: 29.8 us -> 24.9 us
    pallas_call x1, Pallas kernels: 20.7 us -> 15.8 us  [lookup(): pl.pallas_call(lookup_kernel, out_shape=out_of(index.shape, jnp.bfloat16)...]
where the time goes in v2:
time: 114 us; the launch traced here: 113 us
  starting transfers between devices  42.4 us (37%)
  waiting for transfers between devices  42.4 us (37%)
  Pallas kernels  24.9 us (22%)
  local copies, waits for them, and re-layouts  1.85 us (2%)
    ppermute x25, waiting for transfers between devices, shift(): lax.ppermute(value, AXES, [(at(*d), at(*target(*d))) for d in PLACES])  38.7 us
    ppermute x25, starting transfers between devices, shift(): lax.ppermute(value, AXES, [(at(*d), at(*target(*d))) for d in PLACES])  37.8 us
    pallas_call x1, Pallas kernels, lookup(): pl.pallas_call(lookup_kernel, out_shape=out_of(index.shape, jnp.bfloat16)...  15.8 us
    ppermute x1, starting transfers between devices, along(): lax.ppermute(value, axis, [(i, (i + step) % RING) for i in range(RING)])  3.58 us
    pallas_call x2, Pallas kernels, early_product(): pl.pallas_call(early_kernel, out_shape=out_of((rows, dosage.shape[1]), jn...  2.75 us
  transfers between devices with their start and end apart: 31, of which 16 were waited for; matrix products, arithmetic and copies ran while one was open for 0% of the time, Pallas kernels for 6%

profile of v2, /device:TPU:0, one launch (start us, length us, event | category | flops | bytes accessed | tf_op | source)
XLA Modules:
  0.0 113.5 jit_solution(14577579787900125210)
XLA Ops:
  0.7 1.4 %collective-permute-done.b_ref = f32[24,128]{1,0:T(8,128)S(1)} collective-permute-done((f32[24,128]{1,0:T(8,128)}, f32[24,128]{1,0:T(8,128)S(1)}, u32[]{:S(2)}, u32[]{:S(2)}) %collective-permute-start) | collective-permute-done | bytes 12320 | tf_op jit(solution)/shard_map/ppermute | solution.py:35
  2.8 2.0 %collective-permute-start.1 = (f32[48,128]{1,0:T(8,128)S(1)}, f32[48,128]{1,0:T(8,128)S(1)}, u32[]{:S(2)}, u32[]{:S(2)}) collective-permute-start(f32[48,128]{1,0:T(8,128)S(1)} %shard_map.59.pair_ref), channel_id=1, source_target_pairs={{0,2},{1,7},{2,4},{3,1},{4,6},{5,3},{6,0},{7,5},{8,10},{9,15},{10,... | collective-permute-start | bytes 73736 | tf_op jit(solution)/shard_map/ppermute | solution.py:27
  4.8 3.6 %collective-permute-start.3 = (f32[24,128]{1,0:T(8,128)S(1)}, f32[24,128]{1,0:T(8,128)S(1)}, u32[]{:S(2)}, u32[]{:S(2)}) collective-permute-start(f32[24,128]{1,0:T(8,128)S(1)} %bitcast.4), channel_id=1, source_target_pairs={{0,4},{2,6},{4,0},{6,2},{1,5},{3,7},{5,1},{7,3},{8,12},{10,14},{12... | collective-permute-start | bytes 36872 | tf_op jit(solution)/shard_map/ppermute | solution.py:31
  8.8 1.6 %collective-permute-done.3.far_ref = f32[24,128]{1,0:T(8,128)S(1)} collective-permute-done((f32[24,128]{1,0:T(8,128)S(1)}, f32[24,128]{1,0:T(8,128)S(1)}, u32[]{:S(2)}, u32[]{:S(2)}) %collective-permute-start.3) | collective-permute-done | bytes 12320 | tf_op jit(solution)/shard_map/ppermute | solution.py:31
  10.9 1.1 copy-done.1
  12.9 15.8 %shard_map.62.refs_0_ = bf16[64,3072]{1,0:T(8,128)(2,1)S(1)} custom-call(s32[64,3072]{1,0:T(8,128)S(1)} %shard_map.61.index_ref, s32[96,128]{1,0:T(8,128)S(1)} %get-tuple-element.26.table_ref, f32[1,128]{1,0:T(1,128)S(1)} %get-tuple-element.27.scale_ref, bf16[96,256]{1,0:T(8,128)(2,1)S(1)} %get-tuple-element.28.plain_ref), custom_call_target="tpu_custom_call" | custom-call | tf_op jit(solution)/shard_map/pallas_call | solution.py:272
  28.7 1.6 %collective-permute-start.5 = (bf16[64,3072]{1,0:T(8,128)(2,1)S(1)}, bf16[64,3072]{1,0:T(8,128)(2,1)S(1)}, u32[]{:S(2)}, u32[]{:S(2)}) collective-permute-start(bf16[64,3072]{1,0:T(8,128)(2,1)S(1)} %shard_map.62.refs_0_), channel_id=1, source_target_pairs={{0,32},{1,25},{2,34},{3,27},{4,36},{5,29},{6,38},{7,31},{8,40},{9,... | collective-permute-start | bytes 1179656 | tf_op jit(solution)/shard_map/ppermute | solution.py:27
  30.2 1.7 %collective-permute-start.6 = (bf16[64,3072]{1,0:T(8,128)(2,1)S(1)}, bf16[64,3072]{1,0:T(8,128)(2,1)S(1)}, u32[]{:S(2)}, u32[]{:S(2)}) collective-permute-start(bf16[64,3072]{1,0:T(8,128)(2,1)S(1)} %shard_map.62.refs_0_), channel_id=1, source_target_pairs={{0,96},{1,9},{2,98},{3,11},{4,100},{5,13},{6,102},{7,15},{8,104},{... | collective-permute-start | bytes 1179656 | tf_op jit(solution)/shard_map/ppermute | solution.py:27
  32.0 5.8 %collective-permute-done.5.refs_0_.refs_1_ = bf16[64,3072]{1,0:T(8,128)(2,1)S(1)} collective-permute-done((bf16[64,3072]{1,0:T(8,128)(2,1)S(1)}, bf16[64,3072]{1,0:T(8,128)(2,1)S(1)}, u32[]{:S(2)}, u32[]{:S(2)}) %collective-permute-start.5) | collective-permute-done | bytes 393248 | tf_op jit(solution)/shard_map/ppermute | solution.py:27
  38.1 3.0 %collective-permute-start.16 = (bf16[32,3072]{1,0:T(8,128)(2,1)S(1)}, bf16[32,3072]{1,0:T(8,128)(2,1)S(1)}, u32[]{:S(2)}, u32[]{:S(2)}) collective-permute-start(bf16[32,3072]{1,0:T(8,128)(2,1)S(1)} %shard_map.72), channel_id=1, source_target_pairs={{0,96},{1,9},{2,98},{3,11},{4,100},{5,13},{6,102},{7,15},{8,104},{... | collective-permute-start | bytes 589832 | tf_op jit(solution)/shard_map/ppermute | solution.py:27
  41.2 3.6 %collective-permute-done.7.refs_3_ = bf16[32,3072]{1,0:T(8,128)(2,1)S(1)} collective-permute-done((bf16[32,3072]{1,0:T(8,128)(2,1)S(1)}, bf16[32,3072]{1,0:T(8,128)(2,1)S(1)}, u32[]{:S(2)}, u32[]{:S(2)}) %collective-permute-start.7) | collective-permute-done | bytes 196640 | tf_op jit(solution)/shard_map/ppermute | solution.py:27
  44.8 3.1 %collective-permute-start.8 = (bf16[4,32,3072]{2,1,0:T(8,128)(2,1)S(1)}, bf16[4,32,3072]{2,1,0:T(8,128)(2,1)S(1)}, u32[]{:S(2)}, u32[]{:S(2)}) collective-permute-start(bf16[4,32,3072]{2,1,0:T(8,128)(2,1)S(1)} %shard_map.64.a0), channel_id=1, source_target_pairs={{0,24},{1,33},{2,26},{3,35},{4,28},{5,37},{6,30},{7,39},{8,0},{9,4... | collective-permute-start | bytes 2359304 | tf_op jit(solution)/shard_map/ppermute | solution.py:27
  47.9 3.3 %collective-permute-start.17 = (bf16[4,32,3072]{2,1,0:T(8,128)(2,1)S(1)}, bf16[4,32,3072]{2,1,0:T(8,128)(2,1)S(1)}, u32[]{:S(2)}, u32[]{:S(2)}) collective-permute-start(bf16[4,32,3072]{2,1,0:T(8,128)(2,1)S(1)} %shard_map.73.a0), channel_id=1, source_target_pairs={{0,24},{1,33},{2,26},{3,35},{4,28},{5,37},{6,30},{7,39},{8,0},{9,4... | collective-permute-start | bytes 2359304 | tf_op jit(solution)/shard_map/ppermute | solution.py:27
  51.2 6.1 %collective-permute-done.8.a1.refs_0_ = bf16[4,32,3072]{2,1,0:T(8,128)(2,1)S(1)} collective-permute-done((bf16[4,32,3072]{2,1,0:T(8,128)(2,1)S(1)}, bf16[4,32,3072]{2,1,0:T(8,128)(2,1)S(1)}, u32[]{:S(2)}, u32[]{:S(2)}) %collective-permute-start.8) | collective-permute-done | bytes 786464 | tf_op jit(solution)/shard_map/ppermute | solution.py:27
  57.4 3.8 %collective-permute-start.10 = (bf16[2,32,3072]{2,1,0:T(8,128)(2,1)S(1)}, bf16[2,32,3072]{2,1,0:T(8,128)(2,1)S(1)}, u32[]{:S(2)}, u32[]{:S(2)}) collective-permute-start(bf16[2,32,3072]{2,1,0:T(8,128)(2,1)S(1)} %shard_map.67), channel_id=1, source_target_pairs={{0,24},{1,33},{2,26},{3,35},{4,28},{5,37},{6,30},{7,39},{8,0},{9,4... | collective-permute-start | bytes 1179656 | tf_op jit(solution)/shard_map/ppermute | solution.py:27
  61.3 4.5 %collective-permute-done.17.a1.refs_0_ = bf16[4,32,3072]{2,1,0:T(8,128)(2,1)S(1)} collective-permute-done((bf16[4,32,3072]{2,1,0:T(8,128)(2,1)S(1)}, bf16[4,32,3072]{2,1,0:T(8,128)(2,1)S(1)}, u32[]{:S(2)}, u32[]{:S(2)}) %collective-permute-start.17) | collective-permute-done | bytes 786464 | tf_op jit(solution)/shard_map/ppermute | solution.py:27
  65.8 3.8 %collective-permute-start.19 = (bf16[2,32,3072]{2,1,0:T(8,128)(2,1)S(1)}, bf16[2,32,3072]{2,1,0:T(8,128)(2,1)S(1)}, u32[]{:S(2)}, u32[]{:S(2)}) collective-permute-start(bf16[2,32,3072]{2,1,0:T(8,128)(2,1)S(1)} %shard_map.75), channel_id=1, source_target_pairs={{0,24},{1,33},{2,26},{3,35},{4,28},{5,37},{6,30},{7,39},{8,0},{9,4... | collective-permute-start | bytes 1179656 | tf_op jit(solution)/shard_map/ppermute | solution.py:27
  70.7 1.4 %shard_map.66.refs_0_ = f32[384,512]{1,0:T(8,128)S(1)} custom-call(bf16[4,32,3072]{2,1,0:T(8,128)(2,1)S(1)} %shard_map.64.a0, bf16[4,32,3072]{2,1,0:T(8,128)(2,1)S(1)} %collective-permute-done.8.a1.refs_0_, bf16[4,32,3072]{2,1,0:T(8,128)(2,1)S(1)} %collective-permute-done.9.a2.refs_0_, bf16[3072,512]{1,0:T(8,128)(2,1)S(1)} %get-tuple-element.29.dosage_ref.refs_3_), custom_call_target="tpu_custom_call" | custom-call | tf_op jit(solution)/shard_map/pallas_call | solution.py:354
  72.1 1.6 %collective-permute-done.11.refs_2_ = bf16[2,32,3072]{2,1,0:T(8,128)(2,1)S(1)} collective-permute-done((bf16[2,32,3072]{2,1,0:T(8,128)(2,1)S(1)}, bf16[2,32,3072]{2,1,0:T(8,128)(2,1)S(1)}, u32[]{:S(2)}, u32[]{:S(2)}) %collective-permute-start.11) | collective-permute-done | bytes 393248 | tf_op jit(solution)/shard_map/ppermute | solution.py:27
  74.6 1.4 %shard_map.74.refs_0_ = f32[384,512]{1,0:T(8,128)S(1)} custom-call(bf16[4,32,3072]{2,1,0:T(8,128)(2,1)S(1)} %shard_map.73.a0, bf16[4,32,3072]{2,1,0:T(8,128)(2,1)S(1)} %collective-permute-done.17.a1.refs_0_, bf16[4,32,3072]{2,1,0:T(8,128)(2,1)S(1)} %collective-permute-done.18.a2.refs_0_, bf16[3072,512]{1,0:T(8,128)(2,1)S(1)} %get-tuple-element.29.dosage_ref.refs_3_), custom_call_target="tpu_custom_call" | custom-call | tf_op jit(solution)/shard_map/pallas_call | solution.py:354
  76.0 2.7 %collective-permute-done.20.refs_2_ = bf16[2,32,3072]{2,1,0:T(8,128)(2,1)S(1)} collective-permute-done((bf16[2,32,3072]{2,1,0:T(8,128)(2,1)S(1)}, bf16[2,32,3072]{2,1,0:T(8,128)(2,1)S(1)}, u32[]{:S(2)}, u32[]{:S(2)}) %collective-permute-start.20) | collective-permute-done | bytes 393248 | tf_op jit(solution)/shard_map/ppermute | solution.py:27
  83.1 2.2 %collective-permute-start.24 = (f32[64,512]{1,0:T(8,128)S(1)}, f32[64,512]{1,0:T(8,128)S(1)}, u32[]{:S(2)}, u32[]{:S(2)}) collective-permute-start(f32[64,512]{1,0:T(8,128)S(1)} %get-tuple-element.45), channel_id=1, source_target_pairs={{0,6},{1,3},{2,0},{3,5},{4,2},{5,7},{6,4},{7,1},{8,14},{9,11},{10,... | collective-permute-start | bytes 393224 | tf_op jit(solution)/shard_map/ppermute | solution.py:27
  85.3 3.2 %collective-permute-done.22 = f32[64,512]{1,0:T(8,128)S(1)} collective-permute-done((f32[64,512]{1,0:T(8,128)S(1)}, f32[64,512]{1,0:T(8,128)S(1)}, u32[]{:S(2)}, u32[]{:S(2)}) %collective-permute-start.22) | collective-permute-done | bytes 131104 | tf_op jit(solution)/shard_map/ppermute | solution.py:27
  89.1 2.7 %collective-permute-start.15 = (f32[80,512]{1,0:T(8,128)S(1)}, f32[80,512]{1,0:T(8,128)S(1)}, u32[]{:S(2)}, u32[]{:S(2)}) collective-permute-start(f32[80,512]{1,0:T(8,128)S(1)} %get-tuple-element.36), channel_id=1, source_target_pairs={{0,6},{1,3},{2,0},{3,5},{4,2},{5,7},{6,4},{7,1},{8,14},{9,11},{10,... | collective-permute-start | bytes 491528 | tf_op jit(solution)/shard_map/ppermute | solution.py:27
  92.0 3.1 %collective-permute-done.15.refs_4_ = f32[80,512]{1,0:T(8,128)S(1)} collective-permute-done((f32[80,512]{1,0:T(8,128)S(1)}, f32[80,512]{1,0:T(8,128)S(1)}, u32[]{:S(2)}, u32[]{:S(2)}) %collective-permute-start.15) | collective-permute-done | bytes 163872 | tf_op jit(solution)/shard_map/ppermute | solution.py:27
  95.0 3.4 %collective-permute-done.14.refs_3_ = f32[80,512]{1,0:T(8,128)S(1)} collective-permute-done((f32[80,512]{1,0:T(8,128)S(1)}, f32[80,512]{1,0:T(8,128)S(1)}, u32[]{:S(2)}, u32[]{:S(2)}) %collective-permute-start.14) | collective-permute-done | bytes 163872 | tf_op jit(solution)/shard_map/ppermute | solution.py:27
  98.5 1.3 %shard_map.71 = (f32[64,512]{1,0:T(8,128)S(1)}, bf16[64,128]{1,0:T(8,128)(2,1)S(1)}, f32[1,512]{1,0:T(1,128)S(1)}) custom-call(f32[1,1]{1,0:T(1,128)} %get-tuple-element.25.refs_0_, s32[1,128]{1,0:T(1,128)S(1)} %add_subtract_fusion.refs_1_.refs_0_, f32[80,512]{1,0:T(8,128)S(1)} %get-tuple-element.33.refs_2_, f32[80,512]{1,0:T(8,128)S(1)} %collective-permute-done.14.refs_3_, ...), custom_call_target="tpu_custom_call" | custom-call | tf_op jit(solution)/shard_map/pallas_call | solution.py:509
  99.8 1.3 %shard_map.79 = (f32[128,512]{1,0:T(8,128)}, bf16[128,128]{1,0:T(8,128)(2,1)S(1)}) custom-call(s32[1,128]{1,0:T(1,128)S(1)} %add_subtract_fusion.refs_1_.refs_0_, f32[1,512]{1,0:T(1,128)S(1)} %get-tuple-element.37.refs_1_, f32[64,512]{1,0:T(8,128)S(1)} %get-tuple-element.38.refs_2_, bf16[64,128]{1,0:T(8,128)(2,1)S(1)} %get-tuple-element.39.refs_3_, ...), custom_call_target="tpu_custom_call" | custom-call | tf_op jit(solution)/shard_map/pallas_call | solution.py:524
  102.3 2.6 %collective-permute-start.27 = (bf16[128,128]{1,0:T(8,128)(2,1)S(1)}, bf16[128,128]{1,0:T(8,128)(2,1)S(1)}, u32[]{:S(2)}, u32[]{:S(2)}) collective-permute-start(bf16[128,128]{1,0:T(8,128)(2,1)S(1)} %get-tuple-element.47), channel_id=1, source_target_pairs={{0,96},{1,25},{2,98},{3,27},{4,100},{5,29},{6,102},{7,31},{8,104},... | collective-permute-start | bytes 98312 | tf_op jit(solution)/shard_map/ppermute | solution.py:27
  104.9 1.9 %collective-permute-done.25 = bf16[128,128]{1,0:T(8,128)(2,1)S(1)} collective-permute-done((bf16[128,128]{1,0:T(8,128)(2,1)S(1)}, bf16[128,128]{1,0:T(8,128)(2,1)S(1)}, u32[]{:S(2)}, u32[]{:S(2)}) %collective-permute-start.25) | collective-permute-done | bytes 32800 | tf_op jit(solution)/shard_map/ppermute | solution.py:27
  107.7 2.9 %collective-permute-start.30 = (bf16[128,128]{1,0:T(8,128)(2,1)S(1)}, bf16[128,128]{1,0:T(8,128)(2,1)S(1)}, u32[]{:S(2)}, u32[]{:S(2)}) collective-permute-start(bf16[128,128]{1,0:T(8,128)(2,1)S(1)} %maximum_maximum_fusion), channel_id=1, source_target_pairs={{0,24},{1,97},{2,26},{3,99},{4,28},{5,101},{6,30},{7,103},{8,0},{9... | collective-permute-start | bytes 98312 | tf_op jit(solution)/shard_map/ppermute | solution.py:27
  110.6 2.2 %collective-permute-done.28 = bf16[128,128]{1,0:T(8,128)(2,1)S(1)} collective-permute-done((bf16[128,128]{1,0:T(8,128)(2,1)S(1)}, bf16[128,128]{1,0:T(8,128)(2,1)S(1)}, u32[]{:S(2)}, u32[]{:S(2)}) %collective-permute-start.28) | collective-permute-done | bytes 32800 | tf_op jit(solution)/shard_map/ppermute | solution.py:27
  (65 shorter events, 13.1 us)
Async XLA Ops:
  0.6 1.5 %collective-permute-start = (f32[24,128]{1,0:T(8,128)}, f32[24,128]{1,0:T(8,128)S(1)}, u32[]{:S(2)}, u32[]{:S(2)}) collective-permute-start(f32[24,128]{1,0:T(8,128)} %bitcast.2), channel_id=1, source_target_pairs={{0,1},{1,0},{2,3},{3,2},{4,5},{5,4},{6,7},{7,6},{8,9},{9,8},{10,11... | collective-permute-start | bytes 36872 | tf_op jit(solution)/shard_map/ppermute | solution.py:35
  2.8 66.9 %copy-start = (s32[3072,512]{1,0:T(8,128)S(1)}, s32[3072,512]{1,0:T(8,128)}, u32[]{:S(2)}) copy-start(s32[3072,512]{1,0:T(8,128)} %dosage_ref.1) | copy-start | bytes 18874372
  2.8 6.0 %collective-permute-start.1 = (f32[48,128]{1,0:T(8,128)S(1)}, f32[48,128]{1,0:T(8,128)S(1)}, u32[]{:S(2)}, u32[]{:S(2)}) collective-permute-start(f32[48,128]{1,0:T(8,128)S(1)} %shard_map.59.pair_ref), channel_id=1, source_target_pairs={{0,2},{1,7},{2,4},{3,1},{4,6},{5,3},{6,0},{7,5},{8,10},{9,15},{10,... | collective-permute-start | bytes 73736 | tf_op jit(solution)/shard_map/ppermute | solution.py:27
  4.8 5.5 %collective-permute-start.3 = (f32[24,128]{1,0:T(8,128)S(1)}, f32[24,128]{1,0:T(8,128)S(1)}, u32[]{:S(2)}, u32[]{:S(2)}) collective-permute-start(f32[24,128]{1,0:T(8,128)S(1)} %bitcast.4), channel_id=1, source_target_pairs={{0,4},{2,6},{4,0},{6,2},{1,5},{3,7},{5,1},{7,3},{8,12},{10,14},{12... | collective-permute-start | bytes 36872 | tf_op jit(solution)/shard_map/ppermute | solution.py:31
  8.8 3.3 %collective-permute-start.2 = (f32[48,128]{1,0:T(8,128)S(1)}, f32[48,128]{1,0:T(8,128)S(1)}, u32[]{:S(2)}, u32[]{:S(2)}) collective-permute-start(f32[48,128]{1,0:T(8,128)S(1)} %collective-permute-done.1.mine_ref), channel_id=1, source_target_pairs={{0,1},{1,0},{2,3},{3,2},{4,5},{5,4},{6,7},{7,6},{8,9},{9,8},{10,11... | collective-permute-start | bytes 73736 | tf_op jit(solution)/shard_map/ppermute | solution.py:35
  10.4 1.7 %collective-permute-start.4 = (f32[24,128]{1,0:T(8,128)S(1)}, f32[24,128]{1,0:T(8,128)S(1)}, u32[]{:S(2)}, u32[]{:S(2)}) collective-permute-start(f32[24,128]{1,0:T(8,128)S(1)} %collective-permute-done.3.far_ref), channel_id=1, source_target_pairs={{0,1},{1,0},{2,3},{3,2},{4,5},{5,4},{6,7},{7,6},{8,9},{9,8},{10,11... | collective-permute-start | bytes 36872 | tf_op jit(solution)/shard_map/ppermute | solution.py:35
  28.7 9.1 %collective-permute-start.5 = (bf16[64,3072]{1,0:T(8,128)(2,1)S(1)}, bf16[64,3072]{1,0:T(8,128)(2,1)S(1)}, u32[]{:S(2)}, u32[]{:S(2)}) collective-permute-start(bf16[64,3072]{1,0:T(8,128)(2,1)S(1)} %shard_map.62.refs_0_), channel_id=1, source_target_pairs={{0,32},{1,25},{2,34},{3,27},{4,36},{5,29},{6,38},{7,31},{8,40},{9,... | collective-permute-start | bytes 1179656 | tf_op jit(solution)/shard_map/ppermute | solution.py:27
  30.2 7.9 %collective-permute-start.6 = (bf16[64,3072]{1,0:T(8,128)(2,1)S(1)}, bf16[64,3072]{1,0:T(8,128)(2,1)S(1)}, u32[]{:S(2)}, u32[]{:S(2)}) collective-permute-start(bf16[64,3072]{1,0:T(8,128)(2,1)S(1)} %shard_map.62.refs_0_), channel_id=1, source_target_pairs={{0,96},{1,9},{2,98},{3,11},{4,100},{5,13},{6,102},{7,15},{8,104},{... | collective-permute-start | bytes 1179656 | tf_op jit(solution)/shard_map/ppermute | solution.py:27
  37.8 6.9 %collective-permute-start.7 = (bf16[32,3072]{1,0:T(8,128)(2,1)S(1)}, bf16[32,3072]{1,0:T(8,128)(2,1)S(1)}, u32[]{:S(2)}, u32[]{:S(2)}) collective-permute-start(bf16[32,3072]{1,0:T(8,128)(2,1)S(1)} %shard_map.63), channel_id=1, source_target_pairs={{0,32},{1,25},{2,34},{3,27},{4,36},{5,29},{6,38},{7,31},{8,40},{9,... | collective-permute-start | bytes 589832 | tf_op jit(solution)/shard_map/ppermute | solution.py:27
  38.1 9.7 %collective-permute-start.16 = (bf16[32,3072]{1,0:T(8,128)(2,1)S(1)}, bf16[32,3072]{1,0:T(8,128)(2,1)S(1)}, u32[]{:S(2)}, u32[]{:S(2)}) collective-permute-start(bf16[32,3072]{1,0:T(8,128)(2,1)S(1)} %shard_map.72), channel_id=1, source_target_pairs={{0,96},{1,9},{2,98},{3,11},{4,100},{5,13},{6,102},{7,15},{8,104},{... | collective-permute-start | bytes 589832 | tf_op jit(solution)/shard_map/ppermute | solution.py:27
  44.8 12.6 %collective-permute-start.8 = (bf16[4,32,3072]{2,1,0:T(8,128)(2,1)S(1)}, bf16[4,32,3072]{2,1,0:T(8,128)(2,1)S(1)}, u32[]{:S(2)}, u32[]{:S(2)}) collective-permute-start(bf16[4,32,3072]{2,1,0:T(8,128)(2,1)S(1)} %shard_map.64.a0), channel_id=1, source_target_pairs={{0,24},{1,33},{2,26},{3,35},{4,28},{5,37},{6,30},{7,39},{8,0},{9,4... | collective-permute-start | bytes 2359304 | tf_op jit(solution)/shard_map/ppermute | solution.py:27
  47.9 13.3 %collective-permute-start.9 = (bf16[4,32,3072]{2,1,0:T(8,128)(2,1)S(1)}, bf16[4,32,3072]{2,1,0:T(8,128)(2,1)S(1)}, u32[]{:S(2)}, u32[]{:S(2)}) collective-permute-start(bf16[4,32,3072]{2,1,0:T(8,128)(2,1)S(1)} %shard_map.64.a0), channel_id=1, source_target_pairs={{0,8},{1,97},{2,10},{3,99},{4,12},{5,101},{6,14},{7,103},{8,16},{9... | collective-permute-start | bytes 2359304 | tf_op jit(solution)/shard_map/ppermute | solution.py:27
  47.9 17.9 %collective-permute-start.17 = (bf16[4,32,3072]{2,1,0:T(8,128)(2,1)S(1)}, bf16[4,32,3072]{2,1,0:T(8,128)(2,1)S(1)}, u32[]{:S(2)}, u32[]{:S(2)}) collective-permute-start(bf16[4,32,3072]{2,1,0:T(8,128)(2,1)S(1)} %shard_map.73.a0), channel_id=1, source_target_pairs={{0,24},{1,33},{2,26},{3,35},{4,28},{5,37},{6,30},{7,39},{8,0},{9,4... | collective-permute-start | bytes 2359304 | tf_op jit(solution)/shard_map/ppermute | solution.py:27
  51.2 18.4 %collective-permute-start.18 = (bf16[4,32,3072]{2,1,0:T(8,128)(2,1)S(1)}, bf16[4,32,3072]{2,1,0:T(8,128)(2,1)S(1)}, u32[]{:S(2)}, u32[]{:S(2)}) collective-permute-start(bf16[4,32,3072]{2,1,0:T(8,128)(2,1)S(1)} %shard_map.73.a0), channel_id=1, source_target_pairs={{0,8},{1,97},{2,10},{3,99},{4,12},{5,101},{6,14},{7,103},{8,16},{9... | collective-permute-start | bytes 2359304 | tf_op jit(solution)/shard_map/ppermute | solution.py:27
  57.4 14.7 %collective-permute-start.10 = (bf16[2,32,3072]{2,1,0:T(8,128)(2,1)S(1)}, bf16[2,32,3072]{2,1,0:T(8,128)(2,1)S(1)}, u32[]{:S(2)}, u32[]{:S(2)}) collective-permute-start(bf16[2,32,3072]{2,1,0:T(8,128)(2,1)S(1)} %shard_map.67), channel_id=1, source_target_pairs={{0,24},{1,33},{2,26},{3,35},{4,28},{5,37},{6,30},{7,39},{8,0},{9,4... | collective-permute-start | bytes 1179656 | tf_op jit(solution)/shard_map/ppermute | solution.py:27
  61.2 12.5 %collective-permute-start.11 = (bf16[2,32,3072]{2,1,0:T(8,128)(2,1)S(1)}, bf16[2,32,3072]{2,1,0:T(8,128)(2,1)S(1)}, u32[]{:S(2)}, u32[]{:S(2)}) collective-permute-start(bf16[2,32,3072]{2,1,0:T(8,128)(2,1)S(1)} %shard_map.68), channel_id=1, source_target_pairs={{0,8},{1,97},{2,10},{3,99},{4,12},{5,101},{6,14},{7,103},{8,16},{9... | collective-permute-start | bytes 1179656 | tf_op jit(solution)/shard_map/ppermute | solution.py:27
  65.8 10.2 %collective-permute-start.19 = (bf16[2,32,3072]{2,1,0:T(8,128)(2,1)S(1)}, bf16[2,32,3072]{2,1,0:T(8,128)(2,1)S(1)}, u32[]{:S(2)}, u32[]{:S(2)}) collective-permute-start(bf16[2,32,3072]{2,1,0:T(8,128)(2,1)S(1)} %shard_map.75), channel_id=1, source_target_pairs={{0,24},{1,33},{2,26},{3,35},{4,28},{5,37},{6,30},{7,39},{8,0},{9,4... | collective-permute-start | bytes 1179656 | tf_op jit(solution)/shard_map/ppermute | solution.py:27
  69.6 9.1 %collective-permute-start.20 = (bf16[2,32,3072]{2,1,0:T(8,128)(2,1)S(1)}, bf16[2,32,3072]{2,1,0:T(8,128)(2,1)S(1)}, u32[]{:S(2)}, u32[]{:S(2)}) collective-permute-start(bf16[2,32,3072]{2,1,0:T(8,128)(2,1)S(1)} %shard_map.76), channel_id=1, source_target_pairs={{0,8},{1,97},{2,10},{3,99},{4,12},{5,101},{6,14},{7,103},{8,16},{9... | collective-permute-start | bytes 1179656 | tf_op jit(solution)/shard_map/ppermute | solution.py:27
  74.5 5.2 %collective-permute-start.12 = (f32[4,80,512]{2,1,0:T(8,128)S(1)}, f32[4,80,512]{2,1,0:T(8,128)S(1)}, u32[]{:S(2)}, u32[]{:S(2)}) collective-permute-start(f32[4,80,512]{2,1,0:T(8,128)S(1)} %get-tuple-element.32), channel_id=1, source_target_pairs={{0,1},{1,0},{2,3},{3,2},{4,5},{5,4},{6,7},{7,6},{8,9},{9,8},{10,11... | collective-permute-start | bytes 1966088 | tf_op jit(solution)/shard_map/ppermute | solution.py:35
  79.5 2.2 %collective-permute-start.21 = (f32[4,64,512]{2,1,0:T(8,128)S(1)}, f32[4,64,512]{2,1,0:T(8,128)S(1)}, u32[]{:S(2)}, u32[]{:S(2)}) collective-permute-start(f32[4,64,512]{2,1,0:T(8,128)S(1)} %get-tuple-element.41), channel_id=1, source_target_pairs={{0,1},{1,0},{2,3},{3,2},{4,5},{5,4},{6,7},{7,6},{8,9},{9,8},{10,11... | collective-permute-start | bytes 1572872 | tf_op jit(solution)/shard_map/ppermute | solution.py:35
  79.8 12.0 %collective-permute-start.13 = (f32[80,512]{1,0:T(8,128)S(1)}, f32[80,512]{1,0:T(8,128)S(1)}, u32[]{:S(2)}, u32[]{:S(2)}) collective-permute-start(f32[80,512]{1,0:T(8,128)S(1)} %get-tuple-element.35), channel_id=1, source_target_pairs={{0,2},{1,7},{2,4},{3,1},{4,6},{5,3},{6,0},{7,5},{8,10},{9,15},{10,... | collective-permute-start | bytes 491528 | tf_op jit(solution)/shard_map/ppermute | solution.py:27
  81.7 6.8 %collective-permute-start.22 = (f32[64,512]{1,0:T(8,128)S(1)}, f32[64,512]{1,0:T(8,128)S(1)}, u32[]{:S(2)}, u32[]{:S(2)}) collective-permute-start(f32[64,512]{1,0:T(8,128)S(1)} %get-tuple-element.44), channel_id=1, source_target_pairs={{0,2},{1,7},{2,4},{3,1},{4,6},{5,3},{6,0},{7,5},{8,10},{9,15},{10,... | collective-permute-start | bytes 393224 | tf_op jit(solution)/shard_map/ppermute | solution.py:27
  83.1 16.6 %collective-permute-start.24 = (f32[64,512]{1,0:T(8,128)S(1)}, f32[64,512]{1,0:T(8,128)S(1)}, u32[]{:S(2)}, u32[]{:S(2)}) collective-permute-start(f32[64,512]{1,0:T(8,128)S(1)} %get-tuple-element.45), channel_id=1, source_target_pairs={{0,6},{1,3},{2,0},{3,5},{4,2},{5,7},{6,4},{7,1},{8,14},{9,11},{10,... | collective-permute-start | bytes 393224 | tf_op jit(solution)/shard_map/ppermute | solution.py:27
  88.5 11.3 %collective-permute-start.23 = (f32[64,512]{1,0:T(8,128)S(1)}, f32[64,512]{1,0:T(8,128)S(1)}, u32[]{:S(2)}, u32[]{:S(2)}) collective-permute-start(f32[64,512]{1,0:T(8,128)S(1)} %add.19), channel_id=1, source_target_pairs={{0,2},{1,7},{2,4},{3,1},{4,6},{5,3},{6,0},{7,5},{8,10},{9,15},{10,... | collective-permute-start | bytes 393224 | tf_op jit(solution)/shard_map/ppermute | solution.py:27
  89.1 6.0 %collective-permute-start.15 = (f32[80,512]{1,0:T(8,128)S(1)}, f32[80,512]{1,0:T(8,128)S(1)}, u32[]{:S(2)}, u32[]{:S(2)}) collective-permute-start(f32[80,512]{1,0:T(8,128)S(1)} %get-tuple-element.36), channel_id=1, source_target_pairs={{0,6},{1,3},{2,0},{3,5},{4,2},{5,7},{6,4},{7,1},{8,14},{9,11},{10,... | collective-permute-start | bytes 491528 | tf_op jit(solution)/shard_map/ppermute | solution.py:27
  91.9 6.6 %collective-permute-start.14 = (f32[80,512]{1,0:T(8,128)S(1)}, f32[80,512]{1,0:T(8,128)S(1)}, u32[]{:S(2)}, u32[]{:S(2)}) collective-permute-start(f32[80,512]{1,0:T(8,128)S(1)} %add.18), channel_id=1, source_target_pairs={{0,2},{1,7},{2,4},{3,1},{4,6},{5,3},{6,0},{7,5},{8,10},{9,15},{10,... | collective-permute-start | bytes 491528 | tf_op jit(solution)/shard_map/ppermute | solution.py:27
  101.1 5.7 %collective-permute-start.25 = (bf16[128,128]{1,0:T(8,128)(2,1)S(1)}, bf16[128,128]{1,0:T(8,128)(2,1)S(1)}, u32[]{:S(2)}, u32[]{:S(2)}) collective-permute-start(bf16[128,128]{1,0:T(8,128)(2,1)S(1)} %get-tuple-element.47), channel_id=1, source_target_pairs={{0,64},{1,17},{2,66},{3,19},{4,68},{5,21},{6,70},{7,23},{8,72},{9,... | collective-permute-start | bytes 98312 | tf_op jit(solution)/shard_map/ppermute | solution.py:27
  101.7 5.5 %collective-permute-start.26 = (bf16[128,128]{1,0:T(8,128)(2,1)S(1)}, bf16[128,128]{1,0:T(8,128)(2,1)S(1)}, u32[]{:S(2)}, u32[]{:S(2)}) collective-permute-start(bf16[128,128]{1,0:T(8,128)(2,1)S(1)} %get-tuple-element.47), channel_id=1, source_target_pairs={{0,32},{1,9},{2,34},{3,11},{4,36},{5,13},{6,38},{7,15},{8,40},{9,1... | collective-permute-start | bytes 98312 | tf_op jit(solution)/shard_map/ppermute | solution.py:27
  102.3 4.9 %collective-permute-start.27 = (bf16[128,128]{1,0:T(8,128)(2,1)S(1)}, bf16[128,128]{1,0:T(8,128)(2,1)S(1)}, u32[]{:S(2)}, u32[]{:S(2)}) collective-permute-start(bf16[128,128]{1,0:T(8,128)(2,1)S(1)} %get-tuple-element.47), channel_id=1, source_target_pairs={{0,96},{1,25},{2,98},{3,27},{4,100},{5,29},{6,102},{7,31},{8,104},... | collective-permute-start | bytes 98312 | tf_op jit(solution)/shard_map/ppermute | solution.py:27
  107.2 5.6 %collective-permute-start.28 = (bf16[128,128]{1,0:T(8,128)(2,1)S(1)}, bf16[128,128]{1,0:T(8,128)(2,1)S(1)}, u32[]{:S(2)}, u32[]{:S(2)}) collective-permute-start(bf16[128,128]{1,0:T(8,128)(2,1)S(1)} %maximum_maximum_fusion), channel_id=1, source_target_pairs={{0,16},{1,65},{2,18},{3,67},{4,20},{5,69},{6,22},{7,71},{8,24},{9,... | collective-permute-start | bytes 98312 | tf_op jit(solution)/shard_map/ppermute | solution.py:27
  107.3 5.5 %collective-permute-start.29 = (bf16[128,128]{1,0:T(8,128)(2,1)S(1)}, bf16[128,128]{1,0:T(8,128)(2,1)S(1)}, u32[]{:S(2)}, u32[]{:S(2)}) collective-permute-start(bf16[128,128]{1,0:T(8,128)(2,1)S(1)} %maximum_maximum_fusion), channel_id=1, source_target_pairs={{0,8},{1,33},{2,10},{3,35},{4,12},{5,37},{6,14},{7,39},{8,16},{9,4... | collective-permute-start | bytes 98312 | tf_op jit(solution)/shard_map/ppermute | solution.py:27
  107.7 5.1 %collective-permute-start.30 = (bf16[128,128]{1,0:T(8,128)(2,1)S(1)}, bf16[128,128]{1,0:T(8,128)(2,1)S(1)}, u32[]{:S(2)}, u32[]{:S(2)}) collective-permute-start(bf16[128,128]{1,0:T(8,128)(2,1)S(1)} %maximum_maximum_fusion), channel_id=1, source_target_pairs={{0,24},{1,97},{2,26},{3,99},{4,28},{5,101},{6,30},{7,103},{8,0},{9... | collective-permute-start | bytes 98312 | tf_op jit(solution)/shard_map/ppermute | solution.py:27
  (3 other events, 10.2 us)

commit v3 on v2

--- a/solution.py
+++ b/solution.py
@@ -11,7 +11,7 @@
 AXES = ("x", "y", "z", "c")
 CHUNKS = 2
 LOW = 128
-COLUMNS = 3
+COLUMNS = 6
 PLACES = [
     (x, y, z, c) for x in range(RING) for y in range(RING) for z in range(RING) for c in range(2)
 ]
@@ -155,16 +155,19 @@
     )(a, b)
 
 
-def copy_kernel(a_ref, out_ref):
-    out_ref[...] = a_ref[...]
+def fetch_kernel(a_ref, *outs):
+    rows = outs[0].shape[0]
+    for k, out in enumerate(outs):
+        out[...] = a_ref[k * rows : (k + 1) * rows, :]
 
 
 def fetched(a):
-    return pl.pallas_call(
-        copy_kernel,
-        out_shape=out_of(a.shape, a.dtype),
+    one = out_of((a.shape[0] // CHUNKS, a.shape[1]), a.dtype)
+    return pl.pallas_call(
+        fetch_kernel,
+        out_shape=(one,) * CHUNKS,
         in_specs=[VMEM],
-        out_specs=VMEM,
+        out_specs=(VMEM,) * CHUNKS,
         compiler_params=room(4),
     )(a)
 
@@ -283,7 +286,7 @@
     )(index, table, scale, plain)
 
 
-def ring_gather(value, first, turn, dim):
+def ring_gather(value, first, turn, halves):
     def line(sign):
         def target(x, y, z, c):
             step = sign if c == turn else -sign
@@ -295,22 +298,22 @@
 
     behind = shift(value, line(1))
     ahead = shift(value, line(-1))
-    low = shift(half_of(behind, 0, dim), line(1))
-    high = shift(half_of(ahead, 1, dim), line(-1))
+    if not halves:
+        return [value, behind, ahead, shift(behind, line(1))]
+    low = shift(half_of(behind, 0), line(1))
+    high = shift(half_of(ahead, 1), line(-1))
     return [value, behind, ahead, low, high]
 
 
-def half_kernel(a_ref, out_ref, *, which, dim):
-    size = out_ref.shape[dim]
-    part = pl.ds(which * size, size)
-    out_ref[...] = a_ref[part] if dim == 0 else a_ref[:, part]
-
-
-def half_of(a, which, dim):
-    shape = tuple(n // 2 if d == dim else n for d, n in enumerate(a.shape))
-    return pl.pallas_call(
-        lambda *refs: half_kernel(*refs, which=which, dim=dim),
-        out_shape=out_of(shape, a.dtype),
+def half_kernel(a_ref, out_ref, *, which):
+    size = out_ref.shape[0]
+    out_ref[...] = a_ref[which * size : (which + 1) * size]
+
+
+def half_of(a, which):
+    return pl.pallas_call(
+        lambda *refs: half_kernel(*refs, which=which),
+        out_shape=out_of((a.shape[0] // 2, *a.shape[1:]), a.dtype),
         in_specs=[VMEM],
         out_specs=VMEM,
         compiler_params=room(3),
@@ -322,24 +325,19 @@
     return (0, -step, step, 2)[k]
 
 
-def stack_kernel(own, behind, ahead, opposite, out_ref, *, which):
-    rows = out_ref.shape[1]
-    part = slice(which * rows, (which + 1) * rows)
-    for k, a in enumerate((own, behind, ahead)):
-        out_ref[k] = a[part, :]
-    out_ref[3] = opposite[...]
-
-
-def stacked(near, which):
-    own, behind, ahead = near[:3]
-    opposite = near[3 + which]
-    return pl.pallas_call(
-        lambda *refs: stack_kernel(*refs, which=which),
-        out_shape=out_of((RING, *opposite.shape), own.dtype),
+def stack_kernel(a0, a1, a2, a3, out_ref):
+    for k, a in enumerate((a0, a1, a2, a3)):
+        out_ref[k] = a[...]
+
+
+def stacked(pieces):
+    return pl.pallas_call(
+        stack_kernel,
+        out_shape=out_of((len(pieces), *pieces[0].shape), pieces[0].dtype),
         in_specs=[VMEM] * 4,
         out_specs=VMEM,
         compiler_params=room(4),
-    )(own, behind, ahead, opposite)
+    )(*pieces)
 
 
 def early_kernel(a0, a1, a2, dosage_ref, out_ref, lhs_ref):
@@ -445,10 +443,10 @@
     return target
 
 
-def reduced(far, dosage, totals, with_totals):
+def reduced(far, dosage, totals, with_totals, turn):
     early = early_product(far[:3], dosage)
     low, high = far[3:]
-    keep, send = late_product(early, low, high, dosage, totals, with_totals, 0, 1)
+    keep, send = late_product(early, low, high, dosage, totals, with_totals, turn, 1)
     got = other_core(send)
     own, ahead, opposite, behind = core_sum(keep, got)
     passing = shift(opposite, z_line(1))
@@ -547,18 +545,20 @@
 def per_device(dosage, phenotype, perm_index, seg_lengths):
     samples, width = dosage.shape
     x, y = lax.axis_index("x"), lax.axis_index("y")
-    perm_index = fetched(perm_index)
+    chunks = fetched(perm_index)
     dosage_bf, totals = convert_dosage(dosage)
     table, scale, pheno_var, plain = make_table(phenotype.reshape(-1, LOW))
     ends = (jnp.cumsum(seg_lengths) - 1 - (x * RING + y) * width)[None, :].astype(jnp.int32)
     count = float(samples * lax.axis_size("z") * lax.axis_size("c"))
 
-    traits = lookup(perm_index, table, scale, plain)
-    near = ring_gather(traits, True, 0, 0)
-    far = [ring_gather(stacked(near, k), False, 1, 0) for k in range(CHUNKS)]
-    parts = reduced(far[0], dosage_bf, totals, True)
+    far = []
+    for k, chunk in enumerate(chunks):
+        traits = lookup(chunk, table, scale, plain)
+        near = ring_gather(traits, True, k, False)
+        far.append(ring_gather(stacked(near), False, 1, True))
+    parts = reduced(far[0], dosage_bf, totals, True, 0)
     z0, most0, inverse = final_first(pheno_var, ends, parts, totals.shape[0], count)
-    parts = reduced(far[1], dosage_bf, totals, False)
+    parts = reduced(far[1], dosage_bf, totals, False, 1)
     zscore, most = final_second(ends, inverse, z0, most0, parts, count)
     return (zscore, largest(largest(most, True), False).astype(jnp.float32))
 

time: 114 us -> 110 us (0.965)
  waiting for transfers between devices: 42.4 us -> 35.7 us
  starting transfers between devices: 42.4 us -> 44.1 us
    ppermute x25 -> x27, waiting for transfers between devices: 38.7 us -> 32.3 us  [shift(): lax.ppermute(value, AXES, [(at(*d), at(*target(*d))) for d in PLACES])]
    ppermute x25 -> x27, starting transfers between devices: 37.8 us -> 40 us  [shift(): lax.ppermute(value, AXES, [(at(*d), at(*target(*d))) for d in PLACES])]
    pallas_call x1 -> x2, Pallas kernels: 15.8 us -> 16.5 us  [lookup(): pl.pallas_call(lookup_kernel, out_shape=out_of(index.shape, jnp.bfloat16)...]
  transfers between devices with their start and end apart: 31 -> 33, of which waited for: 16 -> 16; matrix products, arithmetic and copies ran while one was open for 0% -> 0% of each run, Pallas kernels for 6% -> 14%
where the time goes in v3:
time: 110 us; the launch traced here: 109 us
  starting transfers between devices  44.1 us (40%)
  waiting for transfers between devices  35.7 us (32%)
  Pallas kernels  25.6 us (23%)
  local copies, waits for them, and re-layouts  2.19 us (2%)
    ppermute x27, starting transfers between devices, shift(): lax.ppermute(value, AXES, [(at(*d), at(*target(*d))) for d in PLACES])  40 us
    ppermute x27, waiting for transfers between devices, shift(): lax.ppermute(value, AXES, [(at(*d), at(*target(*d))) for d in PLACES])  32.3 us
    pallas_call x2, Pallas kernels, lookup(): pl.pallas_call(lookup_kernel, out_shape=out_of(index.shape, jnp.bfloat16)...  16.5 us
    ppermute x1, starting transfers between devices, along(): lax.ppermute(value, axis, [(i, (i + step) % RING) for i in range(RING)])  3.58 us
    pallas_call x2, Pallas kernels, early_product(): pl.pallas_call(early_kernel, out_shape=out_of((rows, dosage.shape[1]), jn...  2.74 us
  transfers between devices with their start and end apart: 33, of which 16 were waited for; matrix products, arithmetic and copies ran while one was open for 0% of the time, Pallas kernels for 14%

profile of v3, /device:TPU:0, one launch (start us, length us, event | category | flops | bytes accessed | tf_op | source)
XLA Modules:
  0.0 109.5 jit_solution(4740836644279521456)
XLA Ops:
  0.7 1.4 %collective-permute-done.b_ref = f32[24,128]{1,0:T(8,128)S(1)} collective-permute-done((f32[24,128]{1,0:T(8,128)}, f32[24,128]{1,0:T(8,128)S(1)}, u32[]{:S(2)}, u32[]{:S(2)}) %collective-permute-start) | collective-permute-done | bytes 12320 | tf_op jit(solution)/shard_map/ppermute | solution.py:35
  3.2 2.0 %collective-permute-start.1 = (f32[48,128]{1,0:T(8,128)S(1)}, f32[48,128]{1,0:T(8,128)S(1)}, u32[]{:S(2)}, u32[]{:S(2)}) collective-permute-start(f32[48,128]{1,0:T(8,128)S(1)} %shard_map.59.pair_ref), channel_id=1, source_target_pairs={{0,2},{1,7},{2,4},{3,1},{4,6},{5,3},{6,0},{7,5},{8,10},{9,15},{10,... | collective-permute-start | bytes 73736 | tf_op jit(solution)/shard_map/ppermute | solution.py:27
  5.2 3.6 %collective-permute-start.3 = (f32[24,128]{1,0:T(8,128)S(1)}, f32[24,128]{1,0:T(8,128)S(1)}, u32[]{:S(2)}, u32[]{:S(2)}) collective-permute-start(f32[24,128]{1,0:T(8,128)S(1)} %bitcast.4), channel_id=1, source_target_pairs={{0,4},{2,6},{4,0},{6,2},{1,5},{3,7},{5,1},{7,3},{8,12},{10,14},{12... | collective-permute-start | bytes 36872 | tf_op jit(solution)/shard_map/ppermute | solution.py:31
  9.1 1.6 %collective-permute-done.3.far_ref = f32[24,128]{1,0:T(8,128)S(1)} collective-permute-done((f32[24,128]{1,0:T(8,128)S(1)}, f32[24,128]{1,0:T(8,128)S(1)}, u32[]{:S(2)}, u32[]{:S(2)}) %collective-permute-start.3) | collective-permute-done | bytes 12320 | tf_op jit(solution)/shard_map/ppermute | solution.py:31
  12.9 8.3 %shard_map.62.a0 = bf16[32,3072]{1,0:T(8,128)(2,1)S(1)} custom-call(s32[32,3072]{1,0:T(8,128)S(1)} %get-tuple-element.28.index_ref, s32[96,128]{1,0:T(8,128)S(1)} %get-tuple-element.29.table_ref, f32[1,128]{1,0:T(1,128)S(1)} %get-tuple-element.30.scale_ref, bf16[96,256]{1,0:T(8,128)(2,1)S(1)} %get-tuple-element.31.plain_ref), custom_call_target="tpu_custom_call" | custom-call | tf_op jit(solution)/shard_map/pallas_call | solution.py:275
  21.2 1.6 %collective-permute-start.5 = (bf16[32,3072]{1,0:T(8,128)(2,1)S(1)}, bf16[32,3072]{1,0:T(8,128)(2,1)S(1)}, u32[]{:S(2)}, u32[]{:S(2)}) collective-permute-start(bf16[32,3072]{1,0:T(8,128)(2,1)S(1)} %shard_map.62.a0), channel_id=1, source_target_pairs={{0,32},{1,25},{2,34},{3,27},{4,36},{5,29},{6,38},{7,31},{8,40},{9,... | collective-permute-start | bytes 589832 | tf_op jit(solution)/shard_map/ppermute | solution.py:27
  22.8 8.3 %shard_map.71.a0 = bf16[32,3072]{1,0:T(8,128)(2,1)S(1)} custom-call(s32[32,3072]{1,0:T(8,128)S(1)} %get-tuple-element.43.index_ref, s32[96,128]{1,0:T(8,128)S(1)} %get-tuple-element.29.table_ref, f32[1,128]{1,0:T(1,128)S(1)} %get-tuple-element.30.scale_ref, bf16[96,256]{1,0:T(8,128)(2,1)S(1)} %get-tuple-element.31.plain_ref), custom_call_target="tpu_custom_call" | custom-call | tf_op jit(solution)/shard_map/pallas_call | solution.py:275
  31.0 1.8 %collective-permute-start.16 = (bf16[32,3072]{1,0:T(8,128)(2,1)S(1)}, bf16[32,3072]{1,0:T(8,128)(2,1)S(1)}, u32[]{:S(2)}, u32[]{:S(2)}) collective-permute-start(bf16[32,3072]{1,0:T(8,128)(2,1)S(1)} %shard_map.71.a0), channel_id=1, source_target_pairs={{0,96},{1,9},{2,98},{3,11},{4,100},{5,13},{6,102},{7,15},{8,104},{... | collective-permute-start | bytes 589832 | tf_op jit(solution)/shard_map/ppermute | solution.py:27
  32.8 1.6 %collective-permute-start.6 = (bf16[32,3072]{1,0:T(8,128)(2,1)S(1)}, bf16[32,3072]{1,0:T(8,128)(2,1)S(1)}, u32[]{:S(2)}, u32[]{:S(2)}) collective-permute-start(bf16[32,3072]{1,0:T(8,128)(2,1)S(1)} %shard_map.62.a0), channel_id=1, source_target_pairs={{0,96},{1,9},{2,98},{3,11},{4,100},{5,13},{6,102},{7,15},{8,104},{... | collective-permute-start | bytes 589832 | tf_op jit(solution)/shard_map/ppermute | solution.py:27
  35.2 1.6 %collective-permute-done.16.a1 = bf16[32,3072]{1,0:T(8,128)(2,1)S(1)} collective-permute-done((bf16[32,3072]{1,0:T(8,128)(2,1)S(1)}, bf16[32,3072]{1,0:T(8,128)(2,1)S(1)}, u32[]{:S(2)}, u32[]{:S(2)}) %collective-permute-start.16) | collective-permute-done | bytes 196640 | tf_op jit(solution)/shard_map/ppermute | solution.py:27
  36.8 2.9 %collective-permute-start.18 = (bf16[32,3072]{1,0:T(8,128)(2,1)S(1)}, bf16[32,3072]{1,0:T(8,128)(2,1)S(1)}, u32[]{:S(2)}, u32[]{:S(2)}) collective-permute-start(bf16[32,3072]{1,0:T(8,128)(2,1)S(1)} %collective-permute-done.16.a1), channel_id=1, source_target_pairs={{0,96},{1,9},{2,98},{3,11},{4,100},{5,13},{6,102},{7,15},{8,104},{... | collective-permute-start | bytes 589832 | tf_op jit(solution)/shard_map/ppermute | solution.py:27
  39.7 1.6 %collective-permute-done.7.a3 = bf16[32,3072]{1,0:T(8,128)(2,1)S(1)} collective-permute-done((bf16[32,3072]{1,0:T(8,128)(2,1)S(1)}, bf16[32,3072]{1,0:T(8,128)(2,1)S(1)}, u32[]{:S(2)}, u32[]{:S(2)}) %collective-permute-start.7) | collective-permute-done | bytes 196640 | tf_op jit(solution)/shard_map/ppermute | solution.py:27
  41.3 3.1 %collective-permute-start.8 = (bf16[4,32,3072]{2,1,0:T(8,128)(2,1)S(1)}, bf16[4,32,3072]{2,1,0:T(8,128)(2,1)S(1)}, u32[]{:S(2)}, u32[]{:S(2)}) collective-permute-start(bf16[4,32,3072]{2,1,0:T(8,128)(2,1)S(1)} %shard_map.63.a0), channel_id=1, source_target_pairs={{0,24},{1,33},{2,26},{3,35},{4,28},{5,37},{6,30},{7,39},{8,0},{9,4... | collective-permute-start | bytes 2359304 | tf_op jit(solution)/shard_map/ppermute | solution.py:27
  44.5 3.3 %collective-permute-start.19 = (bf16[4,32,3072]{2,1,0:T(8,128)(2,1)S(1)}, bf16[4,32,3072]{2,1,0:T(8,128)(2,1)S(1)}, u32[]{:S(2)}, u32[]{:S(2)}) collective-permute-start(bf16[4,32,3072]{2,1,0:T(8,128)(2,1)S(1)} %shard_map.72.a0), channel_id=1, source_target_pairs={{0,24},{1,33},{2,26},{3,35},{4,28},{5,37},{6,30},{7,39},{8,0},{9,4... | collective-permute-start | bytes 2359304 | tf_op jit(solution)/shard_map/ppermute | solution.py:27
  47.8 6.1 %collective-permute-done.8.a1.refs_0_ = bf16[4,32,3072]{2,1,0:T(8,128)(2,1)S(1)} collective-permute-done((bf16[4,32,3072]{2,1,0:T(8,128)(2,1)S(1)}, bf16[4,32,3072]{2,1,0:T(8,128)(2,1)S(1)}, u32[]{:S(2)}, u32[]{:S(2)}) %collective-permute-start.8) | collective-permute-done | bytes 786464 | tf_op jit(solution)/shard_map/ppermute | solution.py:27
  54.0 3.8 %collective-permute-start.10 = (bf16[2,32,3072]{2,1,0:T(8,128)(2,1)S(1)}, bf16[2,32,3072]{2,1,0:T(8,128)(2,1)S(1)}, u32[]{:S(2)}, u32[]{:S(2)}) collective-permute-start(bf16[2,32,3072]{2,1,0:T(8,128)(2,1)S(1)} %shard_map.66), channel_id=1, source_target_pairs={{0,24},{1,33},{2,26},{3,35},{4,28},{5,37},{6,30},{7,39},{8,0},{9,4... | collective-permute-start | bytes 1179656 | tf_op jit(solution)/shard_map/ppermute | solution.py:27
  57.9 4.5 %collective-permute-done.19.a1.refs_0_ = bf16[4,32,3072]{2,1,0:T(8,128)(2,1)S(1)} collective-permute-done((bf16[4,32,3072]{2,1,0:T(8,128)(2,1)S(1)}, bf16[4,32,3072]{2,1,0:T(8,128)(2,1)S(1)}, u32[]{:S(2)}, u32[]{:S(2)}) %collective-permute-start.19) | collective-permute-done | bytes 786464 | tf_op jit(solution)/shard_map/ppermute | solution.py:27
  62.4 3.8 %collective-permute-start.21 = (bf16[2,32,3072]{2,1,0:T(8,128)(2,1)S(1)}, bf16[2,32,3072]{2,1,0:T(8,128)(2,1)S(1)}, u32[]{:S(2)}, u32[]{:S(2)}) collective-permute-start(bf16[2,32,3072]{2,1,0:T(8,128)(2,1)S(1)} %shard_map.74), channel_id=1, source_target_pairs={{0,24},{1,33},{2,26},{3,35},{4,28},{5,37},{6,30},{7,39},{8,0},{9,4... | collective-permute-start | bytes 1179656 | tf_op jit(solution)/shard_map/ppermute | solution.py:27
  67.5 1.4 %shard_map.65.refs_0_ = f32[384,512]{1,0:T(8,128)S(1)} custom-call(bf16[4,32,3072]{2,1,0:T(8,128)(2,1)S(1)} %shard_map.63.a0, bf16[4,32,3072]{2,1,0:T(8,128)(2,1)S(1)} %collective-permute-done.8.a1.refs_0_, bf16[4,32,3072]{2,1,0:T(8,128)(2,1)S(1)} %collective-permute-done.9.a2.refs_0_, bf16[3072,512]{1,0:T(8,128)(2,1)S(1)} %get-tuple-element.32.dosage_ref.refs_3_), custom_call_target="tpu_custom_call" | custom-call | tf_op jit(solution)/shard_map/pallas_call | solution.py:352
  68.9 1.4 %collective-permute-done.11.refs_2_ = bf16[2,32,3072]{2,1,0:T(8,128)(2,1)S(1)} collective-permute-done((bf16[2,32,3072]{2,1,0:T(8,128)(2,1)S(1)}, bf16[2,32,3072]{2,1,0:T(8,128)(2,1)S(1)}, u32[]{:S(2)}, u32[]{:S(2)}) %collective-permute-start.11) | collective-permute-done | bytes 393248 | tf_op jit(solution)/shard_map/ppermute | solution.py:27
  72.6 2.9 %collective-permute-done.22.refs_2_ = bf16[2,32,3072]{2,1,0:T(8,128)(2,1)S(1)} collective-permute-done((bf16[2,32,3072]{2,1,0:T(8,128)(2,1)S(1)}, bf16[2,32,3072]{2,1,0:T(8,128)(2,1)S(1)}, u32[]{:S(2)}, u32[]{:S(2)}) %collective-permute-start.22) | collective-permute-done | bytes 393248 | tf_op jit(solution)/shard_map/ppermute | solution.py:27
  76.4 1.4 %collective-permute-start.13 = (f32[80,512]{1,0:T(8,128)S(1)}, f32[80,512]{1,0:T(8,128)S(1)}, u32[]{:S(2)}, u32[]{:S(2)}) collective-permute-start(f32[80,512]{1,0:T(8,128)S(1)} %get-tuple-element.38), channel_id=1, source_target_pairs={{0,2},{1,7},{2,4},{3,1},{4,6},{5,3},{6,0},{7,5},{8,10},{9,15},{10,... | collective-permute-start | bytes 491528 | tf_op jit(solution)/shard_map/ppermute | solution.py:27
  78.2 1.4 %collective-permute-start.24 = (f32[64,512]{1,0:T(8,128)S(1)}, f32[64,512]{1,0:T(8,128)S(1)}, u32[]{:S(2)}, u32[]{:S(2)}) collective-permute-start(f32[64,512]{1,0:T(8,128)S(1)} %get-tuple-element.48), channel_id=1, source_target_pairs={{0,2},{1,7},{2,4},{3,1},{4,6},{5,3},{6,0},{7,5},{8,10},{9,15},{10,... | collective-permute-start | bytes 393224 | tf_op jit(solution)/shard_map/ppermute | solution.py:27
  80.0 1.9 %collective-permute-start.26 = (f32[64,512]{1,0:T(8,128)S(1)}, f32[64,512]{1,0:T(8,128)S(1)}, u32[]{:S(2)}, u32[]{:S(2)}) collective-permute-start(f32[64,512]{1,0:T(8,128)S(1)} %get-tuple-element.49), channel_id=1, source_target_pairs={{0,6},{1,3},{2,0},{3,5},{4,2},{5,7},{6,4},{7,1},{8,14},{9,11},{10,... | collective-permute-start | bytes 393224 | tf_op jit(solution)/shard_map/ppermute | solution.py:27
  81.9 2.9 %collective-permute-done.24 = f32[64,512]{1,0:T(8,128)S(1)} collective-permute-done((f32[64,512]{1,0:T(8,128)S(1)}, f32[64,512]{1,0:T(8,128)S(1)}, u32[]{:S(2)}, u32[]{:S(2)}) %collective-permute-start.24) | collective-permute-done | bytes 131104 | tf_op jit(solution)/shard_map/ppermute | solution.py:27
  86.1 2.0 %collective-permute-start.15 = (f32[80,512]{1,0:T(8,128)S(1)}, f32[80,512]{1,0:T(8,128)S(1)}, u32[]{:S(2)}, u32[]{:S(2)}) collective-permute-start(f32[80,512]{1,0:T(8,128)S(1)} %get-tuple-element.39), channel_id=1, source_target_pairs={{0,6},{1,3},{2,0},{3,5},{4,2},{5,7},{6,4},{7,1},{8,14},{9,11},{10,... | collective-permute-start | bytes 491528 | tf_op jit(solution)/shard_map/ppermute | solution.py:27
  88.2 3.7 %collective-permute-done.15.refs_4_ = f32[80,512]{1,0:T(8,128)S(1)} collective-permute-done((f32[80,512]{1,0:T(8,128)S(1)}, f32[80,512]{1,0:T(8,128)S(1)}, u32[]{:S(2)}, u32[]{:S(2)}) %collective-permute-start.15) | collective-permute-done | bytes 163872 | tf_op jit(solution)/shard_map/ppermute | solution.py:27
  91.9 2.8 %collective-permute-done.14.refs_3_ = f32[80,512]{1,0:T(8,128)S(1)} collective-permute-done((f32[80,512]{1,0:T(8,128)S(1)}, f32[80,512]{1,0:T(8,128)S(1)}, u32[]{:S(2)}, u32[]{:S(2)}) %collective-permute-start.14) | collective-permute-done | bytes 163872 | tf_op jit(solution)/shard_map/ppermute | solution.py:27
  98.7 2.2 %collective-permute-start.29 = (bf16[128,128]{1,0:T(8,128)(2,1)S(1)}, bf16[128,128]{1,0:T(8,128)(2,1)S(1)}, u32[]{:S(2)}, u32[]{:S(2)}) collective-permute-start(bf16[128,128]{1,0:T(8,128)(2,1)S(1)} %get-tuple-element.51), channel_id=1, source_target_pairs={{0,96},{1,25},{2,98},{3,27},{4,100},{5,29},{6,102},{7,31},{8,104},... | collective-permute-start | bytes 98312 | tf_op jit(solution)/shard_map/ppermute | solution.py:27
  100.9 1.9 %collective-permute-done.27 = bf16[128,128]{1,0:T(8,128)(2,1)S(1)} collective-permute-done((bf16[128,128]{1,0:T(8,128)(2,1)S(1)}, bf16[128,128]{1,0:T(8,128)(2,1)S(1)}, u32[]{:S(2)}, u32[]{:S(2)}) %collective-permute-start.27) | collective-permute-done | bytes 32800 | tf_op jit(solution)/shard_map/ppermute | solution.py:27
  103.8 2.8 %collective-permute-start.32 = (bf16[128,128]{1,0:T(8,128)(2,1)S(1)}, bf16[128,128]{1,0:T(8,128)(2,1)S(1)}, u32[]{:S(2)}, u32[]{:S(2)}) collective-permute-start(bf16[128,128]{1,0:T(8,128)(2,1)S(1)} %maximum_maximum_fusion), channel_id=1, source_target_pairs={{0,24},{1,97},{2,26},{3,99},{4,28},{5,101},{6,30},{7,103},{8,0},{9... | collective-permute-start | bytes 98312 | tf_op jit(solution)/shard_map/ppermute | solution.py:27
  106.6 2.2 %collective-permute-done.30 = bf16[128,128]{1,0:T(8,128)(2,1)S(1)} collective-permute-done((bf16[128,128]{1,0:T(8,128)(2,1)S(1)}, bf16[128,128]{1,0:T(8,128)(2,1)S(1)}, u32[]{:S(2)}, u32[]{:S(2)}) %collective-permute-start.30) | collective-permute-done | bytes 32800 | tf_op jit(solution)/shard_map/ppermute | solution.py:27
  (68 shorter events, 17.0 us)
Async XLA Ops:
  0.6 1.5 %collective-permute-start = (f32[24,128]{1,0:T(8,128)}, f32[24,128]{1,0:T(8,128)S(1)}, u32[]{:S(2)}, u32[]{:S(2)}) collective-permute-start(f32[24,128]{1,0:T(8,128)} %bitcast.2), channel_id=1, source_target_pairs={{0,1},{1,0},{2,3},{3,2},{4,5},{5,4},{6,7},{7,6},{8,9},{9,8},{10,11... | collective-permute-start | bytes 36872 | tf_op jit(solution)/shard_map/ppermute | solution.py:35
  3.2 6.0 %collective-permute-start.1 = (f32[48,128]{1,0:T(8,128)S(1)}, f32[48,128]{1,0:T(8,128)S(1)}, u32[]{:S(2)}, u32[]{:S(2)}) collective-permute-start(f32[48,128]{1,0:T(8,128)S(1)} %shard_map.59.pair_ref), channel_id=1, source_target_pairs={{0,2},{1,7},{2,4},{3,1},{4,6},{5,3},{6,0},{7,5},{8,10},{9,15},{10,... | collective-permute-start | bytes 73736 | tf_op jit(solution)/shard_map/ppermute | solution.py:27
  5.2 5.5 %collective-permute-start.3 = (f32[24,128]{1,0:T(8,128)S(1)}, f32[24,128]{1,0:T(8,128)S(1)}, u32[]{:S(2)}, u32[]{:S(2)}) collective-permute-start(f32[24,128]{1,0:T(8,128)S(1)} %bitcast.4), channel_id=1, source_target_pairs={{0,4},{2,6},{4,0},{6,2},{1,5},{3,7},{5,1},{7,3},{8,12},{10,14},{12... | collective-permute-start | bytes 36872 | tf_op jit(solution)/shard_map/ppermute | solution.py:31
  9.1 3.0 %collective-permute-start.2 = (f32[48,128]{1,0:T(8,128)S(1)}, f32[48,128]{1,0:T(8,128)S(1)}, u32[]{:S(2)}, u32[]{:S(2)}) collective-permute-start(f32[48,128]{1,0:T(8,128)S(1)} %collective-permute-done.1.mine_ref), channel_id=1, source_target_pairs={{0,1},{1,0},{2,3},{3,2},{4,5},{5,4},{6,7},{7,6},{8,9},{9,8},{10,11... | collective-permute-start | bytes 73736 | tf_op jit(solution)/shard_map/ppermute | solution.py:35
  21.2 13.2 %collective-permute-start.5 = (bf16[32,3072]{1,0:T(8,128)(2,1)S(1)}, bf16[32,3072]{1,0:T(8,128)(2,1)S(1)}, u32[]{:S(2)}, u32[]{:S(2)}) collective-permute-start(bf16[32,3072]{1,0:T(8,128)(2,1)S(1)} %shard_map.62.a0), channel_id=1, source_target_pairs={{0,32},{1,25},{2,34},{3,27},{4,36},{5,29},{6,38},{7,31},{8,40},{9,... | collective-permute-start | bytes 589832 | tf_op jit(solution)/shard_map/ppermute | solution.py:27
  31.0 5.7 %collective-permute-start.16 = (bf16[32,3072]{1,0:T(8,128)(2,1)S(1)}, bf16[32,3072]{1,0:T(8,128)(2,1)S(1)}, u32[]{:S(2)}, u32[]{:S(2)}) collective-permute-start(bf16[32,3072]{1,0:T(8,128)(2,1)S(1)} %shard_map.71.a0), channel_id=1, source_target_pairs={{0,96},{1,9},{2,98},{3,11},{4,100},{5,13},{6,102},{7,15},{8,104},{... | collective-permute-start | bytes 589832 | tf_op jit(solution)/shard_map/ppermute | solution.py:27
  32.8 6.9 %collective-permute-start.6 = (bf16[32,3072]{1,0:T(8,128)(2,1)S(1)}, bf16[32,3072]{1,0:T(8,128)(2,1)S(1)}, u32[]{:S(2)}, u32[]{:S(2)}) collective-permute-start(bf16[32,3072]{1,0:T(8,128)(2,1)S(1)} %shard_map.62.a0), channel_id=1, source_target_pairs={{0,96},{1,9},{2,98},{3,11},{4,100},{5,13},{6,102},{7,15},{8,104},{... | collective-permute-start | bytes 589832 | tf_op jit(solution)/shard_map/ppermute | solution.py:27
  34.4 6.9 %collective-permute-start.7 = (bf16[32,3072]{1,0:T(8,128)(2,1)S(1)}, bf16[32,3072]{1,0:T(8,128)(2,1)S(1)}, u32[]{:S(2)}, u32[]{:S(2)}) collective-permute-start(bf16[32,3072]{1,0:T(8,128)(2,1)S(1)} %collective-permute-done.5.a1), channel_id=1, source_target_pairs={{0,32},{1,25},{2,34},{3,27},{4,36},{5,29},{6,38},{7,31},{8,40},{9,... | collective-permute-start | bytes 589832 | tf_op jit(solution)/shard_map/ppermute | solution.py:27
  34.9 9.6 %collective-permute-start.17 = (bf16[32,3072]{1,0:T(8,128)(2,1)S(1)}, bf16[32,3072]{1,0:T(8,128)(2,1)S(1)}, u32[]{:S(2)}, u32[]{:S(2)}) collective-permute-start(bf16[32,3072]{1,0:T(8,128)(2,1)S(1)} %shard_map.71.a0), channel_id=1, source_target_pairs={{0,32},{1,25},{2,34},{3,27},{4,36},{5,29},{6,38},{7,31},{8,40},{9,... | collective-permute-start | bytes 589832 | tf_op jit(solution)/shard_map/ppermute | solution.py:27
  36.8 7.7 %collective-permute-start.18 = (bf16[32,3072]{1,0:T(8,128)(2,1)S(1)}, bf16[32,3072]{1,0:T(8,128)(2,1)S(1)}, u32[]{:S(2)}, u32[]{:S(2)}) collective-permute-start(bf16[32,3072]{1,0:T(8,128)(2,1)S(1)} %collective-permute-done.16.a1), channel_id=1, source_target_pairs={{0,96},{1,9},{2,98},{3,11},{4,100},{5,13},{6,102},{7,15},{8,104},{... | collective-permute-start | bytes 589832 | tf_op jit(solution)/shard_map/ppermute | solution.py:27
  41.3 12.6 %collective-permute-start.8 = (bf16[4,32,3072]{2,1,0:T(8,128)(2,1)S(1)}, bf16[4,32,3072]{2,1,0:T(8,128)(2,1)S(1)}, u32[]{:S(2)}, u32[]{:S(2)}) collective-permute-start(bf16[4,32,3072]{2,1,0:T(8,128)(2,1)S(1)} %shard_map.63.a0), channel_id=1, source_target_pairs={{0,24},{1,33},{2,26},{3,35},{4,28},{5,37},{6,30},{7,39},{8,0},{9,4... | collective-permute-start | bytes 2359304 | tf_op jit(solution)/shard_map/ppermute | solution.py:27
  44.4 13.3 %collective-permute-start.9 = (bf16[4,32,3072]{2,1,0:T(8,128)(2,1)S(1)}, bf16[4,32,3072]{2,1,0:T(8,128)(2,1)S(1)}, u32[]{:S(2)}, u32[]{:S(2)}) collective-permute-start(bf16[4,32,3072]{2,1,0:T(8,128)(2,1)S(1)} %shard_map.63.a0), channel_id=1, source_target_pairs={{0,8},{1,97},{2,10},{3,99},{4,12},{5,101},{6,14},{7,103},{8,16},{9... | collective-permute-start | bytes 2359304 | tf_op jit(solution)/shard_map/ppermute | solution.py:27
  44.5 17.9 %collective-permute-start.19 = (bf16[4,32,3072]{2,1,0:T(8,128)(2,1)S(1)}, bf16[4,32,3072]{2,1,0:T(8,128)(2,1)S(1)}, u32[]{:S(2)}, u32[]{:S(2)}) collective-permute-start(bf16[4,32,3072]{2,1,0:T(8,128)(2,1)S(1)} %shard_map.72.a0), channel_id=1, source_target_pairs={{0,24},{1,33},{2,26},{3,35},{4,28},{5,37},{6,30},{7,39},{8,0},{9,4... | collective-permute-start | bytes 2359304 | tf_op jit(solution)/shard_map/ppermute | solution.py:27
  47.8 18.4 %collective-permute-start.20 = (bf16[4,32,3072]{2,1,0:T(8,128)(2,1)S(1)}, bf16[4,32,3072]{2,1,0:T(8,128)(2,1)S(1)}, u32[]{:S(2)}, u32[]{:S(2)}) collective-permute-start(bf16[4,32,3072]{2,1,0:T(8,128)(2,1)S(1)} %shard_map.72.a0), channel_id=1, source_target_pairs={{0,8},{1,97},{2,10},{3,99},{4,12},{5,101},{6,14},{7,103},{8,16},{9... | collective-permute-start | bytes 2359304 | tf_op jit(solution)/shard_map/ppermute | solution.py:27
  54.0 14.9 %collective-permute-start.10 = (bf16[2,32,3072]{2,1,0:T(8,128)(2,1)S(1)}, bf16[2,32,3072]{2,1,0:T(8,128)(2,1)S(1)}, u32[]{:S(2)}, u32[]{:S(2)}) collective-permute-start(bf16[2,32,3072]{2,1,0:T(8,128)(2,1)S(1)} %shard_map.66), channel_id=1, source_target_pairs={{0,24},{1,33},{2,26},{3,35},{4,28},{5,37},{6,30},{7,39},{8,0},{9,4... | collective-permute-start | bytes 1179656 | tf_op jit(solution)/shard_map/ppermute | solution.py:27
  57.8 12.5 %collective-permute-start.11 = (bf16[2,32,3072]{2,1,0:T(8,128)(2,1)S(1)}, bf16[2,32,3072]{2,1,0:T(8,128)(2,1)S(1)}, u32[]{:S(2)}, u32[]{:S(2)}) collective-permute-start(bf16[2,32,3072]{2,1,0:T(8,128)(2,1)S(1)} %shard_map.67), channel_id=1, source_target_pairs={{0,8},{1,97},{2,10},{3,99},{4,12},{5,101},{6,14},{7,103},{8,16},{9... | collective-permute-start | bytes 1179656 | tf_op jit(solution)/shard_map/ppermute | solution.py:27
  62.4 10.2 %collective-permute-start.21 = (bf16[2,32,3072]{2,1,0:T(8,128)(2,1)S(1)}, bf16[2,32,3072]{2,1,0:T(8,128)(2,1)S(1)}, u32[]{:S(2)}, u32[]{:S(2)}) collective-permute-start(bf16[2,32,3072]{2,1,0:T(8,128)(2,1)S(1)} %shard_map.74), channel_id=1, source_target_pairs={{0,24},{1,33},{2,26},{3,35},{4,28},{5,37},{6,30},{7,39},{8,0},{9,4... | collective-permute-start | bytes 1179656 | tf_op jit(solution)/shard_map/ppermute | solution.py:27
  66.2 9.2 %collective-permute-start.22 = (bf16[2,32,3072]{2,1,0:T(8,128)(2,1)S(1)}, bf16[2,32,3072]{2,1,0:T(8,128)(2,1)S(1)}, u32[]{:S(2)}, u32[]{:S(2)}) collective-permute-start(bf16[2,32,3072]{2,1,0:T(8,128)(2,1)S(1)} %shard_map.75), channel_id=1, source_target_pairs={{0,8},{1,97},{2,10},{3,99},{4,12},{5,101},{6,14},{7,103},{8,16},{9... | collective-permute-start | bytes 1179656 | tf_op jit(solution)/shard_map/ppermute | solution.py:27
  71.1 5.2 %collective-permute-start.12 = (f32[4,80,512]{2,1,0:T(8,128)S(1)}, f32[4,80,512]{2,1,0:T(8,128)S(1)}, u32[]{:S(2)}, u32[]{:S(2)}) collective-permute-start(f32[4,80,512]{2,1,0:T(8,128)S(1)} %get-tuple-element.35), channel_id=1, source_target_pairs={{0,1},{1,0},{2,3},{3,2},{4,5},{5,4},{6,7},{7,6},{8,9},{9,8},{10,11... | collective-permute-start | bytes 1966088 | tf_op jit(solution)/shard_map/ppermute | solution.py:35
  76.2 2.0 %collective-permute-start.23 = (f32[4,64,512]{2,1,0:T(8,128)S(1)}, f32[4,64,512]{2,1,0:T(8,128)S(1)}, u32[]{:S(2)}, u32[]{:S(2)}) collective-permute-start(f32[4,64,512]{2,1,0:T(8,128)S(1)} %get-tuple-element.45), channel_id=1, source_target_pairs={{0,1},{1,0},{2,3},{3,2},{4,5},{5,4},{6,7},{7,6},{8,9},{9,8},{10,11... | collective-permute-start | bytes 1572872 | tf_op jit(solution)/shard_map/ppermute | solution.py:35
  76.4 11.7 %collective-permute-start.13 = (f32[80,512]{1,0:T(8,128)S(1)}, f32[80,512]{1,0:T(8,128)S(1)}, u32[]{:S(2)}, u32[]{:S(2)}) collective-permute-start(f32[80,512]{1,0:T(8,128)S(1)} %get-tuple-element.38), channel_id=1, source_target_pairs={{0,2},{1,7},{2,4},{3,1},{4,6},{5,3},{6,0},{7,5},{8,10},{9,15},{10,... | collective-permute-start | bytes 491528 | tf_op jit(solution)/shard_map/ppermute | solution.py:27
  78.2 6.5 %collective-permute-start.24 = (f32[64,512]{1,0:T(8,128)S(1)}, f32[64,512]{1,0:T(8,128)S(1)}, u32[]{:S(2)}, u32[]{:S(2)}) collective-permute-start(f32[64,512]{1,0:T(8,128)S(1)} %get-tuple-element.48), channel_id=1, source_target_pairs={{0,2},{1,7},{2,4},{3,1},{4,6},{5,3},{6,0},{7,5},{8,10},{9,15},{10,... | collective-permute-start | bytes 393224 | tf_op jit(solution)/shard_map/ppermute | solution.py:27
  80.0 16.0 %collective-permute-start.26 = (f32[64,512]{1,0:T(8,128)S(1)}, f32[64,512]{1,0:T(8,128)S(1)}, u32[]{:S(2)}, u32[]{:S(2)}) collective-permute-start(f32[64,512]{1,0:T(8,128)S(1)} %get-tuple-element.49), channel_id=1, source_target_pairs={{0,6},{1,3},{2,0},{3,5},{4,2},{5,7},{6,4},{7,1},{8,14},{9,11},{10,... | collective-permute-start | bytes 393224 | tf_op jit(solution)/shard_map/ppermute | solution.py:27
  84.8 11.3 %collective-permute-start.25 = (f32[64,512]{1,0:T(8,128)S(1)}, f32[64,512]{1,0:T(8,128)S(1)}, u32[]{:S(2)}, u32[]{:S(2)}) collective-permute-start(f32[64,512]{1,0:T(8,128)S(1)} %add.19), channel_id=1, source_target_pairs={{0,2},{1,7},{2,4},{3,1},{4,6},{5,3},{6,0},{7,5},{8,10},{9,15},{10,... | collective-permute-start | bytes 393224 | tf_op jit(solution)/shard_map/ppermute | solution.py:27
  86.1 5.8 %collective-permute-start.15 = (f32[80,512]{1,0:T(8,128)S(1)}, f32[80,512]{1,0:T(8,128)S(1)}, u32[]{:S(2)}, u32[]{:S(2)}) collective-permute-start(f32[80,512]{1,0:T(8,128)S(1)} %get-tuple-element.39), channel_id=1, source_target_pairs={{0,6},{1,3},{2,0},{3,5},{4,2},{5,7},{6,4},{7,1},{8,14},{9,11},{10,... | collective-permute-start | bytes 491528 | tf_op jit(solution)/shard_map/ppermute | solution.py:27
  88.1 6.6 %collective-permute-start.14 = (f32[80,512]{1,0:T(8,128)S(1)}, f32[80,512]{1,0:T(8,128)S(1)}, u32[]{:S(2)}, u32[]{:S(2)}) collective-permute-start(f32[80,512]{1,0:T(8,128)S(1)} %add.18), channel_id=1, source_target_pairs={{0,2},{1,7},{2,4},{3,1},{4,6},{5,3},{6,0},{7,5},{8,10},{9,15},{10,... | collective-permute-start | bytes 491528 | tf_op jit(solution)/shard_map/ppermute | solution.py:27
  97.3 5.4 %collective-permute-start.27 = (bf16[128,128]{1,0:T(8,128)(2,1)S(1)}, bf16[128,128]{1,0:T(8,128)(2,1)S(1)}, u32[]{:S(2)}, u32[]{:S(2)}) collective-permute-start(bf16[128,128]{1,0:T(8,128)(2,1)S(1)} %get-tuple-element.51), channel_id=1, source_target_pairs={{0,64},{1,17},{2,66},{3,19},{4,68},{5,21},{6,70},{7,23},{8,72},{9,... | collective-permute-start | bytes 98312 | tf_op jit(solution)/shard_map/ppermute | solution.py:27
  97.7 5.5 %collective-permute-start.28 = (bf16[128,128]{1,0:T(8,128)(2,1)S(1)}, bf16[128,128]{1,0:T(8,128)(2,1)S(1)}, u32[]{:S(2)}, u32[]{:S(2)}) collective-permute-start(bf16[128,128]{1,0:T(8,128)(2,1)S(1)} %get-tuple-element.51), channel_id=1, source_target_pairs={{0,32},{1,9},{2,34},{3,11},{4,36},{5,13},{6,38},{7,15},{8,40},{9,1... | collective-permute-start | bytes 98312 | tf_op jit(solution)/shard_map/ppermute | solution.py:27
  98.7 4.4 %collective-permute-start.29 = (bf16[128,128]{1,0:T(8,128)(2,1)S(1)}, bf16[128,128]{1,0:T(8,128)(2,1)S(1)}, u32[]{:S(2)}, u32[]{:S(2)}) collective-permute-start(bf16[128,128]{1,0:T(8,128)(2,1)S(1)} %get-tuple-element.51), channel_id=1, source_target_pairs={{0,96},{1,25},{2,98},{3,27},{4,100},{5,29},{6,102},{7,31},{8,104},... | collective-permute-start | bytes 98312 | tf_op jit(solution)/shard_map/ppermute | solution.py:27
  103.2 5.6 %collective-permute-start.30 = (bf16[128,128]{1,0:T(8,128)(2,1)S(1)}, bf16[128,128]{1,0:T(8,128)(2,1)S(1)}, u32[]{:S(2)}, u32[]{:S(2)}) collective-permute-start(bf16[128,128]{1,0:T(8,128)(2,1)S(1)} %maximum_maximum_fusion), channel_id=1, source_target_pairs={{0,16},{1,65},{2,18},{3,67},{4,20},{5,69},{6,22},{7,71},{8,24},{9,... | collective-permute-start | bytes 98312 | tf_op jit(solution)/shard_map/ppermute | solution.py:27
  103.3 5.5 %collective-permute-start.31 = (bf16[128,128]{1,0:T(8,128)(2,1)S(1)}, bf16[128,128]{1,0:T(8,128)(2,1)S(1)}, u32[]{:S(2)}, u32[]{:S(2)}) collective-permute-start(bf16[128,128]{1,0:T(8,128)(2,1)S(1)} %maximum_maximum_fusion), channel_id=1, source_target_pairs={{0,8},{1,33},{2,10},{3,35},{4,12},{5,37},{6,14},{7,39},{8,16},{9,4... | collective-permute-start | bytes 98312 | tf_op jit(solution)/shard_map/ppermute | solution.py:27
  103.8 5.1 %collective-permute-start.32 = (bf16[128,128]{1,0:T(8,128)(2,1)S(1)}, bf16[128,128]{1,0:T(8,128)(2,1)S(1)}, u32[]{:S(2)}, u32[]{:S(2)}) collective-permute-start(bf16[128,128]{1,0:T(8,128)(2,1)S(1)} %maximum_maximum_fusion), channel_id=1, source_target_pairs={{0,24},{1,97},{2,26},{3,99},{4,28},{5,101},{6,30},{7,103},{8,0},{9... | collective-permute-start | bytes 98312 | tf_op jit(solution)/shard_map/ppermute | solution.py:27
  (5 other events, 78.0 us)

commit v4 on v3

--- a/solution.py
+++ b/solution.py
@@ -11,7 +11,7 @@
 AXES = ("x", "y", "z", "c")
 CHUNKS = 2
 LOW = 128
-COLUMNS = 6
+COLUMNS = 12
 PLACES = [
     (x, y, z, c) for x in range(RING) for y in range(RING) for z in range(RING) for c in range(2)
 ]
@@ -56,7 +56,10 @@
 
     @pl.when(pl.program_id(0) == pl.num_programs(0) - 1)
     def _():
-        totals_ref[...] = acc_ref[...].astype(jnp.float32)
+        totals_ref[...] = jnp.zeros_like(totals_ref)
+        for k in range(2):
+            total = jnp.sum(acc_ref[8 * k : 8 * k + 8, :], axis=0, keepdims=True)
+            totals_ref[k : k + 1, :] = total.astype(jnp.float32)
 
 
 def convert_dosage(dosage):
@@ -65,11 +68,11 @@
     return pl.pallas_call(
         dosage_kernel,
         grid=(samples // block,),
-        out_shape=(out_of(dosage.shape, jnp.bfloat16), out_of((16, width), jnp.float32)),
+        out_shape=(out_of(dosage.shape, jnp.bfloat16), out_of((8, width), jnp.float32)),
         in_specs=[pl.BlockSpec((block, width), lambda i: (i, 0))],
         out_specs=(
             pl.BlockSpec((block, width), lambda i: (i, 0)),
-            pl.BlockSpec((16, width), lambda i: (0, 0)),
+            pl.BlockSpec((8, width), lambda i: (0, 0)),
         ),
         scratch_shapes=[pltpu.VMEM((16, width), jnp.int32)],
         compiler_params=room(8),
@@ -233,7 +236,7 @@
     groups = rows // 8
     scale = jnp.broadcast_to(scale_ref[...], (8, LOW))
     units = COLUMNS * groups
-    dotted = units // 2
+    dotted = units * 11 // 24
 
     def step(t, _):
         base = pl.multiple_of(t * COLUMNS * LOW, LOW)
@@ -271,7 +274,7 @@
 
 def lookup(index, table, scale, plain):
     groups = index.shape[0] // 8
-    slots = (COLUMNS * groups // 2, 8, LOW)
+    slots = (COLUMNS * groups * 11 // 24, 8, LOW)
     return pl.pallas_call(
         lookup_kernel,
         out_shape=out_of(index.shape, jnp.bfloat16),
@@ -460,8 +463,7 @@
         var_ref, end_ref, p, q, r, z_ref, most_ref, inverse_ref = refs
         rows = (p.shape[0] - extra) // 2
         totals = p[2 * rows :, :] + q[2 * rows :, :] + r[2 * rows :, :]
-        allele_sum = jnp.sum(totals[0:8], axis=0, keepdims=True)
-        allele_sq = jnp.sum(totals[8:16], axis=0, keepdims=True)
+        allele_sum, allele_sq = totals[0:1], totals[1:2]
         allele_var = allele_sq / count - (allele_sum / count) ** 2
         inverse = 1.0 / jnp.sqrt(count * (var_ref[0, 0] + EPSILON) * (allele_var + EPSILON))
         inverse_ref[...] = inverse

time: 110 us -> 108 us (0.982)
  waiting for transfers between devices: 35.7 us -> 33.5 us
    ppermute x27, waiting for transfers between devices: 32.3 us -> 30.1 us  [shift(): lax.ppermute(value, AXES, [(at(*d), at(*target(*d))) for d in PLACES])]
where the time goes in v4:
time: 108 us; the launch traced here: 107 us
  starting transfers between devices  44 us (41%)
  waiting for transfers between devices  33.5 us (31%)
  Pallas kernels  25.6 us (24%)
  local copies, waits for them, and re-layouts  2.19 us (2%)
    ppermute x27, starting transfers between devices, shift(): lax.ppermute(value, AXES, [(at(*d), at(*target(*d))) for d in PLACES])  39.9 us
    ppermute x27, waiting for transfers between devices, shift(): lax.ppermute(value, AXES, [(at(*d), at(*target(*d))) for d in PLACES])  30.1 us
    pallas_call x2, Pallas kernels, lookup(): pl.pallas_call(lookup_kernel, out_shape=out_of(index.shape, jnp.bfloat16)...  16.5 us
    ppermute x1, starting transfers between devices, along(): lax.ppermute(value, axis, [(i, (i + step) % RING) for i in range(RING)])  3.58 us
    pallas_call x2, Pallas kernels, early_product(): pl.pallas_call(early_kernel, out_shape=out_of((rows, dosage.shape[1]), jn...  2.75 us
    unnamed x8, local copies, waits for them, and re-layouts  2.19 us
  transfers between devices with their start and end apart: 33, of which 16 were waited for; matrix products, arithmetic and copies ran while one was open for 0% of the time, Pallas kernels for 14%

profile of v4, /device:TPU:0, one launch (start us, length us, event | category | flops | bytes accessed | tf_op | source)
XLA Modules:
  0.0 107.1 jit_solution(11710002789174165428)
XLA Ops:
  0.7 1.4 %collective-permute-done.b_ref = f32[24,128]{1,0:T(8,128)S(1)} collective-permute-done((f32[24,128]{1,0:T(8,128)}, f32[24,128]{1,0:T(8,128)S(1)}, u32[]{:S(2)}, u32[]{:S(2)}) %collective-permute-start) | collective-permute-done | bytes 12320 | tf_op jit(solution)/shard_map/ppermute | solution.py:35
  3.2 2.0 %collective-permute-start.1 = (f32[48,128]{1,0:T(8,128)S(1)}, f32[48,128]{1,0:T(8,128)S(1)}, u32[]{:S(2)}, u32[]{:S(2)}) collective-permute-start(f32[48,128]{1,0:T(8,128)S(1)} %shard_map.59.pair_ref), channel_id=1, source_target_pairs={{0,2},{1,7},{2,4},{3,1},{4,6},{5,3},{6,0},{7,5},{8,10},{9,15},{10,... | collective-permute-start | bytes 73736 | tf_op jit(solution)/shard_map/ppermute | solution.py:27
  5.2 3.6 %collective-permute-start.3 = (f32[24,128]{1,0:T(8,128)S(1)}, f32[24,128]{1,0:T(8,128)S(1)}, u32[]{:S(2)}, u32[]{:S(2)}) collective-permute-start(f32[24,128]{1,0:T(8,128)S(1)} %bitcast.4), channel_id=1, source_target_pairs={{0,4},{2,6},{4,0},{6,2},{1,5},{3,7},{5,1},{7,3},{8,12},{10,14},{12... | collective-permute-start | bytes 36872 | tf_op jit(solution)/shard_map/ppermute | solution.py:31
  9.1 1.6 %collective-permute-done.3.far_ref = f32[24,128]{1,0:T(8,128)S(1)} collective-permute-done((f32[24,128]{1,0:T(8,128)S(1)}, f32[24,128]{1,0:T(8,128)S(1)}, u32[]{:S(2)}, u32[]{:S(2)}) %collective-permute-start.3) | collective-permute-done | bytes 12320 | tf_op jit(solution)/shard_map/ppermute | solution.py:31
  12.9 8.3 %shard_map.62.a0 = bf16[32,3072]{1,0:T(8,128)(2,1)S(1)} custom-call(s32[32,3072]{1,0:T(8,128)S(1)} %get-tuple-element.28.index_ref, s32[96,128]{1,0:T(8,128)S(1)} %get-tuple-element.29.table_ref, f32[1,128]{1,0:T(1,128)S(1)} %get-tuple-element.30.scale_ref, bf16[96,256]{1,0:T(8,128)(2,1)S(1)} %get-tuple-element.31.plain_ref), custom_call_target="tpu_custom_call" | custom-call | tf_op jit(solution)/shard_map/pallas_call | solution.py:278
  21.2 1.6 %collective-permute-start.5 = (bf16[32,3072]{1,0:T(8,128)(2,1)S(1)}, bf16[32,3072]{1,0:T(8,128)(2,1)S(1)}, u32[]{:S(2)}, u32[]{:S(2)}) collective-permute-start(bf16[32,3072]{1,0:T(8,128)(2,1)S(1)} %shard_map.62.a0), channel_id=1, source_target_pairs={{0,32},{1,25},{2,34},{3,27},{4,36},{5,29},{6,38},{7,31},{8,40},{9,... | collective-permute-start | bytes 589832 | tf_op jit(solution)/shard_map/ppermute | solution.py:27
  22.7 8.2 %shard_map.71.a0 = bf16[32,3072]{1,0:T(8,128)(2,1)S(1)} custom-call(s32[32,3072]{1,0:T(8,128)S(1)} %get-tuple-element.43.index_ref, s32[96,128]{1,0:T(8,128)S(1)} %get-tuple-element.29.table_ref, f32[1,128]{1,0:T(1,128)S(1)} %get-tuple-element.30.scale_ref, bf16[96,256]{1,0:T(8,128)(2,1)S(1)} %get-tuple-element.31.plain_ref), custom_call_target="tpu_custom_call" | custom-call | tf_op jit(solution)/shard_map/pallas_call | solution.py:278
  31.0 1.8 %collective-permute-start.16 = (bf16[32,3072]{1,0:T(8,128)(2,1)S(1)}, bf16[32,3072]{1,0:T(8,128)(2,1)S(1)}, u32[]{:S(2)}, u32[]{:S(2)}) collective-permute-start(bf16[32,3072]{1,0:T(8,128)(2,1)S(1)} %shard_map.71.a0), channel_id=1, source_target_pairs={{0,96},{1,9},{2,98},{3,11},{4,100},{5,13},{6,102},{7,15},{8,104},{... | collective-permute-start | bytes 589832 | tf_op jit(solution)/shard_map/ppermute | solution.py:27
  32.8 1.5 %collective-permute-start.6 = (bf16[32,3072]{1,0:T(8,128)(2,1)S(1)}, bf16[32,3072]{1,0:T(8,128)(2,1)S(1)}, u32[]{:S(2)}, u32[]{:S(2)}) collective-permute-start(bf16[32,3072]{1,0:T(8,128)(2,1)S(1)} %shard_map.62.a0), channel_id=1, source_target_pairs={{0,96},{1,9},{2,98},{3,11},{4,100},{5,13},{6,102},{7,15},{8,104},{... | collective-permute-start | bytes 589832 | tf_op jit(solution)/shard_map/ppermute | solution.py:27
  35.1 1.6 %collective-permute-done.16.a1 = bf16[32,3072]{1,0:T(8,128)(2,1)S(1)} collective-permute-done((bf16[32,3072]{1,0:T(8,128)(2,1)S(1)}, bf16[32,3072]{1,0:T(8,128)(2,1)S(1)}, u32[]{:S(2)}, u32[]{:S(2)}) %collective-permute-start.16) | collective-permute-done | bytes 196640 | tf_op jit(solution)/shard_map/ppermute | solution.py:27
  36.7 3.0 %collective-permute-start.18 = (bf16[32,3072]{1,0:T(8,128)(2,1)S(1)}, bf16[32,3072]{1,0:T(8,128)(2,1)S(1)}, u32[]{:S(2)}, u32[]{:S(2)}) collective-permute-start(bf16[32,3072]{1,0:T(8,128)(2,1)S(1)} %collective-permute-done.16.a1), channel_id=1, source_target_pairs={{0,96},{1,9},{2,98},{3,11},{4,100},{5,13},{6,102},{7,15},{8,104},{... | collective-permute-start | bytes 589832 | tf_op jit(solution)/shard_map/ppermute | solution.py:27
  39.7 1.5 %collective-permute-done.7.a3 = bf16[32,3072]{1,0:T(8,128)(2,1)S(1)} collective-permute-done((bf16[32,3072]{1,0:T(8,128)(2,1)S(1)}, bf16[32,3072]{1,0:T(8,128)(2,1)S(1)}, u32[]{:S(2)}, u32[]{:S(2)}) %collective-permute-start.7) | collective-permute-done | bytes 196640 | tf_op jit(solution)/shard_map/ppermute | solution.py:27
  41.3 3.1 %collective-permute-start.8 = (bf16[4,32,3072]{2,1,0:T(8,128)(2,1)S(1)}, bf16[4,32,3072]{2,1,0:T(8,128)(2,1)S(1)}, u32[]{:S(2)}, u32[]{:S(2)}) collective-permute-start(bf16[4,32,3072]{2,1,0:T(8,128)(2,1)S(1)} %shard_map.63.a0), channel_id=1, source_target_pairs={{0,24},{1,33},{2,26},{3,35},{4,28},{5,37},{6,30},{7,39},{8,0},{9,4... | collective-permute-start | bytes 2359304 | tf_op jit(solution)/shard_map/ppermute | solution.py:27
  44.5 3.3 %collective-permute-start.19 = (bf16[4,32,3072]{2,1,0:T(8,128)(2,1)S(1)}, bf16[4,32,3072]{2,1,0:T(8,128)(2,1)S(1)}, u32[]{:S(2)}, u32[]{:S(2)}) collective-permute-start(bf16[4,32,3072]{2,1,0:T(8,128)(2,1)S(1)} %shard_map.72.a0), channel_id=1, source_target_pairs={{0,24},{1,33},{2,26},{3,35},{4,28},{5,37},{6,30},{7,39},{8,0},{9,4... | collective-permute-start | bytes 2359304 | tf_op jit(solution)/shard_map/ppermute | solution.py:27
  47.8 6.1 %collective-permute-done.8.a1.refs_0_ = bf16[4,32,3072]{2,1,0:T(8,128)(2,1)S(1)} collective-permute-done((bf16[4,32,3072]{2,1,0:T(8,128)(2,1)S(1)}, bf16[4,32,3072]{2,1,0:T(8,128)(2,1)S(1)}, u32[]{:S(2)}, u32[]{:S(2)}) %collective-permute-start.8) | collective-permute-done | bytes 786464 | tf_op jit(solution)/shard_map/ppermute | solution.py:27
  53.9 3.8 %collective-permute-start.10 = (bf16[2,32,3072]{2,1,0:T(8,128)(2,1)S(1)}, bf16[2,32,3072]{2,1,0:T(8,128)(2,1)S(1)}, u32[]{:S(2)}, u32[]{:S(2)}) collective-permute-start(bf16[2,32,3072]{2,1,0:T(8,128)(2,1)S(1)} %shard_map.66), channel_id=1, source_target_pairs={{0,24},{1,33},{2,26},{3,35},{4,28},{5,37},{6,30},{7,39},{8,0},{9,4... | collective-permute-start | bytes 1179656 | tf_op jit(solution)/shard_map/ppermute | solution.py:27
  57.8 4.5 %collective-permute-done.19.a1.refs_0_ = bf16[4,32,3072]{2,1,0:T(8,128)(2,1)S(1)} collective-permute-done((bf16[4,32,3072]{2,1,0:T(8,128)(2,1)S(1)}, bf16[4,32,3072]{2,1,0:T(8,128)(2,1)S(1)}, u32[]{:S(2)}, u32[]{:S(2)}) %collective-permute-start.19) | collective-permute-done | bytes 786464 | tf_op jit(solution)/shard_map/ppermute | solution.py:27
  62.3 3.8 %collective-permute-start.21 = (bf16[2,32,3072]{2,1,0:T(8,128)(2,1)S(1)}, bf16[2,32,3072]{2,1,0:T(8,128)(2,1)S(1)}, u32[]{:S(2)}, u32[]{:S(2)}) collective-permute-start(bf16[2,32,3072]{2,1,0:T(8,128)(2,1)S(1)} %shard_map.74), channel_id=1, source_target_pairs={{0,24},{1,33},{2,26},{3,35},{4,28},{5,37},{6,30},{7,39},{8,0},{9,4... | collective-permute-start | bytes 1179656 | tf_op jit(solution)/shard_map/ppermute | solution.py:27
  67.3 1.4 %shard_map.65.refs_0_ = f32[384,512]{1,0:T(8,128)S(1)} custom-call(bf16[4,32,3072]{2,1,0:T(8,128)(2,1)S(1)} %shard_map.63.a0, bf16[4,32,3072]{2,1,0:T(8,128)(2,1)S(1)} %collective-permute-done.8.a1.refs_0_, bf16[4,32,3072]{2,1,0:T(8,128)(2,1)S(1)} %collective-permute-done.9.a2.refs_0_, bf16[3072,512]{1,0:T(8,128)(2,1)S(1)} %get-tuple-element.32.dosage_ref.refs_3_), custom_call_target="tpu_custom_call" | custom-call | tf_op jit(solution)/shard_map/pallas_call | solution.py:355
  68.7 1.5 %collective-permute-done.11.refs_2_ = bf16[2,32,3072]{2,1,0:T(8,128)(2,1)S(1)} collective-permute-done((bf16[2,32,3072]{2,1,0:T(8,128)(2,1)S(1)}, bf16[2,32,3072]{2,1,0:T(8,128)(2,1)S(1)}, u32[]{:S(2)}, u32[]{:S(2)}) %collective-permute-start.11) | collective-permute-done | bytes 393248 | tf_op jit(solution)/shard_map/ppermute | solution.py:27
  71.1 1.4 %shard_map.73.refs_0_ = f32[384,512]{1,0:T(8,128)S(1)} custom-call(bf16[4,32,3072]{2,1,0:T(8,128)(2,1)S(1)} %shard_map.72.a0, bf16[4,32,3072]{2,1,0:T(8,128)(2,1)S(1)} %collective-permute-done.19.a1.refs_0_, bf16[4,32,3072]{2,1,0:T(8,128)(2,1)S(1)} %collective-permute-done.20.a2.refs_0_, bf16[3072,512]{1,0:T(8,128)(2,1)S(1)} %get-tuple-element.32.dosage_ref.refs_3_), custom_call_target="tpu_custom_call" | custom-call | tf_op jit(solution)/shard_map/pallas_call | solution.py:355
  72.5 2.7 %collective-permute-done.22.refs_2_ = bf16[2,32,3072]{2,1,0:T(8,128)(2,1)S(1)} collective-permute-done((bf16[2,32,3072]{2,1,0:T(8,128)(2,1)S(1)}, bf16[2,32,3072]{2,1,0:T(8,128)(2,1)S(1)}, u32[]{:S(2)}, u32[]{:S(2)}) %collective-permute-start.22) | collective-permute-done | bytes 393248 | tf_op jit(solution)/shard_map/ppermute | solution.py:27
  76.1 1.4 %collective-permute-start.13 = (f32[72,512]{1,0:T(8,128)S(1)}, f32[72,512]{1,0:T(8,128)S(1)}, u32[]{:S(2)}, u32[]{:S(2)}) collective-permute-start(f32[72,512]{1,0:T(8,128)S(1)} %get-tuple-element.38), channel_id=1, source_target_pairs={{0,2},{1,7},{2,4},{3,1},{4,6},{5,3},{6,0},{7,5},{8,10},{9,15},{10,... | collective-permute-start | bytes 442376 | tf_op jit(solution)/shard_map/ppermute | solution.py:27
  78.0 1.4 %collective-permute-start.24 = (f32[64,512]{1,0:T(8,128)S(1)}, f32[64,512]{1,0:T(8,128)S(1)}, u32[]{:S(2)}, u32[]{:S(2)}) collective-permute-start(f32[64,512]{1,0:T(8,128)S(1)} %get-tuple-element.48), channel_id=1, source_target_pairs={{0,2},{1,7},{2,4},{3,1},{4,6},{5,3},{6,0},{7,5},{8,10},{9,15},{10,... | collective-permute-start | bytes 393224 | tf_op jit(solution)/shard_map/ppermute | solution.py:27
  79.8 1.9 %collective-permute-start.26 = (f32[64,512]{1,0:T(8,128)S(1)}, f32[64,512]{1,0:T(8,128)S(1)}, u32[]{:S(2)}, u32[]{:S(2)}) collective-permute-start(f32[64,512]{1,0:T(8,128)S(1)} %get-tuple-element.49), channel_id=1, source_target_pairs={{0,6},{1,3},{2,0},{3,5},{4,2},{5,7},{6,4},{7,1},{8,14},{9,11},{10,... | collective-permute-start | bytes 393224 | tf_op jit(solution)/shard_map/ppermute | solution.py:27
  82.0 2.5 %collective-permute-done.24 = f32[64,512]{1,0:T(8,128)S(1)} collective-permute-done((f32[64,512]{1,0:T(8,128)S(1)}, f32[64,512]{1,0:T(8,128)S(1)}, u32[]{:S(2)}, u32[]{:S(2)}) %collective-permute-start.24) | collective-permute-done | bytes 131104 | tf_op jit(solution)/shard_map/ppermute | solution.py:27
  85.9 1.7 %collective-permute-start.14 = (f32[72,512]{1,0:T(8,128)S(1)}, f32[72,512]{1,0:T(8,128)S(1)}, u32[]{:S(2)}, u32[]{:S(2)}) collective-permute-start(f32[72,512]{1,0:T(8,128)S(1)} %add.18), channel_id=1, source_target_pairs={{0,2},{1,7},{2,4},{3,1},{4,6},{5,3},{6,0},{7,5},{8,10},{9,15},{10,... | collective-permute-start | bytes 442376 | tf_op jit(solution)/shard_map/ppermute | solution.py:27
  88.4 4.0 %collective-permute-done.14.refs_3_ = f32[72,512]{1,0:T(8,128)S(1)} collective-permute-done((f32[72,512]{1,0:T(8,128)S(1)}, f32[72,512]{1,0:T(8,128)S(1)}, u32[]{:S(2)}, u32[]{:S(2)}) %collective-permute-start.14) | collective-permute-done | bytes 147488 | tf_op jit(solution)/shard_map/ppermute | solution.py:27
  96.4 2.1 %collective-permute-start.29 = (bf16[128,128]{1,0:T(8,128)(2,1)S(1)}, bf16[128,128]{1,0:T(8,128)(2,1)S(1)}, u32[]{:S(2)}, u32[]{:S(2)}) collective-permute-start(bf16[128,128]{1,0:T(8,128)(2,1)S(1)} %get-tuple-element.51), channel_id=1, source_target_pairs={{0,96},{1,25},{2,98},{3,27},{4,100},{5,29},{6,102},{7,31},{8,104},... | collective-permute-start | bytes 98312 | tf_op jit(solution)/shard_map/ppermute | solution.py:27
  98.5 1.9 %collective-permute-done.27 = bf16[128,128]{1,0:T(8,128)(2,1)S(1)} collective-permute-done((bf16[128,128]{1,0:T(8,128)(2,1)S(1)}, bf16[128,128]{1,0:T(8,128)(2,1)S(1)}, u32[]{:S(2)}, u32[]{:S(2)}) %collective-permute-start.27) | collective-permute-done | bytes 32800 | tf_op jit(solution)/shard_map/ppermute | solution.py:27
  101.6 2.6 %collective-permute-start.32 = (bf16[128,128]{1,0:T(8,128)(2,1)S(1)}, bf16[128,128]{1,0:T(8,128)(2,1)S(1)}, u32[]{:S(2)}, u32[]{:S(2)}) collective-permute-start(bf16[128,128]{1,0:T(8,128)(2,1)S(1)} %maximum_maximum_fusion), channel_id=1, source_target_pairs={{0,24},{1,97},{2,26},{3,99},{4,28},{5,101},{6,30},{7,103},{8,0},{9... | collective-permute-start | bytes 98312 | tf_op jit(solution)/shard_map/ppermute | solution.py:27
  104.2 2.2 %collective-permute-done.30 = bf16[128,128]{1,0:T(8,128)(2,1)S(1)} collective-permute-done((bf16[128,128]{1,0:T(8,128)(2,1)S(1)}, bf16[128,128]{1,0:T(8,128)(2,1)S(1)}, u32[]{:S(2)}, u32[]{:S(2)}) %collective-permute-start.30) | collective-permute-done | bytes 32800 | tf_op jit(solution)/shard_map/ppermute | solution.py:27
  (68 shorter events, 16.7 us)
Async XLA Ops:
  0.6 1.5 %collective-permute-start = (f32[24,128]{1,0:T(8,128)}, f32[24,128]{1,0:T(8,128)S(1)}, u32[]{:S(2)}, u32[]{:S(2)}) collective-permute-start(f32[24,128]{1,0:T(8,128)} %bitcast.2), channel_id=1, source_target_pairs={{0,1},{1,0},{2,3},{3,2},{4,5},{5,4},{6,7},{7,6},{8,9},{9,8},{10,11... | collective-permute-start | bytes 36872 | tf_op jit(solution)/shard_map/ppermute | solution.py:35
  3.2 6.0 %collective-permute-start.1 = (f32[48,128]{1,0:T(8,128)S(1)}, f32[48,128]{1,0:T(8,128)S(1)}, u32[]{:S(2)}, u32[]{:S(2)}) collective-permute-start(f32[48,128]{1,0:T(8,128)S(1)} %shard_map.59.pair_ref), channel_id=1, source_target_pairs={{0,2},{1,7},{2,4},{3,1},{4,6},{5,3},{6,0},{7,5},{8,10},{9,15},{10,... | collective-permute-start | bytes 73736 | tf_op jit(solution)/shard_map/ppermute | solution.py:27
  5.2 5.5 %collective-permute-start.3 = (f32[24,128]{1,0:T(8,128)S(1)}, f32[24,128]{1,0:T(8,128)S(1)}, u32[]{:S(2)}, u32[]{:S(2)}) collective-permute-start(f32[24,128]{1,0:T(8,128)S(1)} %bitcast.4), channel_id=1, source_target_pairs={{0,4},{2,6},{4,0},{6,2},{1,5},{3,7},{5,1},{7,3},{8,12},{10,14},{12... | collective-permute-start | bytes 36872 | tf_op jit(solution)/shard_map/ppermute | solution.py:31
  9.1 3.0 %collective-permute-start.2 = (f32[48,128]{1,0:T(8,128)S(1)}, f32[48,128]{1,0:T(8,128)S(1)}, u32[]{:S(2)}, u32[]{:S(2)}) collective-permute-start(f32[48,128]{1,0:T(8,128)S(1)} %collective-permute-done.1.mine_ref), channel_id=1, source_target_pairs={{0,1},{1,0},{2,3},{3,2},{4,5},{5,4},{6,7},{7,6},{8,9},{9,8},{10,11... | collective-permute-start | bytes 73736 | tf_op jit(solution)/shard_map/ppermute | solution.py:35
  21.2 13.2 %collective-permute-start.5 = (bf16[32,3072]{1,0:T(8,128)(2,1)S(1)}, bf16[32,3072]{1,0:T(8,128)(2,1)S(1)}, u32[]{:S(2)}, u32[]{:S(2)}) collective-permute-start(bf16[32,3072]{1,0:T(8,128)(2,1)S(1)} %shard_map.62.a0), channel_id=1, source_target_pairs={{0,32},{1,25},{2,34},{3,27},{4,36},{5,29},{6,38},{7,31},{8,40},{9,... | collective-permute-start | bytes 589832 | tf_op jit(solution)/shard_map/ppermute | solution.py:27
  31.0 5.7 %collective-permute-start.16 = (bf16[32,3072]{1,0:T(8,128)(2,1)S(1)}, bf16[32,3072]{1,0:T(8,128)(2,1)S(1)}, u32[]{:S(2)}, u32[]{:S(2)}) collective-permute-start(bf16[32,3072]{1,0:T(8,128)(2,1)S(1)} %shard_map.71.a0), channel_id=1, source_target_pairs={{0,96},{1,9},{2,98},{3,11},{4,100},{5,13},{6,102},{7,15},{8,104},{... | collective-permute-start | bytes 589832 | tf_op jit(solution)/shard_map/ppermute | solution.py:27
  32.8 6.9 %collective-permute-start.6 = (bf16[32,3072]{1,0:T(8,128)(2,1)S(1)}, bf16[32,3072]{1,0:T(8,128)(2,1)S(1)}, u32[]{:S(2)}, u32[]{:S(2)}) collective-permute-start(bf16[32,3072]{1,0:T(8,128)(2,1)S(1)} %shard_map.62.a0), channel_id=1, source_target_pairs={{0,96},{1,9},{2,98},{3,11},{4,100},{5,13},{6,102},{7,15},{8,104},{... | collective-permute-start | bytes 589832 | tf_op jit(solution)/shard_map/ppermute | solution.py:27
  34.4 6.9 %collective-permute-start.7 = (bf16[32,3072]{1,0:T(8,128)(2,1)S(1)}, bf16[32,3072]{1,0:T(8,128)(2,1)S(1)}, u32[]{:S(2)}, u32[]{:S(2)}) collective-permute-start(bf16[32,3072]{1,0:T(8,128)(2,1)S(1)} %collective-permute-done.5.a1), channel_id=1, source_target_pairs={{0,32},{1,25},{2,34},{3,27},{4,36},{5,29},{6,38},{7,31},{8,40},{9,... | collective-permute-start | bytes 589832 | tf_op jit(solution)/shard_map/ppermute | solution.py:27
  34.8 9.5 %collective-permute-start.17 = (bf16[32,3072]{1,0:T(8,128)(2,1)S(1)}, bf16[32,3072]{1,0:T(8,128)(2,1)S(1)}, u32[]{:S(2)}, u32[]{:S(2)}) collective-permute-start(bf16[32,3072]{1,0:T(8,128)(2,1)S(1)} %shard_map.71.a0), channel_id=1, source_target_pairs={{0,32},{1,25},{2,34},{3,27},{4,36},{5,29},{6,38},{7,31},{8,40},{9,... | collective-permute-start | bytes 589832 | tf_op jit(solution)/shard_map/ppermute | solution.py:27
  36.7 7.7 %collective-permute-start.18 = (bf16[32,3072]{1,0:T(8,128)(2,1)S(1)}, bf16[32,3072]{1,0:T(8,128)(2,1)S(1)}, u32[]{:S(2)}, u32[]{:S(2)}) collective-permute-start(bf16[32,3072]{1,0:T(8,128)(2,1)S(1)} %collective-permute-done.16.a1), channel_id=1, source_target_pairs={{0,96},{1,9},{2,98},{3,11},{4,100},{5,13},{6,102},{7,15},{8,104},{... | collective-permute-start | bytes 589832 | tf_op jit(solution)/shard_map/ppermute | solution.py:27
  41.3 12.6 %collective-permute-start.8 = (bf16[4,32,3072]{2,1,0:T(8,128)(2,1)S(1)}, bf16[4,32,3072]{2,1,0:T(8,128)(2,1)S(1)}, u32[]{:S(2)}, u32[]{:S(2)}) collective-permute-start(bf16[4,32,3072]{2,1,0:T(8,128)(2,1)S(1)} %shard_map.63.a0), channel_id=1, source_target_pairs={{0,24},{1,33},{2,26},{3,35},{4,28},{5,37},{6,30},{7,39},{8,0},{9,4... | collective-permute-start | bytes 2359304 | tf_op jit(solution)/shard_map/ppermute | solution.py:27
  44.4 13.3 %collective-permute-start.9 = (bf16[4,32,3072]{2,1,0:T(8,128)(2,1)S(1)}, bf16[4,32,3072]{2,1,0:T(8,128)(2,1)S(1)}, u32[]{:S(2)}, u32[]{:S(2)}) collective-permute-start(bf16[4,32,3072]{2,1,0:T(8,128)(2,1)S(1)} %shard_map.63.a0), channel_id=1, source_target_pairs={{0,8},{1,97},{2,10},{3,99},{4,12},{5,101},{6,14},{7,103},{8,16},{9... | collective-permute-start | bytes 2359304 | tf_op jit(solution)/shard_map/ppermute | solution.py:27
  44.5 17.9 %collective-permute-start.19 = (bf16[4,32,3072]{2,1,0:T(8,128)(2,1)S(1)}, bf16[4,32,3072]{2,1,0:T(8,128)(2,1)S(1)}, u32[]{:S(2)}, u32[]{:S(2)}) collective-permute-start(bf16[4,32,3072]{2,1,0:T(8,128)(2,1)S(1)} %shard_map.72.a0), channel_id=1, source_target_pairs={{0,24},{1,33},{2,26},{3,35},{4,28},{5,37},{6,30},{7,39},{8,0},{9,4... | collective-permute-start | bytes 2359304 | tf_op jit(solution)/shard_map/ppermute | solution.py:27
  47.8 18.4 %collective-permute-start.20 = (bf16[4,32,3072]{2,1,0:T(8,128)(2,1)S(1)}, bf16[4,32,3072]{2,1,0:T(8,128)(2,1)S(1)}, u32[]{:S(2)}, u32[]{:S(2)}) collective-permute-start(bf16[4,32,3072]{2,1,0:T(8,128)(2,1)S(1)} %shard_map.72.a0), channel_id=1, source_target_pairs={{0,8},{1,97},{2,10},{3,99},{4,12},{5,101},{6,14},{7,103},{8,16},{9... | collective-permute-start | bytes 2359304 | tf_op jit(solution)/shard_map/ppermute | solution.py:27
  53.9 14.7 %collective-permute-start.10 = (bf16[2,32,3072]{2,1,0:T(8,128)(2,1)S(1)}, bf16[2,32,3072]{2,1,0:T(8,128)(2,1)S(1)}, u32[]{:S(2)}, u32[]{:S(2)}) collective-permute-start(bf16[2,32,3072]{2,1,0:T(8,128)(2,1)S(1)} %shard_map.66), channel_id=1, source_target_pairs={{0,24},{1,33},{2,26},{3,35},{4,28},{5,37},{6,30},{7,39},{8,0},{9,4... | collective-permute-start | bytes 1179656 | tf_op jit(solution)/shard_map/ppermute | solution.py:27
  57.7 12.5 %collective-permute-start.11 = (bf16[2,32,3072]{2,1,0:T(8,128)(2,1)S(1)}, bf16[2,32,3072]{2,1,0:T(8,128)(2,1)S(1)}, u32[]{:S(2)}, u32[]{:S(2)}) collective-permute-start(bf16[2,32,3072]{2,1,0:T(8,128)(2,1)S(1)} %shard_map.67), channel_id=1, source_target_pairs={{0,8},{1,97},{2,10},{3,99},{4,12},{5,101},{6,14},{7,103},{8,16},{9... | collective-permute-start | bytes 1179656 | tf_op jit(solution)/shard_map/ppermute | solution.py:27
  62.3 10.2 %collective-permute-start.21 = (bf16[2,32,3072]{2,1,0:T(8,128)(2,1)S(1)}, bf16[2,32,3072]{2,1,0:T(8,128)(2,1)S(1)}, u32[]{:S(2)}, u32[]{:S(2)}) collective-permute-start(bf16[2,32,3072]{2,1,0:T(8,128)(2,1)S(1)} %shard_map.74), channel_id=1, source_target_pairs={{0,24},{1,33},{2,26},{3,35},{4,28},{5,37},{6,30},{7,39},{8,0},{9,4... | collective-permute-start | bytes 1179656 | tf_op jit(solution)/shard_map/ppermute | solution.py:27
  66.1 9.1 %collective-permute-start.22 = (bf16[2,32,3072]{2,1,0:T(8,128)(2,1)S(1)}, bf16[2,32,3072]{2,1,0:T(8,128)(2,1)S(1)}, u32[]{:S(2)}, u32[]{:S(2)}) collective-permute-start(bf16[2,32,3072]{2,1,0:T(8,128)(2,1)S(1)} %shard_map.75), channel_id=1, source_target_pairs={{0,8},{1,97},{2,10},{3,99},{4,12},{5,101},{6,14},{7,103},{8,16},{9... | collective-permute-start | bytes 1179656 | tf_op jit(solution)/shard_map/ppermute | solution.py:27
  71.0 5.0 %collective-permute-start.12 = (f32[4,72,512]{2,1,0:T(8,128)S(1)}, f32[4,72,512]{2,1,0:T(8,128)S(1)}, u32[]{:S(2)}, u32[]{:S(2)}) collective-permute-start(f32[4,72,512]{2,1,0:T(8,128)S(1)} %get-tuple-element.35), channel_id=1, source_target_pairs={{0,1},{1,0},{2,3},{3,2},{4,5},{5,4},{6,7},{7,6},{8,9},{9,8},{10,11... | collective-permute-start | bytes 1769480 | tf_op jit(solution)/shard_map/ppermute | solution.py:35
  76.0 2.0 %collective-permute-start.23 = (f32[4,64,512]{2,1,0:T(8,128)S(1)}, f32[4,64,512]{2,1,0:T(8,128)S(1)}, u32[]{:S(2)}, u32[]{:S(2)}) collective-permute-start(f32[4,64,512]{2,1,0:T(8,128)S(1)} %get-tuple-element.45), channel_id=1, source_target_pairs={{0,1},{1,0},{2,3},{3,2},{4,5},{5,4},{6,7},{7,6},{8,9},{9,8},{10,11... | collective-permute-start | bytes 1572872 | tf_op jit(solution)/shard_map/ppermute | solution.py:35
  76.1 9.7 %collective-permute-start.13 = (f32[72,512]{1,0:T(8,128)S(1)}, f32[72,512]{1,0:T(8,128)S(1)}, u32[]{:S(2)}, u32[]{:S(2)}) collective-permute-start(f32[72,512]{1,0:T(8,128)S(1)} %get-tuple-element.38), channel_id=1, source_target_pairs={{0,2},{1,7},{2,4},{3,1},{4,6},{5,3},{6,0},{7,5},{8,10},{9,15},{10,... | collective-permute-start | bytes 442376 | tf_op jit(solution)/shard_map/ppermute | solution.py:27
  78.0 6.5 %collective-permute-start.24 = (f32[64,512]{1,0:T(8,128)S(1)}, f32[64,512]{1,0:T(8,128)S(1)}, u32[]{:S(2)}, u32[]{:S(2)}) collective-permute-start(f32[64,512]{1,0:T(8,128)S(1)} %get-tuple-element.48), channel_id=1, source_target_pairs={{0,2},{1,7},{2,4},{3,1},{4,6},{5,3},{6,0},{7,5},{8,10},{9,15},{10,... | collective-permute-start | bytes 393224 | tf_op jit(solution)/shard_map/ppermute | solution.py:27
  79.8 13.9 %collective-permute-start.26 = (f32[64,512]{1,0:T(8,128)S(1)}, f32[64,512]{1,0:T(8,128)S(1)}, u32[]{:S(2)}, u32[]{:S(2)}) collective-permute-start(f32[64,512]{1,0:T(8,128)S(1)} %get-tuple-element.49), channel_id=1, source_target_pairs={{0,6},{1,3},{2,0},{3,5},{4,2},{5,7},{6,4},{7,1},{8,14},{9,11},{10,... | collective-permute-start | bytes 393224 | tf_op jit(solution)/shard_map/ppermute | solution.py:27
  81.6 6.7 %collective-permute-start.15 = (f32[72,512]{1,0:T(8,128)S(1)}, f32[72,512]{1,0:T(8,128)S(1)}, u32[]{:S(2)}, u32[]{:S(2)}) collective-permute-start(f32[72,512]{1,0:T(8,128)S(1)} %get-tuple-element.39), channel_id=1, source_target_pairs={{0,6},{1,3},{2,0},{3,5},{4,2},{5,7},{6,4},{7,1},{8,14},{9,11},{10,... | collective-permute-start | bytes 442376 | tf_op jit(solution)/shard_map/ppermute | solution.py:27
  84.5 9.1 %collective-permute-start.25 = (f32[64,512]{1,0:T(8,128)S(1)}, f32[64,512]{1,0:T(8,128)S(1)}, u32[]{:S(2)}, u32[]{:S(2)}) collective-permute-start(f32[64,512]{1,0:T(8,128)S(1)} %add.19), channel_id=1, source_target_pairs={{0,2},{1,7},{2,4},{3,1},{4,6},{5,3},{6,0},{7,5},{8,10},{9,15},{10,... | collective-permute-start | bytes 393224 | tf_op jit(solution)/shard_map/ppermute | solution.py:27
  85.9 6.5 %collective-permute-start.14 = (f32[72,512]{1,0:T(8,128)S(1)}, f32[72,512]{1,0:T(8,128)S(1)}, u32[]{:S(2)}, u32[]{:S(2)}) collective-permute-start(f32[72,512]{1,0:T(8,128)S(1)} %add.18), channel_id=1, source_target_pairs={{0,2},{1,7},{2,4},{3,1},{4,6},{5,3},{6,0},{7,5},{8,10},{9,15},{10,... | collective-permute-start | bytes 442376 | tf_op jit(solution)/shard_map/ppermute | solution.py:27
  95.0 5.5 %collective-permute-start.27 = (bf16[128,128]{1,0:T(8,128)(2,1)S(1)}, bf16[128,128]{1,0:T(8,128)(2,1)S(1)}, u32[]{:S(2)}, u32[]{:S(2)}) collective-permute-start(bf16[128,128]{1,0:T(8,128)(2,1)S(1)} %get-tuple-element.51), channel_id=1, source_target_pairs={{0,64},{1,17},{2,66},{3,19},{4,68},{5,21},{6,70},{7,23},{8,72},{9,... | collective-permute-start | bytes 98312 | tf_op jit(solution)/shard_map/ppermute | solution.py:27
  95.3 5.5 %collective-permute-start.28 = (bf16[128,128]{1,0:T(8,128)(2,1)S(1)}, bf16[128,128]{1,0:T(8,128)(2,1)S(1)}, u32[]{:S(2)}, u32[]{:S(2)}) collective-permute-start(bf16[128,128]{1,0:T(8,128)(2,1)S(1)} %get-tuple-element.51), channel_id=1, source_target_pairs={{0,32},{1,9},{2,34},{3,11},{4,36},{5,13},{6,38},{7,15},{8,40},{9,1... | collective-permute-start | bytes 98312 | tf_op jit(solution)/shard_map/ppermute | solution.py:27
  96.4 4.4 %collective-permute-start.29 = (bf16[128,128]{1,0:T(8,128)(2,1)S(1)}, bf16[128,128]{1,0:T(8,128)(2,1)S(1)}, u32[]{:S(2)}, u32[]{:S(2)}) collective-permute-start(bf16[128,128]{1,0:T(8,128)(2,1)S(1)} %get-tuple-element.51), channel_id=1, source_target_pairs={{0,96},{1,25},{2,98},{3,27},{4,100},{5,29},{6,102},{7,31},{8,104},... | collective-permute-start | bytes 98312 | tf_op jit(solution)/shard_map/ppermute | solution.py:27
  100.8 5.6 %collective-permute-start.30 = (bf16[128,128]{1,0:T(8,128)(2,1)S(1)}, bf16[128,128]{1,0:T(8,128)(2,1)S(1)}, u32[]{:S(2)}, u32[]{:S(2)}) collective-permute-start(bf16[128,128]{1,0:T(8,128)(2,1)S(1)} %maximum_maximum_fusion), channel_id=1, source_target_pairs={{0,16},{1,65},{2,18},{3,67},{4,20},{5,69},{6,22},{7,71},{8,24},{9,... | collective-permute-start | bytes 98312 | tf_op jit(solution)/shard_map/ppermute | solution.py:27
  100.9 5.5 %collective-permute-start.31 = (bf16[128,128]{1,0:T(8,128)(2,1)S(1)}, bf16[128,128]{1,0:T(8,128)(2,1)S(1)}, u32[]{:S(2)}, u32[]{:S(2)}) collective-permute-start(bf16[128,128]{1,0:T(8,128)(2,1)S(1)} %maximum_maximum_fusion), channel_id=1, source_target_pairs={{0,8},{1,33},{2,10},{3,35},{4,12},{5,37},{6,14},{7,39},{8,16},{9,4... | collective-permute-start | bytes 98312 | tf_op jit(solution)/shard_map/ppermute | solution.py:27
  101.6 4.9 %collective-permute-start.32 = (bf16[128,128]{1,0:T(8,128)(2,1)S(1)}, bf16[128,128]{1,0:T(8,128)(2,1)S(1)}, u32[]{:S(2)}, u32[]{:S(2)}) collective-permute-start(bf16[128,128]{1,0:T(8,128)(2,1)S(1)} %maximum_maximum_fusion), channel_id=1, source_target_pairs={{0,24},{1,97},{2,26},{3,99},{4,28},{5,101},{6,30},{7,103},{8,0},{9... | collective-permute-start | bytes 98312 | tf_op jit(solution)/shard_map/ppermute | solution.py:27
  (5 other events, 77.6 us)
